TPU v7x, 256 devices: a whole 4x4x8 slice. The times are simulated.
256 devices in a mesh: ha: 8 (over z_lo, y), wa: 32 (over x, z_hi, core).
Axes of the slice: x: 4, y: 4, z: 8 (z_hi: 4, z_lo: 2; z = z_hi * 2 + z_lo), core: 2. Of those that a mesh axis runs over, the one named last changes fastest.
Arguments:
- block_input: bfloat16 [3, 184, 320, 128], P(None, 'ha', 'wa'), may hold values from -6 to 6
- cotangent: bfloat16 [3, 184, 320, 128], P(None, 'ha', 'wa'), may hold values from -6 to 6
- kernel_one: bfloat16 [3, 3, 3, 128, 128], replicated, may hold values from -0.109375 to 0.109375
- bias_one: float32 [128], replicated, may hold values from -3 to 3
- kernel_two: bfloat16 [3, 3, 3, 128, 128], replicated, may hold values from -0.109375 to 0.109375
- scale_one: float32 [128], replicated, may hold values from 0.5 to 2
- shift_one: float32 [128], replicated, may hold values from -1 to 1
- scale_two: float32 [128], replicated, may hold values from 0.5 to 2
- shift_two: float32 [128], replicated, may hold values from -1 to 1
Outputs:
- grad_input: bfloat16 [3, 184, 320, 128], P(None, 'ha', 'wa')
- grad_kernel_one: float32 [3, 3, 3, 128, 128], replicated
- grad_bias_one: float32 [128], replicated
- grad_kernel_two: float32 [3, 3, 3, 128, 128], replicated
- grad_bias_two: float32 [128], replicated
All inputs are finite; a program needn't handle non-finite values.
Results may differ from a plain program's by a relative error of at most 0.0054.
Values may be sent and summed in bfloat16 or wider, within the bound.
No kernel may reach another device: no remote copies, remote signals or barrier semaphores. Data moves between devices by JAX's collectives and lax.ppermute only.
A program may use at most 64 MiB of HBM per device.

v0:
```python
import math

import jax
import jax.numpy as jnp
from jax import lax
from jax.experimental import pallas as pl
from jax.experimental.pallas import tpu as pltpu
from jax.sharding import PartitionSpec as P

CELLS = 176640
AXES = ("ha", "wa")
f32 = jnp.float32
bf16 = jnp.bfloat16


def coords(d):
    return {"zl": d // 128, "y": (d // 32) % 4, "x": (d // 8) % 4, "zh": (d // 2) % 4, "c": d % 2}


def device_of(p):
    return (((p["zl"] * 4 + p["y"]) * 4 + p["x"]) * 4 + p["zh"]) * 2 + p["c"]


def shift_pairs(axis, size, k):
    pairs = []
    for d in range(256):
        p = coords(d)
        a = axis if isinstance(axis, str) else axis[p["c"]]
        p[a] = (p[a] + k) % size
        pairs.append((d, device_of(p)))
    return pairs


def shifted(v, axis, size, k):
    return lax.ppermute(v, AXES, shift_pairs(axis, size, k))


ORDER = (2, 1, 3)


def scatter(own, send, axis):
    got = {k: shifted(send[k], axis, 4, k) for k in ORDER}
    return own + got[1].astype(f32) + got[2].astype(f32) + got[3].astype(f32)


def gather(v, axis, here):
    got = {k: shifted(v, axis, 4, k) for k in ORDER}
    out = lax.dynamic_update_index_in_dim(jnp.zeros((4,) + v.shape, v.dtype), v, here, 0)
    for k in (1, 3, 2):
        out = lax.dynamic_update_index_in_dim(out, got[k], (here - k) % 4, 0)
    return out


def total(pos, own, send):
    first, second = pos[3], pos[4]
    kept, *sends = combine(pos, own, shifted(send, "c", 2, 1))
    v = scatter(kept, dict(enumerate(sends, 1)), ("x", "y"))
    v = v.reshape(4, 224, 128)
    parts = {k: lax.dynamic_index_in_dim(v, (second + k) % 4, 0, keepdims=False) for k in range(4)}
    v = scatter(parts[0], parts, ("y", "x"))
    v = v + shifted(v, "zl", 2, 1)
    v = v.astype(bf16)
    got = {k: shifted(v, "zh", 4, k) for k in ORDER}
    v = ((v.astype(f32) + got[2].astype(f32)) + (got[1].astype(f32) + got[3].astype(f32))).astype(bf16)
    v = gather(v, ("y", "x"), second)
    v = gather(v, ("x", "y"), first).reshape(28, 128, 128)
    return v, shifted(v, "c", 2, 1)


def exchange(low, high, axis, size):
    up = [(i, i + 1) for i in range(size - 1)]
    down = [(i + 1, i) for i in range(size - 1)]
    return lax.ppermute(high, axis, up), lax.ppermute(low, axis, down)


def nt(a, k, kt, kw):
    w = jnp.concatenate([k[kt, kh, kw] for kh in range(3)], axis=1)
    return lax.dot_general(a, w, (((1,), (1,)), ((), ())), preferred_element_type=f32)


def slope(z, s):
    return s * (1.0 + z * (1.0 - s))


def rows(i, n):
    return pl.ds(pl.multiple_of(i * 32, 32), n)


def local_kernel(
    pos, xin, cot, sides, ends, k1, k2, vectors,
    own_out, send_out, d_out,
    line, x_all, a3, g3, g3own, d3own, a1t, a2t, acc, acc2,
):
    row0, col0, core = pos[0], pos[1], pos[2]
    bias1, scale1, shift1, scale2, shift2 = (vectors[i:i + 1, :] for i in range(5))
    line[...] = jnp.zeros_like(line)
    x_all[...] = jnp.zeros_like(x_all)
    g3own[...] = jnp.zeros_like(g3own)
    d3own[...] = jnp.zeros_like(d3own)

    def masks(first, n):
        q = lax.broadcasted_iota(jnp.int32, (n, 128), 0)
        col, row = (q >> 5) + first, q & 31
        own = (row >= 2) & (row < 25) & (col >= 2) & (col < 12)
        r, c = row + row0, col + col0
        inside = (r >= 0) & (r < 184) & (c >= 0) & (c < 320)
        return own, inside

    def spread(dst, t, first, n, order):
        for k, o in enumerate(order):
            dst[t, first:first + n, k * 128:(k + 1) * 128] = line[o:o + n, :].astype(bf16)

    def place(dst, base, which, main, t):
        for w in range(14):
            at = base + w * 32
            if 2 <= w < 12:
                dst[at + 2:at + 25, :] = main[t, w - 2].astype(f32)
            else:
                dst[at + 2:at + 25, :] = sides[w // 12, which, t, w % 12].astype(f32)
            dst[at:at + 2, :] = ends[0, which, t, w].astype(f32)
            dst[at + 25:at + 27, :] = ends[1, which, t, w].astype(f32)

    def enter(t, bias):
        own, inside = masks(0, 448)
        line[8:456, :] = jnp.zeros((448, 128), f32)
        place(line, 8, 1, cot, t)
        place(x_all, 0, 0, xin, t)
        spread(g3, t, 0, 448, (9, 8, 7))
        go = jnp.where(own, line[8:456, :], 0.0)
        line[8:456, :] = go
        spread(g3own, t, 0, 448, (9, 8, 7))
        z = x_all[...] * scale1 + shift1
        s = jax.nn.sigmoid(z)
        line[8:456, :] = jnp.where(inside, z * s, 0.0)
        spread(a3, t, 0, 448, (7, 8, 9))
        a1t[t] = jnp.transpose(line[40:552, :]).astype(bf16)
        return bias + jnp.sum(go.reshape(56, 8, 128), axis=0)

    bias_two = lax.fori_loop(0, 3, enter, jnp.zeros((8, 128), f32))

    for t in range(3):
        acc[t] = jnp.zeros((384, 128), f32)
        acc2[t] = jnp.zeros((384, 128), f32)

    def first_convs(kw, carry):
        for t in range(3):
            for kt in range(2 - t, 3):
                w = jnp.concatenate([k1[kt, kh, kw] for kh in range(3)], axis=0)
                acc[t] += jnp.dot(a3[t + kt - 2, rows(kw, 384), :], w, preferred_element_type=f32)
        for t in range(3):
            for kt in range(t, 3):
                acc2[t] += nt(g3[t - kt + 2, rows(2 - kw, 384), :], k2, kt, kw)
        return carry

    lax.fori_loop(0, 3, first_convs, 0)
    line[392:400, :] = jnp.zeros((8, 128), f32)

    def middle(t, bias):
        own, inside = masks(1, 384)
        z = (acc[t] + bias1) * scale2 + shift2
        s = jax.nn.sigmoid(z)
        line[8:392, :] = jnp.where(inside, z * s, 0.0)
        a2t[t] = jnp.transpose(line[8:520, :]).astype(bf16)
        d = jnp.where(inside, acc2[t] * slope(z, s) * scale2, 0.0)
        d = d.astype(bf16)
        d_out[t] = d
        do = jnp.where(own, d.astype(f32), 0.0)
        line[8:392, :] = do
        spread(d3own, t, 32, 384, (9, 8, 7))
        return bias + jnp.sum(do.reshape(48, 8, 128), axis=0)

    bias_one = lax.fori_loop(0, 3, middle, jnp.zeros((8, 128), f32))

    def put(b, value):
        half = (b >= 28).astype(jnp.int32)
        at = b - half * 28

        @pl.when(half == core)
        def _():
            own_out[at] = value

        @pl.when(half != core)
        def _():
            send_out[at] = value.astype(bf16)

    def second_convs(kw, carry):
        for base, field, cotan in ((0, a1t, d3own), (27, a2t, g3own)):
            for kt in range(3):
                part = None
                for t in range(2 - kt, 3):
                    term = jnp.dot(field[t + kt - 2], cotan[t, rows(2 - kw, 512), :], preferred_element_type=f32)
                    part = term if part is None else part + term
                for kh in range(3):
                    put(base + kt * 9 + kh * 3 + kw, part[:, kh * 128:(kh + 1) * 128])
        return carry

    lax.fori_loop(0, 3, second_convs, 0)

    extra = lax.broadcasted_iota(jnp.int32, (128, 128), 0)
    b1 = jnp.broadcast_to(jnp.sum(bias_one, axis=0, keepdims=True), (128, 128))
    b2 = jnp.broadcast_to(jnp.sum(bias_two, axis=0, keepdims=True), (128, 128))
    put(jnp.int32(54), jnp.where(extra < 8, b1, jnp.where(extra < 16, b2, 0.0)))
    put(jnp.int32(55), jnp.zeros((128, 128), f32))


def input_kernel(d, xin, cot, k1, vectors, gin, line, d3, acc):
    scale1, shift1 = vectors[1:2, :], vectors[2:3, :]
    line[...] = jnp.zeros_like(line)
    for t in range(3):
        acc[t] = jnp.zeros((320, 128), f32)
        line[8:392, :] = d[t].astype(f32)
        for k, o in enumerate((9, 8, 7)):
            d3[t, :, k * 128:(k + 1) * 128] = line[o:o + 384, :].astype(bf16)

    def convs(kw, carry):
        for t in range(3):
            for kt in range(t, 3):
                acc[t] += nt(d3[t - kt + 2, rows(2 - kw, 320), :], k1, kt, kw)
        return carry

    lax.fori_loop(0, 3, convs, 0)
    for t in range(3):
        for w in range(10):
            z = xin[t, w].astype(f32) * scale1 + shift1
            change = acc[t, w * 32 + 2:w * 32 + 25, :] * (slope(z, jax.nn.sigmoid(z)) * scale1)
            gin[t, w] = (cot[t, w].astype(f32) + change).astype(bf16)


def combine_kernel(pos, own, got, kept, to1, to2, to3):
    def one(j, carry):
        for k, out in enumerate((kept, to1, to2, to3)):
            b = lax.rem(pos[3] + k, 4) * 7 + j
            out[j] = (own[b] + got[b].astype(f32)).astype(out.dtype)
        return carry

    lax.fori_loop(0, 7, one, 0)


def final_kernel(pos, mine, other, one, two, bias_one, bias_two):
    factor = 1.0 / math.sqrt(CELLS)

    def emit(low, high):
        def block(b):
            ref, at = (low, b) if b < 28 else (high, b - 28)
            return ref[at].astype(f32) * factor

        for b in range(27):
            one[b] = block(b)
            two[b] = block(27 + b)
        bias_one[...] = high[26, 0:8, :].astype(f32) * factor
        bias_two[...] = high[26, 8:16, :].astype(f32) * factor

    @pl.when(pos[2] == 0)
    def _():
        emit(mine, other)

    @pl.when(pos[2] != 0)
    def _():
        emit(other, mine)


VMEM = pl.BlockSpec(memory_space=pltpu.VMEM)
SMEM = pl.BlockSpec(memory_space=pltpu.SMEM)


def call(kernel, out, inputs, scratch, mib, flops, size):
    return pl.pallas_call(
        kernel,
        out_shape=tuple(jax.ShapeDtypeStruct(*o) for o in out),
        in_specs=inputs,
        out_specs=(VMEM,) * len(out),
        scratch_shapes=scratch,
        compiler_params=pltpu.CompilerParams(vmem_limit_bytes=mib * 1024 * 1024),
        cost_estimate=pl.CostEstimate(flops=flops, bytes_accessed=size, transcendentals=0),
    )


def local(pos, xin, cot, sides, ends, k1, k2, vectors):
    return call(
        local_kernel,
        [((28, 128, 128), f32), ((28, 128, 128), bf16), ((3, 384, 128), bf16)],
        [SMEM] + [VMEM] * 7,
        [
            pltpu.VMEM((568, 128), f32),
            pltpu.VMEM((448, 128), f32),
            pltpu.VMEM((3, 448, 384), bf16),
            pltpu.VMEM((3, 448, 384), bf16),
            pltpu.VMEM((3, 576, 384), bf16),
            pltpu.VMEM((3, 576, 384), bf16),
            pltpu.VMEM((3, 128, 512), bf16),
            pltpu.VMEM((3, 128, 512), bf16),
            pltpu.VMEM((3, 384, 128), f32),
            pltpu.VMEM((3, 384, 128), f32),
        ],
        24, 4 * 10**9, 8 * 10**6,
    )(pos, xin, cot, sides, ends, k1, k2, vectors)


def input_grad(d, xin, cot, k1, vectors):
    return call(
        input_kernel,
        [((3, 10, 23, 128), bf16)],
        [VMEM] * 5,
        [
            pltpu.VMEM((400, 128), f32),
            pltpu.VMEM((3, 384, 384), bf16),
            pltpu.VMEM((3, 320, 128), f32),
        ],
        16, 10**9, 3 * 10**6,
    )(d, xin, cot, k1, vectors)[0]


def combine(pos, own, got):
    return call(
        combine_kernel, [((7, 128, 128), f32)] + [((7, 128, 128), bf16)] * 3, [SMEM, VMEM, VMEM], [],
        16, 10**6, 10**6,
    )(pos, own, got)


def final(pos, mine, other):
    shape = (27, 128, 128)
    return call(
        final_kernel, [(shape, f32), (shape, f32), ((8, 128), f32), ((8, 128), f32)], [SMEM, VMEM, VMEM], [],
        16, 10**6, 10**6,
    )(pos, mine, other)


def body(block_input, cotangent, kernel_one, bias_one, kernel_two, scale_one, shift_one, scale_two, shift_two):
    xin, cot = jnp.swapaxes(block_input, 1, 2), jnp.swapaxes(cotangent, 1, 2)
    low = jnp.stack([xin[:, :2], cot[:, :2]])
    high = jnp.stack([xin[:, 8:], cot[:, 8:]])
    left, right = exchange(low, high, "wa", 32)

    def edge(s):
        main = jnp.stack([xin[:, :, s], cot[:, :, s]])
        return jnp.concatenate([left[:, :, :, s], main, right[:, :, :, s]], axis=2)

    above, below = exchange(edge(slice(0, 2)), edge(slice(21, 23)), "ha", 8)
    ha, wa = lax.axis_index("ha"), lax.axis_index("wa")
    y, x, c = ha % 4, wa // 8, wa % 2
    first, second = jnp.where(c == 0, x, y), jnp.where(c == 0, y, x)
    pos = jnp.stack([ha * 23 - 2, wa * 10 - 2, c, first, second]).astype(jnp.int32)
    vectors = jnp.pad(jnp.stack([bias_one, scale_one, shift_one, scale_two, shift_two]), ((0, 3), (0, 0)))
    xin, cot, k1, k2 = (jnp.where(wa < 32, v, jnp.zeros_like(v)) for v in (xin, cot, kernel_one, kernel_two))
    own, send, d = local(pos, xin, cot, jnp.stack([left, right]), jnp.stack([above, below]), k1, k2, vectors)
    gin = input_grad(d, xin, cot, k1, vectors)
    grad_one, grad_two, grad_bias_one, grad_bias_two = final(pos, *total(pos, own, send))
    shape = (3, 3, 3, 128, 128)
    return (
        jnp.swapaxes(gin, 1, 2), grad_one.reshape(shape), grad_bias_one[0], grad_two.reshape(shape), grad_bias_two[0],
    )


def solution(mesh):
    split = P(None, "ha", "wa", None)
    return jax.shard_map(
        body,
        mesh=mesh,
        in_specs=(split, split) + (P(),) * 7,
        out_specs=(split,) + (P(),) * 4,
        check_vma=False,
    )
```

profile of v0, /device:TPU:1, one launch (start us, length us, event | category | flops | bytes accessed | tf_op | source)
XLA Modules:
  0.0 112.1 jit_solution(8406370631049856139)
XLA Ops:
  0.6 0.9 slice_bitcast_fusion.2
  1.6 5.1 %collective-permute-start.1 = (bf16[2,3,2,23,128]{4,3,2,1,0:T(8,128)(2,1)S(1)}, bf16[2,3,2,23,128]{4,3,2,1,0:T(8,128)(2,1)S(1)}, u32[]{:S(2)}, u32[]{:S(2)}) collective-permute-start(bf16[2,3,2,23,128]{4,3,2,1,0:T(8,128)(2,1)S(1)} %pad_maximum_fusion.3), channel_id=1, source_target_pairs={{1,0},{2,1},{3,2},{4,3},{5,4},{6,5},{7,6},{8,7},{9,8},{10,9},{11,1... | collective-permute-start | bytes 211976 | tf_op jit(solution)/shard_map/ppermute | solution.py:73
  6.7 3.1 %collective-permute-start = (bf16[2,3,2,23,128]{4,3,2,1,0:T(8,128)(2,1)S(1)}, bf16[2,3,2,23,128]{4,3,2,1,0:T(8,128)(2,1)S(1)}, u32[]{:S(2)}, u32[]{:S(2)}) collective-permute-start(bf16[2,3,2,23,128]{4,3,2,1,0:T(8,128)(2,1)S(1)} %pad_maximum_fusion.2), channel_id=1, source_target_pairs={{0,1},{1,2},{2,3},{3,4},{4,5},{5,6},{6,7},{7,8},{8,9},{9,10},{10,1... | collective-permute-start | bytes 211976 | tf_op jit(solution)/shard_map/ppermute | solution.py:73
  9.8 1.0 broadcast_select_fusion.2
  10.9 1.3 %broadcast_select_fusion = (bf16[3,3,3,128,128]{4,3,2,1,0:T(8,128)(2,1)S(1)}, bf16[3,3,3,128,128]{4,3,2,1,0:T(8,128)(2,1)S(1)}) fusion(bf16[3,3,3,128,128]{4,3,2,1,0:T(8,128)(2,1)S(1)} %copy-done, pred[]{:T(512)S(6)} %lt.95, bf16[3,3,3,128,128]{4,3,2,1,0:T(8,128)(2,1)} %param.11), kind=kLoop, calls=%fused_computation | loop fusion | flops 884736 | bytes 3538945 | tf_op jit(solution)/shard_map/jit(_where)/select_n | solution.py:344
  12.3 1.0 slice_bitcast_fusion.6
  13.4 0.1 stack.95.pos
  13.6 1.3 %collective-permute-start.3 = (bf16[2,3,14,2,128]{4,3,2,1,0:T(2,128)(2,1)S(1)}, bf16[2,3,14,2,128]{4,3,2,1,0:T(2,128)(2,1)S(1)}, u32[]{:S(2)}, u32[]{:S(2)}) collective-permute-start(bf16[2,3,14,2,128]{4,3,2,1,0:T(2,128)(2,1)S(1)} %pad_maximum_fusion.5), channel_id=1, source_target_pairs={{32,0},{64,32},{96,64},{128,96},{160,128},{192,160},{224,192},{33,... | collective-permute-start | bytes 129032 | tf_op jit(solution)/shard_map/ppermute | solution.py:73
  15.0 4.0 %collective-permute-start.2 = (bf16[2,3,14,2,128]{4,3,2,1,0:T(2,128)(2,1)S(1)}, bf16[2,3,14,2,128]{4,3,2,1,0:T(2,128)(2,1)S(1)}, u32[]{:S(2)}, u32[]{:S(2)}) collective-permute-start(bf16[2,3,14,2,128]{4,3,2,1,0:T(2,128)(2,1)S(1)} %pad_maximum_fusion.4), channel_id=1, source_target_pairs={{0,32},{32,64},{64,96},{96,128},{128,160},{160,192},{192,224},{1,3... | collective-permute-start | bytes 129032 | tf_op jit(solution)/shard_map/ppermute | solution.py:73
  19.0 1.3 %collective-permute-done.2 = bf16[2,3,14,2,128]{4,3,2,1,0:T(2,128)(2,1)S(1)} collective-permute-done((bf16[2,3,14,2,128]{4,3,2,1,0:T(2,128)(2,1)S(1)}, bf16[2,3,14,2,128]{4,3,2,1,0:T(2,128)(2,1)S(1)}, u32[]{:S(2)}, u32[]{:S(2)}) %collective-permute-start.2) | collective-permute-done | bytes 43040 | tf_op jit(solution)/shard_map/ppermute | solution.py:73
  20.3 0.1 pad_maximum_fusion.1.ends
  20.4 12.8 %shard_map.128 = (f32[28,128,128]{2,1,0:T(8,128)S(1)}, bf16[28,128,128]{2,1,0:T(8,128)(2,1)S(1)}, bf16[3,384,128]{2,1,0:T(8,128)(2,1)S(1)}) custom-call(s32[5]{0:T(128)S(1)} %stack.95.pos, bf16[3,10,23,128]{3,2,1,0:T(8,128)(2,1)S(1)} %get-tuple-element.47.xin, bf16[3,10,23,128]{3,2,1,0:T(8,128)(2,1)S(1)} %get-tuple-element.46.cot, ...), custom_call_target="tpu_custom_call" | custom-call | flops 4000000000 | bytes 8000000 | tf_op jit(solution)/shard_map/pallas_call | solution.py:279
  33.2 0.6 collective-permute-start.4
  33.8 2.1 %collective-permute-done.4.got = bf16[28,128,128]{2,1,0:T(8,128)(2,1)S(1)} collective-permute-done((bf16[28,128,128]{2,1,0:T(8,128)(2,1)S(1)}, bf16[28,128,128]{2,1,0:T(8,128)(2,1)S(1)}, u32[]{:S(2)}, u32[]{:S(2)}) %collective-permute-start.4) | collective-permute-done | bytes 917536 | tf_op jit(solution)/shard_map/ppermute | solution.py:35
  35.9 0.8 shard_map.130
  36.6 4.6 %collective-permute-start.7 = (bf16[7,128,128]{2,1,0:T(8,128)(2,1)S(1)}, bf16[7,128,128]{2,1,0:T(8,128)(2,1)S(1)}, u32[]{:S(2)}, u32[]{:S(2)}) collective-permute-start(bf16[7,128,128]{2,1,0:T(8,128)(2,1)S(1)} %get-tuple-element.22), channel_id=1, source_target_pairs={{0,24},{1,97},{2,26},{3,99},{4,28},{5,101},{6,30},{7,103},{8,0},{9... | collective-permute-start | bytes 688136 | tf_op jit(solution)/shard_map/ppermute | solution.py:35
  41.2 0.7 collective-permute-start.5
  41.9 4.7 %collective-permute-done.7 = bf16[7,128,128]{2,1,0:T(8,128)(2,1)S(1)} collective-permute-done((bf16[7,128,128]{2,1,0:T(8,128)(2,1)S(1)}, bf16[7,128,128]{2,1,0:T(8,128)(2,1)S(1)}, u32[]{:S(2)}, u32[]{:S(2)}) %collective-permute-start.7) | collective-permute-done | bytes 229408 | tf_op jit(solution)/shard_map/ppermute | solution.py:35
  46.7 1.1 collective-permute-done.6
  47.7 2.1 %collective-permute-done.5 = bf16[7,128,128]{2,1,0:T(8,128)(2,1)S(1)} collective-permute-done((bf16[7,128,128]{2,1,0:T(8,128)(2,1)S(1)}, bf16[7,128,128]{2,1,0:T(8,128)(2,1)S(1)}, u32[]{:S(2)}, u32[]{:S(2)}) %collective-permute-start.5) | collective-permute-done | bytes 229408 | tf_op jit(solution)/shard_map/ppermute | solution.py:35
  49.8 0.1 convert_add_fusion
  49.9 9.6 %collective-permute-start.10 = (f32[224,128]{1,0:T(8,128)S(1)}, f32[224,128]{1,0:T(8,128)S(1)}, u32[]{:S(2)}, u32[]{:S(2)}) collective-permute-start(f32[224,128]{1,0:T(8,128)S(1)} %get-tuple-element.30), channel_id=1, source_target_pairs={{0,96},{1,25},{2,98},{3,27},{4,100},{5,29},{6,102},{7,31},{8,104},... | collective-permute-start | bytes 344072 | tf_op jit(solution)/shard_map/ppermute | solution.py:35
  59.6 0.2 collective-permute-start.9
  59.8 0.6 collective-permute-start.8
  60.4 2.1 %collective-permute-done.10 = f32[224,128]{1,0:T(8,128)S(1)} collective-permute-done((f32[224,128]{1,0:T(8,128)S(1)}, f32[224,128]{1,0:T(8,128)S(1)}, u32[]{:S(2)}, u32[]{:S(2)}) %collective-permute-start.10) | collective-permute-done | bytes 114720 | tf_op jit(solution)/shard_map/ppermute | solution.py:35
  62.5 2.3 %collective-permute-done.9 = f32[224,128]{1,0:T(8,128)S(1)} collective-permute-done((f32[224,128]{1,0:T(8,128)S(1)}, f32[224,128]{1,0:T(8,128)S(1)}, u32[]{:S(2)}, u32[]{:S(2)}) %collective-permute-start.9) | collective-permute-done | bytes 114720 | tf_op jit(solution)/shard_map/ppermute | solution.py:35
  64.8 1.1 collective-permute-done.8
  65.9 2.7 %collective-permute-start.11 = (f32[224,128]{1,0:T(8,128)S(1)}, f32[224,128]{1,0:T(8,128)S(1)}, u32[]{:S(2)}, u32[]{:S(2)}) collective-permute-start(f32[224,128]{1,0:T(8,128)S(1)} %fusion.1), channel_id=1, source_target_pairs={{0,128},{1,129},{2,130},{3,131},{4,132},{5,133},{6,134},{7,135},{8... | collective-permute-start | bytes 344072 | tf_op jit(solution)/shard_map/ppermute | solution.py:35
  68.6 2.2 %collective-permute-done.11 = f32[224,128]{1,0:T(8,128)S(1)} collective-permute-done((f32[224,128]{1,0:T(8,128)S(1)}, f32[224,128]{1,0:T(8,128)S(1)}, u32[]{:S(2)}, u32[]{:S(2)}) %collective-permute-start.11) | collective-permute-done | bytes 114720 | tf_op jit(solution)/shard_map/ppermute | solution.py:35
  70.8 0.1 collective-permute-start.14
  70.9 2.4 %collective-permute-start.13 = (bf16[224,128]{1,0:T(8,128)(2,1)S(1)}, bf16[224,128]{1,0:T(8,128)(2,1)S(1)}, u32[]{:S(2)}, u32[]{:S(2)}) collective-permute-start(bf16[224,128]{1,0:T(8,128)(2,1)S(1)} %add_convert_fusion.1), channel_id=1, source_target_pairs={{0,2},{1,3},{2,4},{3,5},{4,6},{5,7},{6,0},{7,1},{8,10},{9,11},{10,... | collective-permute-start | bytes 172040 | tf_op jit(solution)/shard_map/ppermute | solution.py:35
  73.2 0.2 collective-permute-start.12
  73.5 1.3 %collective-permute-done.14 = bf16[224,128]{1,0:T(8,128)(2,1)S(1)} collective-permute-done((bf16[224,128]{1,0:T(8,128)(2,1)S(1)}, bf16[224,128]{1,0:T(8,128)(2,1)S(1)}, u32[]{:S(2)}, u32[]{:S(2)}) %collective-permute-start.14) | collective-permute-done | bytes 57376 | tf_op jit(solution)/shard_map/ppermute | solution.py:35
  74.8 1.5 %collective-permute-done.13 = bf16[224,128]{1,0:T(8,128)(2,1)S(1)} collective-permute-done((bf16[224,128]{1,0:T(8,128)(2,1)S(1)}, bf16[224,128]{1,0:T(8,128)(2,1)S(1)}, u32[]{:S(2)}, u32[]{:S(2)}) %collective-permute-start.13) | collective-permute-done | bytes 57376 | tf_op jit(solution)/shard_map/ppermute | solution.py:35
  76.3 4.0 %collective-permute-done.12 = bf16[224,128]{1,0:T(8,128)(2,1)S(1)} collective-permute-done((bf16[224,128]{1,0:T(8,128)(2,1)S(1)}, bf16[224,128]{1,0:T(8,128)(2,1)S(1)}, u32[]{:S(2)}, u32[]{:S(2)}) %collective-permute-start.12) | collective-permute-done | bytes 57376 | tf_op jit(solution)/shard_map/ppermute | solution.py:35
  80.5 0.1 collective-permute-start.15
  80.7 2.5 %collective-permute-start.16 = (bf16[224,128]{1,0:T(8,128)(2,1)S(1)}, bf16[224,128]{1,0:T(8,128)(2,1)S(1)}, u32[]{:S(2)}, u32[]{:S(2)}) collective-permute-start(bf16[224,128]{1,0:T(8,128)(2,1)S(1)} %get-tuple-element.28), channel_id=1, source_target_pairs={{0,96},{1,25},{2,98},{3,27},{4,100},{5,29},{6,102},{7,31},{8,104},... | collective-permute-start | bytes 172040 | tf_op jit(solution)/shard_map/ppermute | solution.py:35
  83.2 1.9 %collective-permute-done.15 = bf16[224,128]{1,0:T(8,128)(2,1)S(1)} collective-permute-done((bf16[224,128]{1,0:T(8,128)(2,1)S(1)}, bf16[224,128]{1,0:T(8,128)(2,1)S(1)}, u32[]{:S(2)}, u32[]{:S(2)}) %collective-permute-start.15) | collective-permute-done | bytes 57376 | tf_op jit(solution)/shard_map/ppermute | solution.py:35
  85.1 2.6 %collective-permute-done.17 = bf16[224,128]{1,0:T(8,128)(2,1)S(1)} collective-permute-done((bf16[224,128]{1,0:T(8,128)(2,1)S(1)}, bf16[224,128]{1,0:T(8,128)(2,1)S(1)}, u32[]{:S(2)}, u32[]{:S(2)}) %collective-permute-start.17) | collective-permute-done | bytes 57376 | tf_op jit(solution)/shard_map/ppermute | solution.py:35
  87.8 0.1 collective-permute-start.18
  87.8 2.7 %collective-permute-start.19 = (bf16[4,224,128]{2,1,0:T(8,128)(2,1)S(1)}, bf16[4,224,128]{2,1,0:T(8,128)(2,1)S(1)}, u32[]{:S(2)}, u32[]{:S(2)}) collective-permute-start(bf16[4,224,128]{2,1,0:T(8,128)(2,1)S(1)} %bitcast_dynamic-update-slice_fusion.4), channel_id=1, source_target_pairs={{0,24},{1,97},{2,26},{3,99},{4,28},{5,101},{6,30},{7,103},{8,0},{9... | collective-permute-start | bytes 688136 | tf_op jit(solution)/shard_map/ppermute | solution.py:35
  90.5 0.1 broadcast_in_dim.32
  90.7 6.3 %collective-permute-done.18 = bf16[4,224,128]{2,1,0:T(8,128)(2,1)S(1)} collective-permute-done((bf16[4,224,128]{2,1,0:T(8,128)(2,1)S(1)}, bf16[4,224,128]{2,1,0:T(8,128)(2,1)S(1)}, u32[]{:S(2)}, u32[]{:S(2)}) %collective-permute-start.18) | collective-permute-done | bytes 229408 | tf_op jit(solution)/shard_map/ppermute | solution.py:35
  97.1 8.6 %collective-permute-start.21 = (bf16[28,128,128]{2,1,0:T(8,128)(2,1)S(1)}, bf16[28,128,128]{2,1,0:T(8,128)(2,1)S(1)}, u32[]{:S(2)}, u32[]{:S(2)}) collective-permute-start(bf16[28,128,128]{2,1,0:T(8,128)(2,1)S(1)} %bitcast.71), channel_id=1, source_target_pairs={{0,1},{1,0},{2,3},{3,2},{4,5},{5,4},{6,7},{7,6},{8,9},{9,8},{10,11... | collective-permute-start | bytes 2752520 | tf_op jit(solution)/shard_map/ppermute | solution.py:35
  105.7 2.7 %shard_map.129 = bf16[3,10,23,128]{3,2,1,0:T(8,128)(2,1)} custom-call(bf16[3,384,128]{2,1,0:T(8,128)(2,1)S(1)} %get-tuple-element.16.d, bf16[3,10,23,128]{3,2,1,0:T(8,128)(2,1)S(1)} %get-tuple-element.47.xin, bf16[3,10,23,128]{3,2,1,0:T(8,128)(2,1)S(1)} %get-tuple-element.46.cot, bf16[3,3,3,128,128]{4,3,2,1,0:T(8,128)(2,1)S(1)} %get-tuple-element.45.k1, ...), custom_call_target="tpu_custom_call" | custom-call | flops 1000000000 | bytes 3000000 | tf_op jit(solution)/shard_map/pallas_call | solution.py:300
  108.5 2.6 %shard_map.131 = (f32[27,128,128]{2,1,0:T(8,128)}, f32[27,128,128]{2,1,0:T(8,128)}, f32[8,128]{1,0:T(8,128)S(1)}, f32[8,128]{1,0:T(8,128)S(1)}) custom-call(s32[5]{0:T(128)S(1)} %stack.95.pos, bf16[28,128,128]{2,1,0:T(8,128)(2,1)S(1)} %bitcast.72, bf16[28,128,128]{2,1,0:T(8,128)(2,1)S(1)} %collective-permute-done.21.other), custom_call_target="tpu_custom_call" | custom-call | flops 1000000 | bytes 1000000 | tf_op jit(solution)/shard_map/pallas_call | solution.py:322
  111.1 0.5 slice_bitcast_fusion.9
  111.6 0.5 slice_bitcast_fusion.8
  (43 shorter events, 0.7 us)
Async XLA Ops:
  0.6 10.2 %copy-start = (bf16[3,3,3,128,128]{4,3,2,1,0:T(8,128)(2,1)S(1)}, bf16[3,3,3,128,128]{4,3,2,1,0:T(8,128)(2,1)}, u32[]{:S(2)}) copy-start(bf16[3,3,3,128,128]{4,3,2,1,0:T(8,128)(2,1)} %param.13) | copy-start | bytes 2654212
  1.6 11.9 %collective-permute-start.1 = (bf16[2,3,2,23,128]{4,3,2,1,0:T(8,128)(2,1)S(1)}, bf16[2,3,2,23,128]{4,3,2,1,0:T(8,128)(2,1)S(1)}, u32[]{:S(2)}, u32[]{:S(2)}) collective-permute-start(bf16[2,3,2,23,128]{4,3,2,1,0:T(8,128)(2,1)S(1)} %pad_maximum_fusion.3), channel_id=1, source_target_pairs={{1,0},{2,1},{3,2},{4,3},{5,4},{6,5},{7,6},{8,7},{9,8},{10,9},{11,1... | collective-permute-start | bytes 211976 | tf_op jit(solution)/shard_map/ppermute | solution.py:73
  6.7 6.7 %collective-permute-start = (bf16[2,3,2,23,128]{4,3,2,1,0:T(8,128)(2,1)S(1)}, bf16[2,3,2,23,128]{4,3,2,1,0:T(8,128)(2,1)S(1)}, u32[]{:S(2)}, u32[]{:S(2)}) collective-permute-start(bf16[2,3,2,23,128]{4,3,2,1,0:T(8,128)(2,1)S(1)} %pad_maximum_fusion.2), channel_id=1, source_target_pairs={{0,1},{1,2},{2,3},{3,4},{4,5},{5,6},{6,7},{7,8},{8,9},{9,10},{10,1... | collective-permute-start | bytes 211976 | tf_op jit(solution)/shard_map/ppermute | solution.py:73
  10.9 2.4 %copy-start.1 = (f32[128]{0:T(128)S(1)}, f32[128]{0:T(128)}, u32[]{:S(2)}) copy-start(f32[128]{0:T(128)} %param.12) | copy-start | bytes 1540
  10.9 2.4 %copy-start.2 = (f32[128]{0:T(128)S(1)}, f32[128]{0:T(128)}, u32[]{:S(2)}) copy-start(f32[128]{0:T(128)} %param.14) | copy-start | bytes 1540
  10.9 2.4 %copy-start.3 = (f32[128]{0:T(128)S(1)}, f32[128]{0:T(128)}, u32[]{:S(2)}) copy-start(f32[128]{0:T(128)} %param.15) | copy-start | bytes 1540
  10.9 2.4 %copy-start.4 = (f32[128]{0:T(128)S(1)}, f32[128]{0:T(128)}, u32[]{:S(2)}) copy-start(f32[128]{0:T(128)} %param.16) | copy-start | bytes 1540
  10.9 2.4 %copy-start.5 = (f32[128]{0:T(128)S(1)}, f32[128]{0:T(128)}, u32[]{:S(2)}) copy-start(f32[128]{0:T(128)} %param.17) | copy-start | bytes 1540
  13.6 5.4 %collective-permute-start.3 = (bf16[2,3,14,2,128]{4,3,2,1,0:T(2,128)(2,1)S(1)}, bf16[2,3,14,2,128]{4,3,2,1,0:T(2,128)(2,1)S(1)}, u32[]{:S(2)}, u32[]{:S(2)}) collective-permute-start(bf16[2,3,14,2,128]{4,3,2,1,0:T(2,128)(2,1)S(1)} %pad_maximum_fusion.5), channel_id=1, source_target_pairs={{32,0},{64,32},{96,64},{128,96},{160,128},{192,160},{224,192},{33,... | collective-permute-start | bytes 129032 | tf_op jit(solution)/shard_map/ppermute | solution.py:73
  15.0 5.3 %collective-permute-start.2 = (bf16[2,3,14,2,128]{4,3,2,1,0:T(2,128)(2,1)S(1)}, bf16[2,3,14,2,128]{4,3,2,1,0:T(2,128)(2,1)S(1)}, u32[]{:S(2)}, u32[]{:S(2)}) collective-permute-start(bf16[2,3,14,2,128]{4,3,2,1,0:T(2,128)(2,1)S(1)} %pad_maximum_fusion.4), channel_id=1, source_target_pairs={{0,32},{32,64},{64,96},{96,128},{128,160},{160,192},{192,224},{1,3... | collective-permute-start | bytes 129032 | tf_op jit(solution)/shard_map/ppermute | solution.py:73
  33.2 2.7 %collective-permute-start.4 = (bf16[28,128,128]{2,1,0:T(8,128)(2,1)S(1)}, bf16[28,128,128]{2,1,0:T(8,128)(2,1)S(1)}, u32[]{:S(2)}, u32[]{:S(2)}) collective-permute-start(bf16[28,128,128]{2,1,0:T(8,128)(2,1)S(1)} %get-tuple-element.18), channel_id=1, source_target_pairs={{0,1},{1,0},{2,3},{3,2},{4,5},{5,4},{6,7},{7,6},{8,9},{9,8},{10,11... | collective-permute-start | bytes 2752520 | tf_op jit(solution)/shard_map/ppermute | solution.py:35
  36.6 10.0 %collective-permute-start.7 = (bf16[7,128,128]{2,1,0:T(8,128)(2,1)S(1)}, bf16[7,128,128]{2,1,0:T(8,128)(2,1)S(1)}, u32[]{:S(2)}, u32[]{:S(2)}) collective-permute-start(bf16[7,128,128]{2,1,0:T(8,128)(2,1)S(1)} %get-tuple-element.22), channel_id=1, source_target_pairs={{0,24},{1,97},{2,26},{3,99},{4,28},{5,101},{6,30},{7,103},{8,0},{9... | collective-permute-start | bytes 688136 | tf_op jit(solution)/shard_map/ppermute | solution.py:35
  41.2 6.5 %collective-permute-start.6 = (bf16[7,128,128]{2,1,0:T(8,128)(2,1)S(1)}, bf16[7,128,128]{2,1,0:T(8,128)(2,1)S(1)}, u32[]{:S(2)}, u32[]{:S(2)}) collective-permute-start(bf16[7,128,128]{2,1,0:T(8,128)(2,1)S(1)} %get-tuple-element.21), channel_id=1, source_target_pairs={{0,16},{1,65},{2,18},{3,67},{4,20},{5,69},{6,22},{7,71},{8,24},{9,... | collective-permute-start | bytes 688136 | tf_op jit(solution)/shard_map/ppermute | solution.py:35
  41.2 8.5 %collective-permute-start.5 = (bf16[7,128,128]{2,1,0:T(8,128)(2,1)S(1)}, bf16[7,128,128]{2,1,0:T(8,128)(2,1)S(1)}, u32[]{:S(2)}, u32[]{:S(2)}) collective-permute-start(bf16[7,128,128]{2,1,0:T(8,128)(2,1)S(1)} %get-tuple-element.20), channel_id=1, source_target_pairs={{0,8},{1,33},{2,10},{3,35},{4,12},{5,37},{6,14},{7,39},{8,16},{9,4... | collective-permute-start | bytes 688136 | tf_op jit(solution)/shard_map/ppermute | solution.py:35
  49.9 12.6 %collective-permute-start.10 = (f32[224,128]{1,0:T(8,128)S(1)}, f32[224,128]{1,0:T(8,128)S(1)}, u32[]{:S(2)}, u32[]{:S(2)}) collective-permute-start(f32[224,128]{1,0:T(8,128)S(1)} %get-tuple-element.30), channel_id=1, source_target_pairs={{0,96},{1,25},{2,98},{3,27},{4,100},{5,29},{6,102},{7,31},{8,104},... | collective-permute-start | bytes 344072 | tf_op jit(solution)/shard_map/ppermute | solution.py:35
  59.6 5.2 %collective-permute-start.9 = (f32[224,128]{1,0:T(8,128)S(1)}, f32[224,128]{1,0:T(8,128)S(1)}, u32[]{:S(2)}, u32[]{:S(2)}) collective-permute-start(f32[224,128]{1,0:T(8,128)S(1)} %get-tuple-element.31), channel_id=1, source_target_pairs={{0,64},{1,17},{2,66},{3,19},{4,68},{5,21},{6,70},{7,23},{8,72},{9,... | collective-permute-start | bytes 344072 | tf_op jit(solution)/shard_map/ppermute | solution.py:35
  59.8 6.1 %collective-permute-start.8 = (f32[224,128]{1,0:T(8,128)S(1)}, f32[224,128]{1,0:T(8,128)S(1)}, u32[]{:S(2)}, u32[]{:S(2)}) collective-permute-start(f32[224,128]{1,0:T(8,128)S(1)} %get-tuple-element.29), channel_id=1, source_target_pairs={{0,32},{1,9},{2,34},{3,11},{4,36},{5,13},{6,38},{7,15},{8,40},{9,1... | collective-permute-start | bytes 344072 | tf_op jit(solution)/shard_map/ppermute | solution.py:35
  65.9 4.9 %collective-permute-start.11 = (f32[224,128]{1,0:T(8,128)S(1)}, f32[224,128]{1,0:T(8,128)S(1)}, u32[]{:S(2)}, u32[]{:S(2)}) collective-permute-start(f32[224,128]{1,0:T(8,128)S(1)} %fusion.1), channel_id=1, source_target_pairs={{0,128},{1,129},{2,130},{3,131},{4,132},{5,133},{6,134},{7,135},{8... | collective-permute-start | bytes 344072 | tf_op jit(solution)/shard_map/ppermute | solution.py:35
  70.8 4.0 %collective-permute-start.14 = (bf16[224,128]{1,0:T(8,128)(2,1)S(1)}, bf16[224,128]{1,0:T(8,128)(2,1)S(1)}, u32[]{:S(2)}, u32[]{:S(2)}) collective-permute-start(bf16[224,128]{1,0:T(8,128)(2,1)S(1)} %add_convert_fusion.1), channel_id=1, source_target_pairs={{0,6},{1,7},{2,0},{3,1},{4,2},{5,3},{6,4},{7,5},{8,14},{9,15},{10,... | collective-permute-start | bytes 172040 | tf_op jit(solution)/shard_map/ppermute | solution.py:35
  70.9 5.4 %collective-permute-start.13 = (bf16[224,128]{1,0:T(8,128)(2,1)S(1)}, bf16[224,128]{1,0:T(8,128)(2,1)S(1)}, u32[]{:S(2)}, u32[]{:S(2)}) collective-permute-start(bf16[224,128]{1,0:T(8,128)(2,1)S(1)} %add_convert_fusion.1), channel_id=1, source_target_pairs={{0,2},{1,3},{2,4},{3,5},{4,6},{5,7},{6,0},{7,1},{8,10},{9,11},{10,... | collective-permute-start | bytes 172040 | tf_op jit(solution)/shard_map/ppermute | solution.py:35
  73.2 7.1 %collective-permute-start.12 = (bf16[224,128]{1,0:T(8,128)(2,1)S(1)}, bf16[224,128]{1,0:T(8,128)(2,1)S(1)}, u32[]{:S(2)}, u32[]{:S(2)}) collective-permute-start(bf16[224,128]{1,0:T(8,128)(2,1)S(1)} %add_convert_fusion.1), channel_id=1, source_target_pairs={{0,4},{1,5},{2,6},{3,7},{4,0},{5,1},{6,2},{7,3},{8,12},{9,13},{10,... | collective-permute-start | bytes 172040 | tf_op jit(solution)/shard_map/ppermute | solution.py:35
  80.5 4.6 %collective-permute-start.15 = (bf16[224,128]{1,0:T(8,128)(2,1)S(1)}, bf16[224,128]{1,0:T(8,128)(2,1)S(1)}, u32[]{:S(2)}, u32[]{:S(2)}) collective-permute-start(bf16[224,128]{1,0:T(8,128)(2,1)S(1)} %get-tuple-element.28), channel_id=1, source_target_pairs={{0,32},{1,9},{2,34},{3,11},{4,36},{5,13},{6,38},{7,15},{8,40},{9,1... | collective-permute-start | bytes 172040 | tf_op jit(solution)/shard_map/ppermute | solution.py:35
  80.7 4.4 %collective-permute-start.16 = (bf16[224,128]{1,0:T(8,128)(2,1)S(1)}, bf16[224,128]{1,0:T(8,128)(2,1)S(1)}, u32[]{:S(2)}, u32[]{:S(2)}) collective-permute-start(bf16[224,128]{1,0:T(8,128)(2,1)S(1)} %get-tuple-element.28), channel_id=1, source_target_pairs={{0,96},{1,25},{2,98},{3,27},{4,100},{5,29},{6,102},{7,31},{8,104},... | collective-permute-start | bytes 172040 | tf_op jit(solution)/shard_map/ppermute | solution.py:35
  83.2 4.5 %collective-permute-start.17 = (bf16[224,128]{1,0:T(8,128)(2,1)S(1)}, bf16[224,128]{1,0:T(8,128)(2,1)S(1)}, u32[]{:S(2)}, u32[]{:S(2)}) collective-permute-start(bf16[224,128]{1,0:T(8,128)(2,1)S(1)} %get-tuple-element.28), channel_id=1, source_target_pairs={{0,64},{1,17},{2,66},{3,19},{4,68},{5,21},{6,70},{7,23},{8,72},{9,... | collective-permute-start | bytes 172040 | tf_op jit(solution)/shard_map/ppermute | solution.py:35
  87.8 9.2 %collective-permute-start.18 = (bf16[4,224,128]{2,1,0:T(8,128)(2,1)S(1)}, bf16[4,224,128]{2,1,0:T(8,128)(2,1)S(1)}, u32[]{:S(2)}, u32[]{:S(2)}) collective-permute-start(bf16[4,224,128]{2,1,0:T(8,128)(2,1)S(1)} %bitcast_dynamic-update-slice_fusion.4), channel_id=1, source_target_pairs={{0,8},{1,33},{2,10},{3,35},{4,12},{5,37},{6,14},{7,39},{8,16},{9,4... | collective-permute-start | bytes 688136 | tf_op jit(solution)/shard_map/ppermute | solution.py:35
  87.8 9.2 %collective-permute-start.19 = (bf16[4,224,128]{2,1,0:T(8,128)(2,1)S(1)}, bf16[4,224,128]{2,1,0:T(8,128)(2,1)S(1)}, u32[]{:S(2)}, u32[]{:S(2)}) collective-permute-start(bf16[4,224,128]{2,1,0:T(8,128)(2,1)S(1)} %bitcast_dynamic-update-slice_fusion.4), channel_id=1, source_target_pairs={{0,24},{1,97},{2,26},{3,99},{4,28},{5,101},{6,30},{7,103},{8,0},{9... | collective-permute-start | bytes 688136 | tf_op jit(solution)/shard_map/ppermute | solution.py:35
  90.5 6.6 %collective-permute-start.20 = (bf16[4,224,128]{2,1,0:T(8,128)(2,1)S(1)}, bf16[4,224,128]{2,1,0:T(8,128)(2,1)S(1)}, u32[]{:S(2)}, u32[]{:S(2)}) collective-permute-start(bf16[4,224,128]{2,1,0:T(8,128)(2,1)S(1)} %bitcast_dynamic-update-slice_fusion.4), channel_id=1, source_target_pairs={{0,16},{1,65},{2,18},{3,67},{4,20},{5,69},{6,22},{7,71},{8,24},{9,... | collective-permute-start | bytes 688136 | tf_op jit(solution)/shard_map/ppermute | solution.py:35
  97.1 11.3 %collective-permute-start.21 = (bf16[28,128,128]{2,1,0:T(8,128)(2,1)S(1)}, bf16[28,128,128]{2,1,0:T(8,128)(2,1)S(1)}, u32[]{:S(2)}, u32[]{:S(2)}) collective-permute-start(bf16[28,128,128]{2,1,0:T(8,128)(2,1)S(1)} %bitcast.71), channel_id=1, source_target_pairs={{0,1},{1,0},{2,3},{3,2},{4,5},{5,4},{6,7},{7,6},{8,9},{9,8},{10,11... | collective-permute-start | bytes 2752520 | tf_op jit(solution)/shard_map/ppermute | solution.py:35
where the time goes:
time: 112 us
  starting transfers between devices  49.1 us (44%)
  waiting for transfers between devices  36.6 us (33%)
  Pallas kernels  18.9 us (17%)
  local copies, waits for them, and re-layouts  3.47 us (3%)
  other arithmetic  2.86 us (3%)
  between operations  1.16 us (1%)
    ppermute x18, starting transfers between devices, shifted(): return lax.ppermute(v, AXES, shift_pairs(axis, size, k))  35.6 us
    ppermute x18, waiting for transfers between devices, shifted(): return lax.ppermute(v, AXES, shift_pairs(axis, size, k))  35.3 us
    ppermute x4, starting transfers between devices, exchange(): return (lax.ppermute(high, axis, up), lax.ppermute(low, axis, down))  13.5 us
    pallas_call x1, Pallas kernels, local(): call(local_kernel, [((28, 128, 128), f32), ((28, 128, 128), bf16), ((3, 3...  12.8 us
    pallas_call x1, Pallas kernels, input_grad(): call(input_kernel, [((3, 10, 23, 128), bf16)], [VMEM] * 5, [pltpu.VMEM((4...  2.72 us
    pallas_call x1, Pallas kernels, final(): call(final_kernel, [(shape, f32), (shape, f32), ((8, 128), f32), ((8, 128...  2.61 us
    select_n x2, other arithmetic, body(): jnp.where(wa < 32, v, jnp.zeros_like(v))  2.35 us
  transfers between devices with their start and end apart: 22, of which 15 were waited for; matrix products, arithmetic and copies ran while one was open for 3% of the time, Pallas kernels for 2%

commit v1 on v0

v1 whole, which is shorter than its diff:
```python
import math

import jax
import jax.numpy as jnp
from jax import lax
from jax.experimental import pallas as pl
from jax.experimental.pallas import tpu as pltpu
from jax.sharding import PartitionSpec as P

CELLS = 176640
AXES = ("ha", "wa")
f32 = jnp.float32
bf16 = jnp.bfloat16


def coords(d):
    return {"zl": d // 128, "y": (d // 32) % 4, "x": (d // 8) % 4, "zh": (d // 2) % 4, "c": d % 2}


def device_of(p):
    return (((p["zl"] * 4 + p["y"]) * 4 + p["x"]) * 4 + p["zh"]) * 2 + p["c"]


def shift_pairs(axis, size, k):
    pairs = []
    for d in range(256):
        p = coords(d)
        a = axis if isinstance(axis, str) else axis[p["c"]]
        p[a] = (p[a] + k) % size
        pairs.append((d, device_of(p)))
    return pairs


def shifted(v, axis, size, k):
    return lax.ppermute(v, AXES, shift_pairs(axis, size, k))


ORDER = (2, 1, 3)


def scatter(own, send, axis):
    got = {k: shifted(send[k], axis, 4, k) for k in ORDER}
    return own + got[1].astype(f32) + got[2].astype(f32) + got[3].astype(f32)


def gather(v, axis, here):
    got = {k: shifted(v, axis, 4, k) for k in ORDER}
    out = lax.dynamic_update_index_in_dim(jnp.zeros((4,) + v.shape, v.dtype), v, here, 0)
    for k in (1, 3, 2):
        out = lax.dynamic_update_index_in_dim(out, got[k], (here - k) % 4, 0)
    return out


def total(pos, own, got):
    first, second = pos[3], pos[4]
    kept, *sends = combine(pos, own, got)
    v = scatter(kept, dict(enumerate(sends, 1)), ("x", "y"))
    v = v.reshape(4, 224, 128)
    parts = {k: lax.dynamic_index_in_dim(v, (second + k) % 4, 0, keepdims=False) for k in range(4)}
    v = scatter(parts[0], parts, ("y", "x"))
    v = v + shifted(v, "zl", 2, 1)
    v = v.astype(bf16)
    got = {k: shifted(v, "zh", 4, k) for k in ORDER}
    v = ((v.astype(f32) + got[2].astype(f32)) + (got[1].astype(f32) + got[3].astype(f32))).astype(bf16)
    v = gather(v, ("y", "x"), second)
    v = gather(v, ("x", "y"), first).reshape(28, 128, 128)
    return v, shifted(v, "c", 2, 1)


def exchange(low, high, axis, size):
    up = [(i, i + 1) for i in range(size - 1)]
    down = [(i + 1, i) for i in range(size - 1)]
    return lax.ppermute(high, axis, up), lax.ppermute(low, axis, down)


def adjoint(field, k, kw, acc, n):
    for s in range(3):
        w = jnp.concatenate(
            [jnp.concatenate([k[kt, kh, kw] for kh in range(3)], axis=1) for kt in range(2 - s, 3)], axis=0
        )
        part = lax.dot_general(
            field[s, rows(2 - kw, n), :], w, (((1,), (1,)), ((), ())), preferred_element_type=f32
        )
        for j, kt in enumerate(range(2 - s, 3)):
            acc[s - 2 + kt] += part[:, j * 128:(j + 1) * 128]


def slope(z, s):
    return s * (1.0 + z * (1.0 - s))


def rows(i, n):
    return pl.ds(pl.multiple_of(i * 32, 32), n)


def local_kernel(
    pos, xin, cot, sides, ends, k1, k2, vectors,
    send_out, bias_out, d_out, field, cotan,
    line, x_all, a3, g3, a2, acc, acc2,
):
    row0, col0, core = pos[0], pos[1], pos[2]
    bias1, scale1, shift1, scale2, shift2 = (vectors[i:i + 1, :] for i in range(5))
    line[...] = jnp.zeros_like(line)
    x_all[...] = jnp.zeros_like(x_all)
    for half in range(2):
        cotan[half, 960:1024, :] = jnp.zeros((64, 384), bf16)

    def masks(first, n):
        q = lax.broadcasted_iota(jnp.int32, (n, 128), 0)
        col, row = (q >> 5) + first, q & 31
        r, c = row + row0, col + col0
        inside = (r >= 0) & (r < 184) & (c >= 0) & (c < 320)
        return (row >= 2) & (row < 25), inside

    def place(dst, base, which, main, t):
        for w in range(14):
            at = base + w * 32
            if 2 <= w < 12:
                dst[at + 2:at + 25, :] = main[t, w - 2].astype(f32)
            else:
                dst[at + 2:at + 25, :] = sides[w // 12, which, t, w % 12].astype(f32)
            dst[at:at + 2, :] = ends[0, which, t, w].astype(f32)
            dst[at + 25:at + 27, :] = ends[1, which, t, w].astype(f32)

    def own_cells(half, t, first):
        at = pl.ds(pl.multiple_of(t * 320, 64), 320)
        for k, o in enumerate((9, 8, 7)):
            cotan[half, at, k * 128:(k + 1) * 128] = line[o + first:o + first + 320, :].astype(bf16)

    def enter(t, bias):
        own, inside = masks(0, 448)
        line[8:456, :] = jnp.zeros((448, 128), f32)
        place(line, 8, 1, cot, t)
        place(x_all, 0, 0, xin, t)
        for k, o in enumerate((9, 8, 7)):
            g3[t, :, k * 128:(k + 1) * 128] = line[o:o + 448, :].astype(bf16)
        go = jnp.where(own, line[8:456, :], 0.0)
        line[8:456, :] = go
        own_cells(1, t, 64)
        z = x_all[...] * scale1 + shift1
        line[8:456, :] = jnp.where(inside, z * jax.nn.sigmoid(z), 0.0)
        for k, o in enumerate((7, 8, 9)):
            a3[t, :, k * 128:(k + 1) * 128] = line[o:o + 448, :].astype(bf16)
        return bias + jnp.sum(go[64:384].reshape(40, 8, 128), axis=0)

    bias_two = lax.fori_loop(0, 3, enter, jnp.zeros((8, 128), f32))
    for t in range(3):
        acc[t] = jnp.zeros((384, 128), f32)
        acc2[t] = jnp.zeros((384, 128), f32)

    def first_convs(kw, carry):
        for s in range(3):
            w = jnp.concatenate(
                [jnp.concatenate([k1[kt, kh, kw] for kh in range(3)], axis=0) for kt in range(s, 3)], axis=1
            )
            part = jnp.dot(a3[s, rows(kw, 384), :], w, preferred_element_type=f32)
            for j, kt in enumerate(range(s, 3)):
                acc[s + 2 - kt] += part[:, j * 128:(j + 1) * 128]
        adjoint(g3, k2, kw, acc2, 384)
        return carry

    lax.fori_loop(0, 3, first_convs, 0)
    line[392:400, :] = jnp.zeros((8, 128), f32)

    def middle(t, bias):
        own, inside = masks(1, 384)
        z = (acc[t] + bias1) * scale2 + shift2
        s = jax.nn.sigmoid(z)
        a2[t] = jnp.where(inside, z * s, 0.0).astype(bf16)
        d = jnp.where(inside, acc2[t] * slope(z, s) * scale2, 0.0).astype(bf16)
        d_out[t] = d
        do = jnp.where(own, d.astype(f32), 0.0)
        line[8:392, :] = do
        own_cells(0, t, 32)
        return bias + jnp.sum(do[32:352].reshape(40, 8, 128), axis=0)

    bias_one = lax.fori_loop(0, 3, middle, jnp.zeros((8, 128), f32))
    tail = [jnp.zeros((64, 128), bf16)]
    for kw in range(3):
        at = slice(kw * 128, (kw + 1) * 128)
        first = [a3[t, (1 + kw) * 32:(1 + kw) * 32 + 320, 128:256] for t in range(3)]
        field[0, at, :] = jnp.transpose(jnp.concatenate(first + tail, axis=0))
        second = [a2[t, kw * 32:kw * 32 + 320, :] for t in range(3)]
        field[1, at, :] = jnp.transpose(jnp.concatenate(second + tail, axis=0))
    low = lax.broadcasted_iota(jnp.int32, (128, 128), 0)
    b1 = jnp.broadcast_to(jnp.sum(bias_one, axis=0, keepdims=True), (128, 128))
    b2 = jnp.broadcast_to(jnp.sum(bias_two, axis=0, keepdims=True), (128, 128))
    biases = jnp.where(low < 8, b1, jnp.where(low < 16, b2, 0.0))
    bias_out[...] = biases
    kernel_grads(field, cotan, 1 - core, biases, send_out)


def kernel_grads(field, cotan, half, biases, out):
    for kt, n in enumerate((384, 640, 1024)):
        start = (2 - kt) * 320
        part = jnp.dot(
            field[half, :, 0:n], cotan[half, start:start + n, :], preferred_element_type=f32
        ).astype(out.dtype)
        for kh in range(3):
            for kw in range(3):
                out[kt * 9 + kh * 3 + kw] = part[kw * 128:(kw + 1) * 128, kh * 128:(kh + 1) * 128]
    out[27] = jnp.where(half == 0, biases, 0.0).astype(out.dtype)


def own_kernel(pos, field, cotan, biases, out):
    kernel_grads(field, cotan, pos[2], biases[...], out)


def input_kernel(d, xin, cot, k1, vectors, gin, line, d3, acc):
    scale1, shift1 = vectors[1:2, :], vectors[2:3, :]
    line[...] = jnp.zeros_like(line)
    for t in range(3):
        acc[t] = jnp.zeros((320, 128), f32)
        line[8:392, :] = d[t].astype(f32)
        for k, o in enumerate((9, 8, 7)):
            d3[t, :, k * 128:(k + 1) * 128] = line[o:o + 384, :].astype(bf16)

    def convs(kw, carry):
        adjoint(d3, k1, kw, acc, 320)
        return carry

    lax.fori_loop(0, 3, convs, 0)
    for t in range(3):
        for w in range(10):
            z = xin[t, w].astype(f32) * scale1 + shift1
            change = acc[t, w * 32 + 2:w * 32 + 25, :] * (slope(z, jax.nn.sigmoid(z)) * scale1)
            gin[t, w] = (cot[t, w].astype(f32) + change).astype(bf16)


def combine_kernel(pos, own, got, kept, to1, to2, to3):
    def one(j, carry):
        for k, out in enumerate((kept, to1, to2, to3)):
            b = lax.rem(pos[3] + k, 4) * 7 + j
            out[j] = (own[b] + got[b].astype(f32)).astype(out.dtype)
        return carry

    lax.fori_loop(0, 7, one, 0)


PIECE = 9


def final_kernel(pos, mine, other, one, two, bias_one, bias_two, wide_one, wide_two, sems):
    factor = 1.0 / math.sqrt(CELLS)

    def emit(low, high):
        copies = []
        for p in range(0, 27, PIECE):
            for i, (src, wide, out) in enumerate(((low, wide_one, one), (high, wide_two, two))):
                wide[p:p + PIECE] = src[p:p + PIECE].astype(f32) * factor
                at = pl.ds(p, PIECE)
                copies.append(pltpu.make_async_copy(wide.at[at], out.at[at], sems.at[i, p // PIECE]))
                copies[-1].start()
        bias_one[...] = low[27, 0:1, :].astype(f32) * factor
        bias_two[...] = low[27, 8:9, :].astype(f32) * factor
        for copy in copies:
            copy.wait()

    @pl.when(pos[2] == 0)
    def _():
        emit(mine, other)

    @pl.when(pos[2] != 0)
    def _():
        emit(other, mine)


VMEM = pl.BlockSpec(memory_space=pltpu.VMEM)
HBM = pl.BlockSpec(memory_space=pltpu.HBM)
SMEM = pl.BlockSpec(memory_space=pltpu.SMEM)


def call(kernel, out, inputs, scratch, mib, flops, size, places=None):
    return pl.pallas_call(
        kernel,
        out_shape=tuple(jax.ShapeDtypeStruct(*o) for o in out),
        in_specs=inputs,
        out_specs=places or (VMEM,) * len(out),
        scratch_shapes=scratch,
        compiler_params=pltpu.CompilerParams(vmem_limit_bytes=mib * 1024 * 1024),
        cost_estimate=pl.CostEstimate(flops=flops, bytes_accessed=size, transcendentals=0),
    )


def local(pos, xin, cot, sides, ends, k1, k2, vectors):
    return call(
        local_kernel,
        [
            ((28, 128, 128), bf16), ((128, 128), f32), ((3, 384, 128), bf16),
            ((2, 384, 1024), bf16), ((2, 1024, 384), bf16),
        ],
        [SMEM] + [VMEM] * 7,
        [
            pltpu.VMEM((464, 128), f32),
            pltpu.VMEM((448, 128), f32),
            pltpu.VMEM((3, 448, 384), bf16),
            pltpu.VMEM((3, 448, 384), bf16),
            pltpu.VMEM((3, 384, 128), bf16),
            pltpu.VMEM((3, 384, 128), f32),
            pltpu.VMEM((3, 384, 128), f32),
        ],
        24, 3 * 10**9, 8 * 10**6,
    )(pos, xin, cot, sides, ends, k1, k2, vectors)


def own_grads(pos, field, cotan, biases):
    return call(
        own_kernel, [((28, 128, 128), f32)], [SMEM, VMEM, VMEM, VMEM], [], 16, 10**9, 3 * 10**6,
    )(pos, field, cotan, biases)[0]


def input_grad(d, xin, cot, k1, vectors):
    return call(
        input_kernel,
        [((3, 10, 23, 128), bf16)],
        [VMEM] * 5,
        [
            pltpu.VMEM((400, 128), f32),
            pltpu.VMEM((3, 384, 384), bf16),
            pltpu.VMEM((3, 320, 128), f32),
        ],
        16, 10**9, 3 * 10**6,
    )(d, xin, cot, k1, vectors)[0]


def combine(pos, own, got):
    return call(
        combine_kernel, [((7, 128, 128), f32)] + [((7, 128, 128), bf16)] * 3, [SMEM, VMEM, VMEM], [],
        16, 10**6, 10**6,
    )(pos, own, got)


def final(pos, mine, other):
    shape = (27, 128, 128)
    return call(
        final_kernel, [(shape, f32), (shape, f32), ((1, 128), f32), ((1, 128), f32)], [SMEM, VMEM, VMEM],
        [pltpu.VMEM(shape, f32), pltpu.VMEM(shape, f32), pltpu.SemaphoreType.DMA((2, 3))],
        56, 10**6, 10**6, (HBM, HBM, VMEM, VMEM),
    )(pos, mine, other)


def body(block_input, cotangent, kernel_one, bias_one, kernel_two, scale_one, shift_one, scale_two, shift_two):
    xin, cot = jnp.swapaxes(block_input, 1, 2), jnp.swapaxes(cotangent, 1, 2)
    low = jnp.stack([xin[:, :2], cot[:, :2]])
    high = jnp.stack([xin[:, 8:], cot[:, 8:]])
    left, right = exchange(low, high, "wa", 32)

    def edge(s):
        main = jnp.stack([xin[:, :, s], cot[:, :, s]])
        return jnp.concatenate([left[:, :, :, s], main, right[:, :, :, s]], axis=2)

    above, below = exchange(edge(slice(0, 2)), edge(slice(21, 23)), "ha", 8)
    ha, wa = lax.axis_index("ha"), lax.axis_index("wa")
    y, x, c = ha % 4, wa // 8, wa % 2
    first, second = jnp.where(c == 0, x, y), jnp.where(c == 0, y, x)
    pos = jnp.stack([ha * 23 - 2, wa * 10 - 2, c, first, second]).astype(jnp.int32)
    vectors = jnp.pad(jnp.stack([bias_one, scale_one, shift_one, scale_two, shift_two]), ((0, 3), (0, 0)))
    xin, cot, k1, k2 = (jnp.where(wa < 32, v, jnp.zeros_like(v)) for v in (xin, cot, kernel_one, kernel_two))
    send, biases, d, field, cotan = local(pos, xin, cot, jnp.stack([left, right]), jnp.stack([above, below]), k1, k2, vectors)
    got = shifted(send, "c", 2, 1)
    own = own_grads(pos, field, cotan, biases)
    gin = input_grad(d, xin, cot, k1, vectors)
    grad_one, grad_two, grad_bias_one, grad_bias_two = final(pos, *total(pos, own, got))
    shape = (3, 3, 3, 128, 128)
    return (
        jnp.swapaxes(gin, 1, 2), grad_one.reshape(shape), grad_bias_one[0], grad_two.reshape(shape), grad_bias_two[0],
    )


def solution(mesh):
    split = P(None, "ha", "wa", None)
    return jax.shard_map(
        body,
        mesh=mesh,
        in_specs=(split, split) + (P(),) * 7,
        out_specs=(split,) + (P(),) * 4,
        check_vma=False,
    )
```

time: 112 us -> 108 us (0.964)
  Pallas kernels: 18.9 us -> 15.5 us
  waiting for transfers between devices: 36.6 us -> 35 us
    pallas_call x2 -> x3, Pallas kernels: 15.4 us -> 12.2 us  [the longest x1 6.81 us: local(): call(local_kernel, [((28, 128, 128), bf16), ((128, 128), f32), ((3, 384,...]
    ppermute x18, waiting for transfers between devices: 35.3 us -> 33.7 us  [shifted(): return lax.ppermute(v, AXES, shift_pairs(axis, size, k))]
  transfers between devices with their start and end apart: 22 -> 22, of which waited for: 15 -> 15; matrix products, arithmetic and copies ran while one was open for 3% -> 4% of each run, Pallas kernels for 2% -> 4%
where the time goes in v1:
time: 108 us; the launch traced here: 107 us
  starting transfers between devices  49 us (45%)
  waiting for transfers between devices  35 us (32%)
  Pallas kernels  15.5 us (14%)
  local copies, waits for them, and re-layouts  3.37 us (3%)
  other arithmetic  2.97 us (3%)
  between operations  1.34 us (1%)
    ppermute x18, starting transfers between devices, shifted(): return lax.ppermute(v, AXES, shift_pairs(axis, size, k))  35.5 us
    ppermute x18, waiting for transfers between devices, shifted(): return lax.ppermute(v, AXES, shift_pairs(axis, size, k))  33.7 us
    ppermute x4, starting transfers between devices, exchange(): return (lax.ppermute(high, axis, up), lax.ppermute(low, axis, down))  13.5 us
    pallas_call x1, Pallas kernels, local(): call(local_kernel, [((28, 128, 128), bf16), ((128, 128), f32), ((3, 384,...  6.81 us
    pallas_call x1, Pallas kernels, final(): call(final_kernel, [(shape, f32), (shape, f32), ((1, 128), f32), ((1, 128...  3.87 us
    pallas_call x1, Pallas kernels, input_grad(): call(input_kernel, [((3, 10, 23, 128), bf16)], [VMEM] * 5, [pltpu.VMEM((4...  2.48 us
    select_n x2, other arithmetic, body(): jnp.where(wa < 32, v, jnp.zeros_like(v))  2.46 us
  transfers between devices with their start and end apart: 22, of which 15 were waited for; matrix products, arithmetic and copies ran while one was open for 4% of the time, Pallas kernels for 4%

profile of v1, /device:TPU:1, one launch (start us, length us, event | category | flops | bytes accessed | tf_op | source)
XLA Modules:
  0.0 107.2 jit_solution(6505434502731310521)
XLA Ops:
  0.6 0.9 slice_bitcast_fusion.2
  1.6 5.1 %collective-permute-start.1 = (bf16[2,3,2,23,128]{4,3,2,1,0:T(8,128)(2,1)S(1)}, bf16[2,3,2,23,128]{4,3,2,1,0:T(8,128)(2,1)S(1)}, u32[]{:S(2)}, u32[]{:S(2)}) collective-permute-start(bf16[2,3,2,23,128]{4,3,2,1,0:T(8,128)(2,1)S(1)} %pad_maximum_fusion.3), channel_id=1, source_target_pairs={{1,0},{2,1},{3,2},{4,3},{5,4},{6,5},{7,6},{8,7},{9,8},{10,9},{11,1... | collective-permute-start | bytes 211976 | tf_op jit(solution)/shard_map/ppermute | solution.py:73
  6.7 3.1 %collective-permute-start = (bf16[2,3,2,23,128]{4,3,2,1,0:T(8,128)(2,1)S(1)}, bf16[2,3,2,23,128]{4,3,2,1,0:T(8,128)(2,1)S(1)}, u32[]{:S(2)}, u32[]{:S(2)}) collective-permute-start(bf16[2,3,2,23,128]{4,3,2,1,0:T(8,128)(2,1)S(1)} %pad_maximum_fusion.2), channel_id=1, source_target_pairs={{0,1},{1,2},{2,3},{3,4},{4,5},{5,6},{6,7},{7,8},{8,9},{9,10},{10,1... | collective-permute-start | bytes 211976 | tf_op jit(solution)/shard_map/ppermute | solution.py:73
  9.8 1.0 broadcast_select_fusion.2
  10.9 1.4 %broadcast_select_fusion = (bf16[3,3,3,128,128]{4,3,2,1,0:T(8,128)(2,1)S(1)}, bf16[3,3,3,128,128]{4,3,2,1,0:T(8,128)(2,1)S(1)}) fusion(bf16[3,3,3,128,128]{4,3,2,1,0:T(8,128)(2,1)S(1)} %copy-done.3, pred[]{:T(512)S(6)} %lt.95, bf16[3,3,3,128,128]{4,3,2,1,0:T(8,128)(2,1)} %param.11), kind=kLoop, calls=%fused_computation | loop fusion | flops 884736 | bytes 3538945 | tf_op jit(solution)/shard_map/jit(_where)/select_n | solution.py:358
  12.4 1.0 slice_bitcast_fusion.6
  13.5 0.1 stack.95.pos
  13.7 1.3 %collective-permute-start.3 = (bf16[2,3,14,2,128]{4,3,2,1,0:T(2,128)(2,1)S(1)}, bf16[2,3,14,2,128]{4,3,2,1,0:T(2,128)(2,1)S(1)}, u32[]{:S(2)}, u32[]{:S(2)}) collective-permute-start(bf16[2,3,14,2,128]{4,3,2,1,0:T(2,128)(2,1)S(1)} %pad_maximum_fusion.5), channel_id=1, source_target_pairs={{32,0},{64,32},{96,64},{128,96},{160,128},{192,160},{224,192},{33,... | collective-permute-start | bytes 129032 | tf_op jit(solution)/shard_map/ppermute | solution.py:73
  15.1 4.0 %collective-permute-start.2 = (bf16[2,3,14,2,128]{4,3,2,1,0:T(2,128)(2,1)S(1)}, bf16[2,3,14,2,128]{4,3,2,1,0:T(2,128)(2,1)S(1)}, u32[]{:S(2)}, u32[]{:S(2)}) collective-permute-start(bf16[2,3,14,2,128]{4,3,2,1,0:T(2,128)(2,1)S(1)} %pad_maximum_fusion.4), channel_id=1, source_target_pairs={{0,32},{32,64},{64,96},{96,128},{128,160},{160,192},{192,224},{1,3... | collective-permute-start | bytes 129032 | tf_op jit(solution)/shard_map/ppermute | solution.py:73
  19.1 1.3 %collective-permute-done.2 = bf16[2,3,14,2,128]{4,3,2,1,0:T(2,128)(2,1)S(1)} collective-permute-done((bf16[2,3,14,2,128]{4,3,2,1,0:T(2,128)(2,1)S(1)}, bf16[2,3,14,2,128]{4,3,2,1,0:T(2,128)(2,1)S(1)}, u32[]{:S(2)}, u32[]{:S(2)}) %collective-permute-start.2) | collective-permute-done | bytes 43040 | tf_op jit(solution)/shard_map/ppermute | solution.py:73
  20.4 0.1 pad_maximum_fusion.1.ends
  20.5 6.8 %shard_map.128 = (bf16[28,128,128]{2,1,0:T(8,128)(2,1)S(1)}, f32[128,128]{1,0:T(8,128)S(1)}, bf16[3,384,128]{2,1,0:T(8,128)(2,1)S(1)}, bf16[2,384,1024]{2,1,0:T(8,128)(2,1)S(1)}, bf16[2,1024,384]{2,1,0:T(8,128)(2,1)S(1)}) custom-call(s32[5]{0:T(128)S(1)} %stack.95.pos, bf16[3,10,23,128]{3,2,1,0:T(8,128)(2,1)S(1)} %get-tuple-element.51.xin, ...), custom_call_target="tpu_custom_call" | custom-call | flops 3000000000 | bytes 8000000 | tf_op jit(solution)/shard_map/pallas_call | solution.py:286
  27.3 0.6 collective-permute-start.4
  27.9 1.6 %shard_map.130.own = f32[28,128,128]{2,1,0:T(8,128)S(1)} custom-call(s32[5]{0:T(128)S(1)} %stack.95.pos, bf16[2,384,1024]{2,1,0:T(8,128)(2,1)S(1)} %get-tuple-element.19.field, bf16[2,1024,384]{2,1,0:T(8,128)(2,1)S(1)} %get-tuple-element.20.cotan, f32[128,128]{1,0:T(8,128)S(1)} %get-tuple-element.21.biases), custom_call_target="tpu_custom_call" | custom-call | flops 1000000000 | bytes 3000000 | tf_op jit(solution)/shard_map/pallas_call | solution.py:307
  29.5 0.5 collective-permute-done.4.got
  30.0 0.8 shard_map.131
  30.8 4.6 %collective-permute-start.7 = (bf16[7,128,128]{2,1,0:T(8,128)(2,1)S(1)}, bf16[7,128,128]{2,1,0:T(8,128)(2,1)S(1)}, u32[]{:S(2)}, u32[]{:S(2)}) collective-permute-start(bf16[7,128,128]{2,1,0:T(8,128)(2,1)S(1)} %get-tuple-element.26), channel_id=1, source_target_pairs={{0,24},{1,97},{2,26},{3,99},{4,28},{5,101},{6,30},{7,103},{8,0},{9... | collective-permute-start | bytes 688136 | tf_op jit(solution)/shard_map/ppermute | solution.py:35
  35.4 0.7 collective-permute-start.5
  36.1 4.7 %collective-permute-done.7 = bf16[7,128,128]{2,1,0:T(8,128)(2,1)S(1)} collective-permute-done((bf16[7,128,128]{2,1,0:T(8,128)(2,1)S(1)}, bf16[7,128,128]{2,1,0:T(8,128)(2,1)S(1)}, u32[]{:S(2)}, u32[]{:S(2)}) %collective-permute-start.7) | collective-permute-done | bytes 229408 | tf_op jit(solution)/shard_map/ppermute | solution.py:35
  40.8 1.1 collective-permute-done.6
  41.8 2.1 %collective-permute-done.5 = bf16[7,128,128]{2,1,0:T(8,128)(2,1)S(1)} collective-permute-done((bf16[7,128,128]{2,1,0:T(8,128)(2,1)S(1)}, bf16[7,128,128]{2,1,0:T(8,128)(2,1)S(1)}, u32[]{:S(2)}, u32[]{:S(2)}) %collective-permute-start.5) | collective-permute-done | bytes 229408 | tf_op jit(solution)/shard_map/ppermute | solution.py:35
  43.9 0.1 convert_add_fusion
  44.1 9.5 %collective-permute-start.10 = (f32[224,128]{1,0:T(8,128)S(1)}, f32[224,128]{1,0:T(8,128)S(1)}, u32[]{:S(2)}, u32[]{:S(2)}) collective-permute-start(f32[224,128]{1,0:T(8,128)S(1)} %get-tuple-element.34), channel_id=1, source_target_pairs={{0,96},{1,25},{2,98},{3,27},{4,100},{5,29},{6,102},{7,31},{8,104},... | collective-permute-start | bytes 344072 | tf_op jit(solution)/shard_map/ppermute | solution.py:35
  53.6 0.2 collective-permute-start.9
  53.8 0.6 collective-permute-start.8
  54.4 2.1 %collective-permute-done.10 = f32[224,128]{1,0:T(8,128)S(1)} collective-permute-done((f32[224,128]{1,0:T(8,128)S(1)}, f32[224,128]{1,0:T(8,128)S(1)}, u32[]{:S(2)}, u32[]{:S(2)}) %collective-permute-start.10) | collective-permute-done | bytes 114720 | tf_op jit(solution)/shard_map/ppermute | solution.py:35
  56.6 2.3 %collective-permute-done.9 = f32[224,128]{1,0:T(8,128)S(1)} collective-permute-done((f32[224,128]{1,0:T(8,128)S(1)}, f32[224,128]{1,0:T(8,128)S(1)}, u32[]{:S(2)}, u32[]{:S(2)}) %collective-permute-start.9) | collective-permute-done | bytes 114720 | tf_op jit(solution)/shard_map/ppermute | solution.py:35
  58.8 1.1 collective-permute-done.8
  59.9 2.7 %collective-permute-start.11 = (f32[224,128]{1,0:T(8,128)S(1)}, f32[224,128]{1,0:T(8,128)S(1)}, u32[]{:S(2)}, u32[]{:S(2)}) collective-permute-start(f32[224,128]{1,0:T(8,128)S(1)} %fusion.1), channel_id=1, source_target_pairs={{0,128},{1,129},{2,130},{3,131},{4,132},{5,133},{6,134},{7,135},{8... | collective-permute-start | bytes 344072 | tf_op jit(solution)/shard_map/ppermute | solution.py:35
  62.6 2.2 %collective-permute-done.11 = f32[224,128]{1,0:T(8,128)S(1)} collective-permute-done((f32[224,128]{1,0:T(8,128)S(1)}, f32[224,128]{1,0:T(8,128)S(1)}, u32[]{:S(2)}, u32[]{:S(2)}) %collective-permute-start.11) | collective-permute-done | bytes 114720 | tf_op jit(solution)/shard_map/ppermute | solution.py:35
  64.8 0.1 collective-permute-start.14
  64.9 2.4 %collective-permute-start.13 = (bf16[224,128]{1,0:T(8,128)(2,1)S(1)}, bf16[224,128]{1,0:T(8,128)(2,1)S(1)}, u32[]{:S(2)}, u32[]{:S(2)}) collective-permute-start(bf16[224,128]{1,0:T(8,128)(2,1)S(1)} %add_convert_fusion.1), channel_id=1, source_target_pairs={{0,2},{1,3},{2,4},{3,5},{4,6},{5,7},{6,0},{7,1},{8,10},{9,11},{10,... | collective-permute-start | bytes 172040 | tf_op jit(solution)/shard_map/ppermute | solution.py:35
  67.3 0.2 collective-permute-start.12
  67.5 1.3 %collective-permute-done.14 = bf16[224,128]{1,0:T(8,128)(2,1)S(1)} collective-permute-done((bf16[224,128]{1,0:T(8,128)(2,1)S(1)}, bf16[224,128]{1,0:T(8,128)(2,1)S(1)}, u32[]{:S(2)}, u32[]{:S(2)}) %collective-permute-start.14) | collective-permute-done | bytes 57376 | tf_op jit(solution)/shard_map/ppermute | solution.py:35
  68.8 1.5 %collective-permute-done.13 = bf16[224,128]{1,0:T(8,128)(2,1)S(1)} collective-permute-done((bf16[224,128]{1,0:T(8,128)(2,1)S(1)}, bf16[224,128]{1,0:T(8,128)(2,1)S(1)}, u32[]{:S(2)}, u32[]{:S(2)}) %collective-permute-start.13) | collective-permute-done | bytes 57376 | tf_op jit(solution)/shard_map/ppermute | solution.py:35
  70.3 4.1 %collective-permute-done.12 = bf16[224,128]{1,0:T(8,128)(2,1)S(1)} collective-permute-done((bf16[224,128]{1,0:T(8,128)(2,1)S(1)}, bf16[224,128]{1,0:T(8,128)(2,1)S(1)}, u32[]{:S(2)}, u32[]{:S(2)}) %collective-permute-start.12) | collective-permute-done | bytes 57376 | tf_op jit(solution)/shard_map/ppermute | solution.py:35
  74.5 0.1 collective-permute-start.15
  74.7 2.5 %collective-permute-start.16 = (bf16[224,128]{1,0:T(8,128)(2,1)S(1)}, bf16[224,128]{1,0:T(8,128)(2,1)S(1)}, u32[]{:S(2)}, u32[]{:S(2)}) collective-permute-start(bf16[224,128]{1,0:T(8,128)(2,1)S(1)} %get-tuple-element.32), channel_id=1, source_target_pairs={{0,96},{1,25},{2,98},{3,27},{4,100},{5,29},{6,102},{7,31},{8,104},... | collective-permute-start | bytes 172040 | tf_op jit(solution)/shard_map/ppermute | solution.py:35
  77.2 1.9 %collective-permute-done.15 = bf16[224,128]{1,0:T(8,128)(2,1)S(1)} collective-permute-done((bf16[224,128]{1,0:T(8,128)(2,1)S(1)}, bf16[224,128]{1,0:T(8,128)(2,1)S(1)}, u32[]{:S(2)}, u32[]{:S(2)}) %collective-permute-start.15) | collective-permute-done | bytes 57376 | tf_op jit(solution)/shard_map/ppermute | solution.py:35
  79.1 2.6 %collective-permute-done.17 = bf16[224,128]{1,0:T(8,128)(2,1)S(1)} collective-permute-done((bf16[224,128]{1,0:T(8,128)(2,1)S(1)}, bf16[224,128]{1,0:T(8,128)(2,1)S(1)}, u32[]{:S(2)}, u32[]{:S(2)}) %collective-permute-start.17) | collective-permute-done | bytes 57376 | tf_op jit(solution)/shard_map/ppermute | solution.py:35
  81.8 0.1 collective-permute-start.18
  81.9 2.7 %collective-permute-start.19 = (bf16[4,224,128]{2,1,0:T(8,128)(2,1)S(1)}, bf16[4,224,128]{2,1,0:T(8,128)(2,1)S(1)}, u32[]{:S(2)}, u32[]{:S(2)}) collective-permute-start(bf16[4,224,128]{2,1,0:T(8,128)(2,1)S(1)} %bitcast_dynamic-update-slice_fusion.4), channel_id=1, source_target_pairs={{0,24},{1,97},{2,26},{3,99},{4,28},{5,101},{6,30},{7,103},{8,0},{9... | collective-permute-start | bytes 688136 | tf_op jit(solution)/shard_map/ppermute | solution.py:35
  84.5 0.1 broadcast_in_dim.32
  84.7 6.3 %collective-permute-done.18 = bf16[4,224,128]{2,1,0:T(8,128)(2,1)S(1)} collective-permute-done((bf16[4,224,128]{2,1,0:T(8,128)(2,1)S(1)}, bf16[4,224,128]{2,1,0:T(8,128)(2,1)S(1)}, u32[]{:S(2)}, u32[]{:S(2)}) %collective-permute-start.18) | collective-permute-done | bytes 229408 | tf_op jit(solution)/shard_map/ppermute | solution.py:35
  91.2 8.6 %collective-permute-start.21 = (bf16[28,128,128]{2,1,0:T(8,128)(2,1)S(1)}, bf16[28,128,128]{2,1,0:T(8,128)(2,1)S(1)}, u32[]{:S(2)}, u32[]{:S(2)}) collective-permute-start(bf16[28,128,128]{2,1,0:T(8,128)(2,1)S(1)} %bitcast.69), channel_id=1, source_target_pairs={{0,1},{1,0},{2,3},{3,2},{4,5},{5,4},{6,7},{7,6},{8,9},{9,8},{10,11... | collective-permute-start | bytes 2752520 | tf_op jit(solution)/shard_map/ppermute | solution.py:35
  99.8 2.5 %shard_map.129 = bf16[3,10,23,128]{3,2,1,0:T(8,128)(2,1)} custom-call(bf16[3,384,128]{2,1,0:T(8,128)(2,1)S(1)} %get-tuple-element.18.d, bf16[3,10,23,128]{3,2,1,0:T(8,128)(2,1)S(1)} %get-tuple-element.51.xin, bf16[3,10,23,128]{3,2,1,0:T(8,128)(2,1)S(1)} %get-tuple-element.50.cot, bf16[3,3,3,128,128]{4,3,2,1,0:T(8,128)(2,1)S(1)} %get-tuple-element.49.k1, ...), custom_call_target="tpu_custom_call" | custom-call | flops 1000000000 | bytes 3000000 | tf_op jit(solution)/shard_map/pallas_call | solution.py:313
  102.3 0.9 copy-done.2
  103.2 3.9 %shard_map.132 = (f32[27,128,128]{2,1,0:T(8,128)}, f32[27,128,128]{2,1,0:T(8,128)}, f32[1,128]{1,0:T(1,128)}, f32[1,128]{1,0:T(1,128)}) custom-call(s32[5]{0:T(128)} %copy-done, bf16[28,128,128]{2,1,0:T(8,128)(2,1)} %bitcast.70, bf16[28,128,128]{2,1,0:T(8,128)(2,1)} %copy-done.2), custom_call_target="tpu_custom_call" | custom-call | flops 1000000 | bytes 1000000 | tf_op jit(solution)/shard_map/pallas_call | solution.py:335
  (48 shorter events, 0.7 us)
Async XLA Ops:
  0.6 10.2 %copy-start.3 = (bf16[3,3,3,128,128]{4,3,2,1,0:T(8,128)(2,1)S(1)}, bf16[3,3,3,128,128]{4,3,2,1,0:T(8,128)(2,1)}, u32[]{:S(2)}) copy-start(bf16[3,3,3,128,128]{4,3,2,1,0:T(8,128)(2,1)} %param.13) | copy-start | bytes 2654212
  1.6 12.0 %collective-permute-start.1 = (bf16[2,3,2,23,128]{4,3,2,1,0:T(8,128)(2,1)S(1)}, bf16[2,3,2,23,128]{4,3,2,1,0:T(8,128)(2,1)S(1)}, u32[]{:S(2)}, u32[]{:S(2)}) collective-permute-start(bf16[2,3,2,23,128]{4,3,2,1,0:T(8,128)(2,1)S(1)} %pad_maximum_fusion.3), channel_id=1, source_target_pairs={{1,0},{2,1},{3,2},{4,3},{5,4},{6,5},{7,6},{8,7},{9,8},{10,9},{11,1... | collective-permute-start | bytes 211976 | tf_op jit(solution)/shard_map/ppermute | solution.py:73
  6.7 6.9 %collective-permute-start = (bf16[2,3,2,23,128]{4,3,2,1,0:T(8,128)(2,1)S(1)}, bf16[2,3,2,23,128]{4,3,2,1,0:T(8,128)(2,1)S(1)}, u32[]{:S(2)}, u32[]{:S(2)}) collective-permute-start(bf16[2,3,2,23,128]{4,3,2,1,0:T(8,128)(2,1)S(1)} %pad_maximum_fusion.2), channel_id=1, source_target_pairs={{0,1},{1,2},{2,3},{3,4},{4,5},{5,6},{6,7},{7,8},{8,9},{9,10},{10,1... | collective-permute-start | bytes 211976 | tf_op jit(solution)/shard_map/ppermute | solution.py:73
  10.9 2.5 %copy-start.4 = (f32[128]{0:T(128)S(1)}, f32[128]{0:T(128)}, u32[]{:S(2)}) copy-start(f32[128]{0:T(128)} %param.12) | copy-start | bytes 1540
  10.9 2.5 %copy-start.5 = (f32[128]{0:T(128)S(1)}, f32[128]{0:T(128)}, u32[]{:S(2)}) copy-start(f32[128]{0:T(128)} %param.14) | copy-start | bytes 1540
  10.9 2.5 %copy-start.6 = (f32[128]{0:T(128)S(1)}, f32[128]{0:T(128)}, u32[]{:S(2)}) copy-start(f32[128]{0:T(128)} %param.15) | copy-start | bytes 1540
  10.9 2.5 %copy-start.7 = (f32[128]{0:T(128)S(1)}, f32[128]{0:T(128)}, u32[]{:S(2)}) copy-start(f32[128]{0:T(128)} %param.16) | copy-start | bytes 1540
  10.9 2.5 %copy-start.8 = (f32[128]{0:T(128)S(1)}, f32[128]{0:T(128)}, u32[]{:S(2)}) copy-start(f32[128]{0:T(128)} %param.17) | copy-start | bytes 1540
  13.6 16.4 %copy-start = (s32[5]{0:T(128)}, s32[5]{0:T(128)S(1)}, u32[]{:S(2)}) copy-start(s32[5]{0:T(128)S(1)} %stack.95.pos) | copy-start | bytes 64
  13.7 5.4 %collective-permute-start.3 = (bf16[2,3,14,2,128]{4,3,2,1,0:T(2,128)(2,1)S(1)}, bf16[2,3,14,2,128]{4,3,2,1,0:T(2,128)(2,1)S(1)}, u32[]{:S(2)}, u32[]{:S(2)}) collective-permute-start(bf16[2,3,14,2,128]{4,3,2,1,0:T(2,128)(2,1)S(1)} %pad_maximum_fusion.5), channel_id=1, source_target_pairs={{32,0},{64,32},{96,64},{128,96},{160,128},{192,160},{224,192},{33,... | collective-permute-start | bytes 129032 | tf_op jit(solution)/shard_map/ppermute | solution.py:73
  15.1 5.3 %collective-permute-start.2 = (bf16[2,3,14,2,128]{4,3,2,1,0:T(2,128)(2,1)S(1)}, bf16[2,3,14,2,128]{4,3,2,1,0:T(2,128)(2,1)S(1)}, u32[]{:S(2)}, u32[]{:S(2)}) collective-permute-start(bf16[2,3,14,2,128]{4,3,2,1,0:T(2,128)(2,1)S(1)} %pad_maximum_fusion.4), channel_id=1, source_target_pairs={{0,32},{32,64},{64,96},{96,128},{128,160},{160,192},{192,224},{1,3... | collective-permute-start | bytes 129032 | tf_op jit(solution)/shard_map/ppermute | solution.py:73
  27.3 2.7 %collective-permute-start.4 = (bf16[28,128,128]{2,1,0:T(8,128)(2,1)S(1)}, bf16[28,128,128]{2,1,0:T(8,128)(2,1)S(1)}, u32[]{:S(2)}, u32[]{:S(2)}) collective-permute-start(bf16[28,128,128]{2,1,0:T(8,128)(2,1)S(1)} %get-tuple-element.22), channel_id=1, source_target_pairs={{0,1},{1,0},{2,3},{3,2},{4,5},{5,4},{6,7},{7,6},{8,9},{9,8},{10,11... | collective-permute-start | bytes 2752520 | tf_op jit(solution)/shard_map/ppermute | solution.py:35
  30.8 10.0 %collective-permute-start.7 = (bf16[7,128,128]{2,1,0:T(8,128)(2,1)S(1)}, bf16[7,128,128]{2,1,0:T(8,128)(2,1)S(1)}, u32[]{:S(2)}, u32[]{:S(2)}) collective-permute-start(bf16[7,128,128]{2,1,0:T(8,128)(2,1)S(1)} %get-tuple-element.26), channel_id=1, source_target_pairs={{0,24},{1,97},{2,26},{3,99},{4,28},{5,101},{6,30},{7,103},{8,0},{9... | collective-permute-start | bytes 688136 | tf_op jit(solution)/shard_map/ppermute | solution.py:35
  35.4 6.5 %collective-permute-start.6 = (bf16[7,128,128]{2,1,0:T(8,128)(2,1)S(1)}, bf16[7,128,128]{2,1,0:T(8,128)(2,1)S(1)}, u32[]{:S(2)}, u32[]{:S(2)}) collective-permute-start(bf16[7,128,128]{2,1,0:T(8,128)(2,1)S(1)} %get-tuple-element.25), channel_id=1, source_target_pairs={{0,16},{1,65},{2,18},{3,67},{4,20},{5,69},{6,22},{7,71},{8,24},{9,... | collective-permute-start | bytes 688136 | tf_op jit(solution)/shard_map/ppermute | solution.py:35
  35.4 8.5 %collective-permute-start.5 = (bf16[7,128,128]{2,1,0:T(8,128)(2,1)S(1)}, bf16[7,128,128]{2,1,0:T(8,128)(2,1)S(1)}, u32[]{:S(2)}, u32[]{:S(2)}) collective-permute-start(bf16[7,128,128]{2,1,0:T(8,128)(2,1)S(1)} %get-tuple-element.24), channel_id=1, source_target_pairs={{0,8},{1,33},{2,10},{3,35},{4,12},{5,37},{6,14},{7,39},{8,16},{9,4... | collective-permute-start | bytes 688136 | tf_op jit(solution)/shard_map/ppermute | solution.py:35
  44.1 12.5 %collective-permute-start.10 = (f32[224,128]{1,0:T(8,128)S(1)}, f32[224,128]{1,0:T(8,128)S(1)}, u32[]{:S(2)}, u32[]{:S(2)}) collective-permute-start(f32[224,128]{1,0:T(8,128)S(1)} %get-tuple-element.34), channel_id=1, source_target_pairs={{0,96},{1,25},{2,98},{3,27},{4,100},{5,29},{6,102},{7,31},{8,104},... | collective-permute-start | bytes 344072 | tf_op jit(solution)/shard_map/ppermute | solution.py:35
  53.6 5.2 %collective-permute-start.9 = (f32[224,128]{1,0:T(8,128)S(1)}, f32[224,128]{1,0:T(8,128)S(1)}, u32[]{:S(2)}, u32[]{:S(2)}) collective-permute-start(f32[224,128]{1,0:T(8,128)S(1)} %get-tuple-element.35), channel_id=1, source_target_pairs={{0,64},{1,17},{2,66},{3,19},{4,68},{5,21},{6,70},{7,23},{8,72},{9,... | collective-permute-start | bytes 344072 | tf_op jit(solution)/shard_map/ppermute | solution.py:35
  53.8 6.1 %collective-permute-start.8 = (f32[224,128]{1,0:T(8,128)S(1)}, f32[224,128]{1,0:T(8,128)S(1)}, u32[]{:S(2)}, u32[]{:S(2)}) collective-permute-start(f32[224,128]{1,0:T(8,128)S(1)} %get-tuple-element.33), channel_id=1, source_target_pairs={{0,32},{1,9},{2,34},{3,11},{4,36},{5,13},{6,38},{7,15},{8,40},{9,1... | collective-permute-start | bytes 344072 | tf_op jit(solution)/shard_map/ppermute | solution.py:35
  59.9 4.9 %collective-permute-start.11 = (f32[224,128]{1,0:T(8,128)S(1)}, f32[224,128]{1,0:T(8,128)S(1)}, u32[]{:S(2)}, u32[]{:S(2)}) collective-permute-start(f32[224,128]{1,0:T(8,128)S(1)} %fusion.1), channel_id=1, source_target_pairs={{0,128},{1,129},{2,130},{3,131},{4,132},{5,133},{6,134},{7,135},{8... | collective-permute-start | bytes 344072 | tf_op jit(solution)/shard_map/ppermute | solution.py:35
  64.8 4.0 %collective-permute-start.14 = (bf16[224,128]{1,0:T(8,128)(2,1)S(1)}, bf16[224,128]{1,0:T(8,128)(2,1)S(1)}, u32[]{:S(2)}, u32[]{:S(2)}) collective-permute-start(bf16[224,128]{1,0:T(8,128)(2,1)S(1)} %add_convert_fusion.1), channel_id=1, source_target_pairs={{0,6},{1,7},{2,0},{3,1},{4,2},{5,3},{6,4},{7,5},{8,14},{9,15},{10,... | collective-permute-start | bytes 172040 | tf_op jit(solution)/shard_map/ppermute | solution.py:35
  64.9 5.4 %collective-permute-start.13 = (bf16[224,128]{1,0:T(8,128)(2,1)S(1)}, bf16[224,128]{1,0:T(8,128)(2,1)S(1)}, u32[]{:S(2)}, u32[]{:S(2)}) collective-permute-start(bf16[224,128]{1,0:T(8,128)(2,1)S(1)} %add_convert_fusion.1), channel_id=1, source_target_pairs={{0,2},{1,3},{2,4},{3,5},{4,6},{5,7},{6,0},{7,1},{8,10},{9,11},{10,... | collective-permute-start | bytes 172040 | tf_op jit(solution)/shard_map/ppermute | solution.py:35
  67.3 7.1 %collective-permute-start.12 = (bf16[224,128]{1,0:T(8,128)(2,1)S(1)}, bf16[224,128]{1,0:T(8,128)(2,1)S(1)}, u32[]{:S(2)}, u32[]{:S(2)}) collective-permute-start(bf16[224,128]{1,0:T(8,128)(2,1)S(1)} %add_convert_fusion.1), channel_id=1, source_target_pairs={{0,4},{1,5},{2,6},{3,7},{4,0},{5,1},{6,2},{7,3},{8,12},{9,13},{10,... | collective-permute-start | bytes 172040 | tf_op jit(solution)/shard_map/ppermute | solution.py:35
  74.5 4.6 %collective-permute-start.15 = (bf16[224,128]{1,0:T(8,128)(2,1)S(1)}, bf16[224,128]{1,0:T(8,128)(2,1)S(1)}, u32[]{:S(2)}, u32[]{:S(2)}) collective-permute-start(bf16[224,128]{1,0:T(8,128)(2,1)S(1)} %get-tuple-element.32), channel_id=1, source_target_pairs={{0,32},{1,9},{2,34},{3,11},{4,36},{5,13},{6,38},{7,15},{8,40},{9,1... | collective-permute-start | bytes 172040 | tf_op jit(solution)/shard_map/ppermute | solution.py:35
  74.7 4.4 %collective-permute-start.16 = (bf16[224,128]{1,0:T(8,128)(2,1)S(1)}, bf16[224,128]{1,0:T(8,128)(2,1)S(1)}, u32[]{:S(2)}, u32[]{:S(2)}) collective-permute-start(bf16[224,128]{1,0:T(8,128)(2,1)S(1)} %get-tuple-element.32), channel_id=1, source_target_pairs={{0,96},{1,25},{2,98},{3,27},{4,100},{5,29},{6,102},{7,31},{8,104},... | collective-permute-start | bytes 172040 | tf_op jit(solution)/shard_map/ppermute | solution.py:35
  77.2 4.5 %collective-permute-start.17 = (bf16[224,128]{1,0:T(8,128)(2,1)S(1)}, bf16[224,128]{1,0:T(8,128)(2,1)S(1)}, u32[]{:S(2)}, u32[]{:S(2)}) collective-permute-start(bf16[224,128]{1,0:T(8,128)(2,1)S(1)} %get-tuple-element.32), channel_id=1, source_target_pairs={{0,64},{1,17},{2,66},{3,19},{4,68},{5,21},{6,70},{7,23},{8,72},{9,... | collective-permute-start | bytes 172040 | tf_op jit(solution)/shard_map/ppermute | solution.py:35
  81.8 9.2 %collective-permute-start.18 = (bf16[4,224,128]{2,1,0:T(8,128)(2,1)S(1)}, bf16[4,224,128]{2,1,0:T(8,128)(2,1)S(1)}, u32[]{:S(2)}, u32[]{:S(2)}) collective-permute-start(bf16[4,224,128]{2,1,0:T(8,128)(2,1)S(1)} %bitcast_dynamic-update-slice_fusion.4), channel_id=1, source_target_pairs={{0,8},{1,33},{2,10},{3,35},{4,12},{5,37},{6,14},{7,39},{8,16},{9,4... | collective-permute-start | bytes 688136 | tf_op jit(solution)/shard_map/ppermute | solution.py:35
  81.9 9.2 %collective-permute-start.19 = (bf16[4,224,128]{2,1,0:T(8,128)(2,1)S(1)}, bf16[4,224,128]{2,1,0:T(8,128)(2,1)S(1)}, u32[]{:S(2)}, u32[]{:S(2)}) collective-permute-start(bf16[4,224,128]{2,1,0:T(8,128)(2,1)S(1)} %bitcast_dynamic-update-slice_fusion.4), channel_id=1, source_target_pairs={{0,24},{1,97},{2,26},{3,99},{4,28},{5,101},{6,30},{7,103},{8,0},{9... | collective-permute-start | bytes 688136 | tf_op jit(solution)/shard_map/ppermute | solution.py:35
  84.5 6.6 %collective-permute-start.20 = (bf16[4,224,128]{2,1,0:T(8,128)(2,1)S(1)}, bf16[4,224,128]{2,1,0:T(8,128)(2,1)S(1)}, u32[]{:S(2)}, u32[]{:S(2)}) collective-permute-start(bf16[4,224,128]{2,1,0:T(8,128)(2,1)S(1)} %bitcast_dynamic-update-slice_fusion.4), channel_id=1, source_target_pairs={{0,16},{1,65},{2,18},{3,67},{4,20},{5,69},{6,22},{7,71},{8,24},{9,... | collective-permute-start | bytes 688136 | tf_op jit(solution)/shard_map/ppermute | solution.py:35
  91.2 11.1 %copy-start.1 = (bf16[4,4,224,128]{3,2,1,0:T(8,128)(2,1)}, bf16[4,4,224,128]{3,2,1,0:T(8,128)(2,1)S(1)}, u32[]{:S(2)}) copy-start(bf16[4,4,224,128]{3,2,1,0:T(8,128)(2,1)S(1)} %bitcast_dynamic-update-slice_fusion) | copy-start | bytes 2752516
  91.2 11.1 %collective-permute-start.21 = (bf16[28,128,128]{2,1,0:T(8,128)(2,1)S(1)}, bf16[28,128,128]{2,1,0:T(8,128)(2,1)S(1)}, u32[]{:S(2)}, u32[]{:S(2)}) collective-permute-start(bf16[28,128,128]{2,1,0:T(8,128)(2,1)S(1)} %bitcast.69), channel_id=1, source_target_pairs={{0,1},{1,0},{2,3},{3,2},{4,5},{5,4},{6,7},{7,6},{8,9},{9,8},{10,11... | collective-permute-start | bytes 2752520 | tf_op jit(solution)/shard_map/ppermute | solution.py:35
  102.3 0.9 copy-start.2

commit v2 on v1

--- a/solution.py
+++ b/solution.py
@@ -38,9 +38,9 @@
 ORDER = (2, 1, 3)
 
 
-def scatter(own, send, axis):
-    got = {k: shifted(send[k], axis, 4, k) for k in ORDER}
-    return own + got[1].astype(f32) + got[2].astype(f32) + got[3].astype(f32)
+def scatter(send, axis):
+    got = {k: shifted(send[k - 1], axis, 4, k) for k in ORDER}
+    return got[1], got[2], got[3]
 
 
 def gather(v, axis, here):
@@ -54,17 +54,18 @@
 def total(pos, own, got):
     first, second = pos[3], pos[4]
     kept, *sends = combine(pos, own, got)
-    v = scatter(kept, dict(enumerate(sends, 1)), ("x", "y"))
-    v = v.reshape(4, 224, 128)
-    parts = {k: lax.dynamic_index_in_dim(v, (second + k) % 4, 0, keepdims=False) for k in range(4)}
-    v = scatter(parts[0], parts, ("y", "x"))
+    kept, *sends = fold(pos, kept, scatter(sends, ("x", "y")))
+    got = scatter(sends, ("y", "x"))
+    v = kept + got[0].astype(f32) + got[1].astype(f32) + got[2].astype(f32)
     v = v + shifted(v, "zl", 2, 1)
     v = v.astype(bf16)
     got = {k: shifted(v, "zh", 4, k) for k in ORDER}
     v = ((v.astype(f32) + got[2].astype(f32)) + (got[1].astype(f32) + got[3].astype(f32))).astype(bf16)
     v = gather(v, ("y", "x"), second)
     v = gather(v, ("x", "y"), first).reshape(28, 128, 128)
-    return v, shifted(v, "c", 2, 1)
+    other = shifted(v, "c", 2, 1)
+    one, two = write_mine(pos, v)
+    return write_other(pos, v, other, one, two)
 
 
 def exchange(low, high, axis, size):
@@ -237,32 +238,55 @@
     lax.fori_loop(0, 7, one, 0)
 
 
+def fold_kernel(pos, own, got1, got2, got3, kept, to1, to2, to3):
+    for k, out in enumerate((kept, to1, to2, to3)):
+        at = lax.rem(pos[4] + k, 4)
+        value = own[at] + got1[at].astype(f32) + got2[at].astype(f32) + got3[at].astype(f32)
+        out[...] = value.astype(out.dtype)
+
+
+FACTOR = 1.0 / math.sqrt(CELLS)
 PIECE = 9
 
 
-def final_kernel(pos, mine, other, one, two, bias_one, bias_two, wide_one, wide_two, sems):
-    factor = 1.0 / math.sqrt(CELLS)
-
-    def emit(low, high):
+def write_half(half, src, one, two, wide, sems):
+    def emit(out):
         copies = []
         for p in range(0, 27, PIECE):
-            for i, (src, wide, out) in enumerate(((low, wide_one, one), (high, wide_two, two))):
-                wide[p:p + PIECE] = src[p:p + PIECE].astype(f32) * factor
-                at = pl.ds(p, PIECE)
-                copies.append(pltpu.make_async_copy(wide.at[at], out.at[at], sems.at[i, p // PIECE]))
-                copies[-1].start()
-        bias_one[...] = low[27, 0:1, :].astype(f32) * factor
-        bias_two[...] = low[27, 8:9, :].astype(f32) * factor
+            wide[p:p + PIECE] = src[p:p + PIECE].astype(f32) * FACTOR
+            at = pl.ds(p, PIECE)
+            copies.append(pltpu.make_async_copy(wide.at[at], out.at[at], sems.at[p // PIECE]))
+            copies[-1].start()
         for copy in copies:
             copy.wait()
 
+    @pl.when(half == 0)
+    def _():
+        emit(one)
+
+    @pl.when(half != 0)
+    def _():
+        emit(two)
+
+
+def mine_kernel(pos, mine, one, two, wide, sems):
+    write_half(pos[2], mine, one, two, wide, sems)
+
+
+def other_kernel(pos, mine, other, one_in, two_in, one, two, bias_one, bias_two, wide, sems):
+    def biases(src):
+        bias_one[...] = src[27, 0:1, :].astype(f32) * FACTOR
+        bias_two[...] = src[27, 8:9, :].astype(f32) * FACTOR
+
     @pl.when(pos[2] == 0)
     def _():
-        emit(mine, other)
+        biases(mine)
 
     @pl.when(pos[2] != 0)
     def _():
-        emit(other, mine)
+        biases(other)
+
+    write_half(1 - pos[2], other, one, two, wide, sems)
 
 
 VMEM = pl.BlockSpec(memory_space=pltpu.VMEM)
@@ -270,13 +294,14 @@
 SMEM = pl.BlockSpec(memory_space=pltpu.SMEM)
 
 
-def call(kernel, out, inputs, scratch, mib, flops, size, places=None):
+def call(kernel, out, inputs, scratch, mib, flops, size, places=None, aliases=None):
     return pl.pallas_call(
         kernel,
         out_shape=tuple(jax.ShapeDtypeStruct(*o) for o in out),
         in_specs=inputs,
         out_specs=places or (VMEM,) * len(out),
         scratch_shapes=scratch,
+        input_output_aliases=aliases or {},
         compiler_params=pltpu.CompilerParams(vmem_limit_bytes=mib * 1024 * 1024),
         cost_estimate=pl.CostEstimate(flops=flops, bytes_accessed=size, transcendentals=0),
     )
@@ -330,13 +355,31 @@
     )(pos, own, got)
 
 
-def final(pos, mine, other):
-    shape = (27, 128, 128)
-    return call(
-        final_kernel, [(shape, f32), (shape, f32), ((1, 128), f32), ((1, 128), f32)], [SMEM, VMEM, VMEM],
-        [pltpu.VMEM(shape, f32), pltpu.VMEM(shape, f32), pltpu.SemaphoreType.DMA((2, 3))],
-        56, 10**6, 10**6, (HBM, HBM, VMEM, VMEM),
-    )(pos, mine, other)
+def fold(pos, kept, got):
+    parts = [v.reshape(4, 224, 128) for v in (kept, *got)]
+    return call(
+        fold_kernel, [((224, 128), f32)] + [((224, 128), bf16)] * 3, [SMEM] + [VMEM] * 4, [], 8, 10**6, 10**6,
+    )(pos, *parts)
+
+
+GRAD = ((27, 128, 128), f32)
+
+
+def write_mine(pos, mine):
+    return call(
+        mine_kernel, [GRAD, GRAD], [SMEM, VMEM],
+        [pltpu.VMEM(*GRAD), pltpu.SemaphoreType.DMA((3,))],
+        8, 10**8, 10**6, (HBM, HBM),
+    )(pos, mine)
+
+
+def write_other(pos, mine, other, one, two):
+    bias = ((1, 128), f32)
+    return call(
+        other_kernel, [GRAD, GRAD, bias, bias], [SMEM, VMEM, VMEM, HBM, HBM],
+        [pltpu.VMEM(*GRAD), pltpu.SemaphoreType.DMA((3,))],
+        8, 10**6, 10**6, (HBM, HBM, VMEM, VMEM), {3: 0, 4: 1},
+    )(pos, mine, other, one, two)
 
 
 def body(block_input, cotangent, kernel_one, bias_one, kernel_two, scale_one, shift_one, scale_two, shift_two):
@@ -360,7 +403,7 @@
     got = shifted(send, "c", 2, 1)
     own = own_grads(pos, field, cotan, biases)
     gin = input_grad(d, xin, cot, k1, vectors)
-    grad_one, grad_two, grad_bias_one, grad_bias_two = final(pos, *total(pos, own, got))
+    grad_one, grad_two, grad_bias_one, grad_bias_two = total(pos, own, got)
     shape = (3, 3, 3, 128, 128)
     return (
         jnp.swapaxes(gin, 1, 2), grad_one.reshape(shape), grad_bias_one[0], grad_two.reshape(shape), grad_bias_two[0],

time: 108 us -> 107 us (level)
  waiting for transfers between devices: 35 us -> 29.7 us
  starting transfers between devices: 49 us -> 53.8 us
    ppermute x18, waiting for transfers between devices: 33.7 us -> 28.4 us  [shifted(): return lax.ppermute(v, AXES, shift_pairs(axis, size, k))]
    ppermute x18, starting transfers between devices: 35.5 us -> 40.4 us  [shifted(): return lax.ppermute(v, AXES, shift_pairs(axis, size, k))]
    pallas_call x1 -> x3, Pallas kernels: 3.87 us -> 4.83 us  [the longest x1 2.35 us: write_other(): call(other_kernel, [GRAD, GRAD, bias, bias], [SMEM, VMEM, VMEM, HBM, HBM]...]
  transfers between devices with their start and end apart: 22 -> 22, of which waited for: 15 -> 13; matrix products, arithmetic and copies ran while one was open for 4% -> 4% of each run, Pallas kernels for 4% -> 5%
where the time goes in v2:
time: 107 us; the launch traced here: 106 us
  starting transfers between devices  53.8 us (50%)
  waiting for transfers between devices  29.7 us (28%)
  Pallas kernels  16.4 us (15%)
  other arithmetic  2.77 us (3%)
  local copies, waits for them, and re-layouts  2.41 us (2%)
  between operations  1.33 us (1%)
    ppermute x18, starting transfers between devices, shifted(): return lax.ppermute(v, AXES, shift_pairs(axis, size, k))  40.4 us
    ppermute x18, waiting for transfers between devices, shifted(): return lax.ppermute(v, AXES, shift_pairs(axis, size, k))  28.4 us
    ppermute x4, starting transfers between devices, exchange(): return (lax.ppermute(high, axis, up), lax.ppermute(low, axis, down))  13.5 us
    pallas_call x1, Pallas kernels, local(): call(local_kernel, [((28, 128, 128), bf16), ((128, 128), f32), ((3, 384,...  6.76 us
    pallas_call x1, Pallas kernels, input_grad(): call(input_kernel, [((3, 10, 23, 128), bf16)], [VMEM] * 5, [pltpu.VMEM((4...  2.46 us
    pallas_call x1, Pallas kernels, write_other(): call(other_kernel, [GRAD, GRAD, bias, bias], [SMEM, VMEM, VMEM, HBM, HBM]...  2.35 us
    select_n x2, other arithmetic, body(): jnp.where(wa < 32, v, jnp.zeros_like(v))  2.35 us
  transfers between devices with their start and end apart: 22, of which 13 were waited for; matrix products, arithmetic and copies ran while one was open for 4% of the time, Pallas kernels for 5%

profile of v2, /device:TPU:1, one launch (start us, length us, event | category | flops | bytes accessed | tf_op | source)
XLA Modules:
  0.0 106.4 jit_solution(13824035231634094159)
XLA Ops:
  0.6 0.9 slice_bitcast_fusion.2
  1.6 5.1 %collective-permute-start.1 = (bf16[2,3,2,23,128]{4,3,2,1,0:T(8,128)(2,1)S(1)}, bf16[2,3,2,23,128]{4,3,2,1,0:T(8,128)(2,1)S(1)}, u32[]{:S(2)}, u32[]{:S(2)}) collective-permute-start(bf16[2,3,2,23,128]{4,3,2,1,0:T(8,128)(2,1)S(1)} %pad_maximum_fusion.3), channel_id=1, source_target_pairs={{1,0},{2,1},{3,2},{4,3},{5,4},{6,5},{7,6},{8,7},{9,8},{10,9},{11,1... | collective-permute-start | bytes 211976 | tf_op jit(solution)/shard_map/ppermute | solution.py:74
  6.7 3.1 %collective-permute-start = (bf16[2,3,2,23,128]{4,3,2,1,0:T(8,128)(2,1)S(1)}, bf16[2,3,2,23,128]{4,3,2,1,0:T(8,128)(2,1)S(1)}, u32[]{:S(2)}, u32[]{:S(2)}) collective-permute-start(bf16[2,3,2,23,128]{4,3,2,1,0:T(8,128)(2,1)S(1)} %pad_maximum_fusion.2), channel_id=1, source_target_pairs={{0,1},{1,2},{2,3},{3,4},{4,5},{5,6},{6,7},{7,8},{8,9},{9,10},{10,1... | collective-permute-start | bytes 211976 | tf_op jit(solution)/shard_map/ppermute | solution.py:74
  9.8 1.0 broadcast_select_fusion.2
  10.9 1.3 %broadcast_select_fusion = (bf16[3,3,3,128,128]{4,3,2,1,0:T(8,128)(2,1)S(1)}, bf16[3,3,3,128,128]{4,3,2,1,0:T(8,128)(2,1)S(1)}) fusion(bf16[3,3,3,128,128]{4,3,2,1,0:T(8,128)(2,1)S(1)} %copy-done, pred[]{:T(512)S(6)} %lt.68, bf16[3,3,3,128,128]{4,3,2,1,0:T(8,128)(2,1)} %param.11), kind=kLoop, calls=%fused_computation | loop fusion | flops 884736 | bytes 3538945 | tf_op jit(solution)/shard_map/jit(_where)/select_n | solution.py:401
  12.3 1.0 slice_bitcast_fusion.6
  13.4 0.1 stack.95.pos
  13.5 0.1 pad_maximum_fusion.5
  13.6 1.3 %collective-permute-start.3 = (bf16[2,3,14,2,128]{4,3,2,1,0:T(2,128)(2,1)S(1)}, bf16[2,3,14,2,128]{4,3,2,1,0:T(2,128)(2,1)S(1)}, u32[]{:S(2)}, u32[]{:S(2)}) collective-permute-start(bf16[2,3,14,2,128]{4,3,2,1,0:T(2,128)(2,1)S(1)} %pad_maximum_fusion.5), channel_id=1, source_target_pairs={{32,0},{64,32},{96,64},{128,96},{160,128},{192,160},{224,192},{33,... | collective-permute-start | bytes 129032 | tf_op jit(solution)/shard_map/ppermute | solution.py:74
  14.9 0.1 pad_maximum_fusion.4
  15.0 4.0 %collective-permute-start.2 = (bf16[2,3,14,2,128]{4,3,2,1,0:T(2,128)(2,1)S(1)}, bf16[2,3,14,2,128]{4,3,2,1,0:T(2,128)(2,1)S(1)}, u32[]{:S(2)}, u32[]{:S(2)}) collective-permute-start(bf16[2,3,14,2,128]{4,3,2,1,0:T(2,128)(2,1)S(1)} %pad_maximum_fusion.4), channel_id=1, source_target_pairs={{0,32},{32,64},{64,96},{96,128},{128,160},{160,192},{192,224},{1,3... | collective-permute-start | bytes 129032 | tf_op jit(solution)/shard_map/ppermute | solution.py:74
  19.0 1.3 %collective-permute-done.2 = bf16[2,3,14,2,128]{4,3,2,1,0:T(2,128)(2,1)S(1)} collective-permute-done((bf16[2,3,14,2,128]{4,3,2,1,0:T(2,128)(2,1)S(1)}, bf16[2,3,14,2,128]{4,3,2,1,0:T(2,128)(2,1)S(1)}, u32[]{:S(2)}, u32[]{:S(2)}) %collective-permute-start.2) | collective-permute-done | bytes 43040 | tf_op jit(solution)/shard_map/ppermute | solution.py:74
  20.3 0.1 pad_maximum_fusion.1.ends
  20.4 6.8 %shard_map.128 = (bf16[28,128,128]{2,1,0:T(8,128)(2,1)S(1)}, f32[128,128]{1,0:T(8,128)S(1)}, bf16[3,384,128]{2,1,0:T(8,128)(2,1)S(1)}, bf16[2,384,1024]{2,1,0:T(8,128)(2,1)S(1)}, bf16[2,1024,384]{2,1,0:T(8,128)(2,1)S(1)}) custom-call(s32[5]{0:T(128)S(1)} %stack.95.pos, bf16[3,10,23,128]{3,2,1,0:T(8,128)(2,1)S(1)} %get-tuple-element.60.xin, ...), custom_call_target="tpu_custom_call" | custom-call | flops 3000000000 | bytes 8000000 | tf_op jit(solution)/shard_map/pallas_call | solution.py:311
  27.2 0.6 collective-permute-start.4
  27.7 1.6 %shard_map.130.own = f32[28,128,128]{2,1,0:T(8,128)S(1)} custom-call(s32[5]{0:T(128)S(1)} %stack.95.pos, bf16[2,384,1024]{2,1,0:T(8,128)(2,1)S(1)} %get-tuple-element.25.field, bf16[2,1024,384]{2,1,0:T(8,128)(2,1)S(1)} %get-tuple-element.26.cotan, f32[128,128]{1,0:T(8,128)S(1)} %get-tuple-element.27.biases), custom_call_target="tpu_custom_call" | custom-call | flops 1000000000 | bytes 3000000 | tf_op jit(solution)/shard_map/pallas_call | solution.py:332
  29.3 0.5 collective-permute-done.4.got
  29.8 0.8 shard_map.131
  30.6 2.3 %collective-permute-start.5 = (bf16[7,128,128]{2,1,0:T(8,128)(2,1)S(1)}, bf16[7,128,128]{2,1,0:T(8,128)(2,1)S(1)}, u32[]{:S(2)}, u32[]{:S(2)}) collective-permute-start(bf16[7,128,128]{2,1,0:T(8,128)(2,1)S(1)} %get-tuple-element.30), channel_id=1, source_target_pairs={{0,8},{1,33},{2,10},{3,35},{4,12},{5,37},{6,14},{7,39},{8,16},{9,4... | collective-permute-start | bytes 688136 | tf_op jit(solution)/shard_map/ppermute | solution.py:35
  32.9 3.5 %collective-permute-start.6 = (bf16[7,128,128]{2,1,0:T(8,128)(2,1)S(1)}, bf16[7,128,128]{2,1,0:T(8,128)(2,1)S(1)}, u32[]{:S(2)}, u32[]{:S(2)}) collective-permute-start(bf16[7,128,128]{2,1,0:T(8,128)(2,1)S(1)} %get-tuple-element.31), channel_id=1, source_target_pairs={{0,16},{1,65},{2,18},{3,67},{4,20},{5,69},{6,22},{7,71},{8,24},{9,... | collective-permute-start | bytes 688136 | tf_op jit(solution)/shard_map/ppermute | solution.py:35
  36.4 2.2 %collective-permute-done.5 = bf16[7,128,128]{2,1,0:T(8,128)(2,1)S(1)} collective-permute-done((bf16[7,128,128]{2,1,0:T(8,128)(2,1)S(1)}, bf16[7,128,128]{2,1,0:T(8,128)(2,1)S(1)}, u32[]{:S(2)}, u32[]{:S(2)}) %collective-permute-start.5) | collective-permute-done | bytes 229408 | tf_op jit(solution)/shard_map/ppermute | solution.py:35
  38.6 3.6 %collective-permute-done.6 = bf16[7,128,128]{2,1,0:T(8,128)(2,1)S(1)} collective-permute-done((bf16[7,128,128]{2,1,0:T(8,128)(2,1)S(1)}, bf16[7,128,128]{2,1,0:T(8,128)(2,1)S(1)}, u32[]{:S(2)}, u32[]{:S(2)}) %collective-permute-start.6) | collective-permute-done | bytes 229408 | tf_op jit(solution)/shard_map/ppermute | solution.py:35
  42.3 0.7 shard_map.132
  42.9 8.1 %collective-permute-start.8 = (bf16[224,128]{1,0:T(8,128)(2,1)S(1)}, bf16[224,128]{1,0:T(8,128)(2,1)S(1)}, u32[]{:S(2)}, u32[]{:S(2)}) collective-permute-start(bf16[224,128]{1,0:T(8,128)(2,1)S(1)} %get-tuple-element.34), channel_id=1, source_target_pairs={{0,32},{1,9},{2,34},{3,11},{4,36},{5,13},{6,38},{7,15},{8,40},{9,1... | collective-permute-start | bytes 172040 | tf_op jit(solution)/shard_map/ppermute | solution.py:35
  51.0 2.7 %collective-permute-start.9 = (bf16[224,128]{1,0:T(8,128)(2,1)S(1)}, bf16[224,128]{1,0:T(8,128)(2,1)S(1)}, u32[]{:S(2)}, u32[]{:S(2)}) collective-permute-start(bf16[224,128]{1,0:T(8,128)(2,1)S(1)} %get-tuple-element.35), channel_id=1, source_target_pairs={{0,64},{1,17},{2,66},{3,19},{4,68},{5,21},{6,70},{7,23},{8,72},{9,... | collective-permute-start | bytes 172040 | tf_op jit(solution)/shard_map/ppermute | solution.py:35
  53.7 0.9 collective-permute-start.10
  54.6 1.3 %collective-permute-done.9 = bf16[224,128]{1,0:T(8,128)(2,1)S(1)} collective-permute-done((bf16[224,128]{1,0:T(8,128)(2,1)S(1)}, bf16[224,128]{1,0:T(8,128)(2,1)S(1)}, u32[]{:S(2)}, u32[]{:S(2)}) %collective-permute-start.9) | collective-permute-done | bytes 57376 | tf_op jit(solution)/shard_map/ppermute | solution.py:35
  55.9 0.9 collective-permute-done.10
  56.8 4.6 %collective-permute-start.11 = (f32[224,128]{1,0:T(8,128)S(1)}, f32[224,128]{1,0:T(8,128)S(1)}, u32[]{:S(2)}, u32[]{:S(2)}) collective-permute-start(f32[224,128]{1,0:T(8,128)S(1)} %convert_add_fusion), channel_id=1, source_target_pairs={{0,128},{1,129},{2,130},{3,131},{4,132},{5,133},{6,134},{7,135},{8... | collective-permute-start | bytes 344072 | tf_op jit(solution)/shard_map/ppermute | solution.py:35
  61.4 2.2 %collective-permute-done.11 = f32[224,128]{1,0:T(8,128)S(1)} collective-permute-done((f32[224,128]{1,0:T(8,128)S(1)}, f32[224,128]{1,0:T(8,128)S(1)}, u32[]{:S(2)}, u32[]{:S(2)}) %collective-permute-start.11) | collective-permute-done | bytes 114720 | tf_op jit(solution)/shard_map/ppermute | solution.py:35
  63.6 0.1 collective-permute-start.14
  63.7 2.4 %collective-permute-start.13 = (bf16[224,128]{1,0:T(8,128)(2,1)S(1)}, bf16[224,128]{1,0:T(8,128)(2,1)S(1)}, u32[]{:S(2)}, u32[]{:S(2)}) collective-permute-start(bf16[224,128]{1,0:T(8,128)(2,1)S(1)} %add_convert_fusion.1), channel_id=1, source_target_pairs={{0,2},{1,3},{2,4},{3,5},{4,6},{5,7},{6,0},{7,1},{8,10},{9,11},{10,... | collective-permute-start | bytes 172040 | tf_op jit(solution)/shard_map/ppermute | solution.py:35
  66.0 1.5 %collective-permute-done.14 = bf16[224,128]{1,0:T(8,128)(2,1)S(1)} collective-permute-done((bf16[224,128]{1,0:T(8,128)(2,1)S(1)}, bf16[224,128]{1,0:T(8,128)(2,1)S(1)}, u32[]{:S(2)}, u32[]{:S(2)}) %collective-permute-start.14) | collective-permute-done | bytes 57376 | tf_op jit(solution)/shard_map/ppermute | solution.py:35
  67.6 1.3 %collective-permute-done.13 = bf16[224,128]{1,0:T(8,128)(2,1)S(1)} collective-permute-done((bf16[224,128]{1,0:T(8,128)(2,1)S(1)}, bf16[224,128]{1,0:T(8,128)(2,1)S(1)}, u32[]{:S(2)}, u32[]{:S(2)}) %collective-permute-start.13) | collective-permute-done | bytes 57376 | tf_op jit(solution)/shard_map/ppermute | solution.py:35
  68.9 4.0 %collective-permute-done.12 = bf16[224,128]{1,0:T(8,128)(2,1)S(1)} collective-permute-done((bf16[224,128]{1,0:T(8,128)(2,1)S(1)}, bf16[224,128]{1,0:T(8,128)(2,1)S(1)}, u32[]{:S(2)}, u32[]{:S(2)}) %collective-permute-start.12) | collective-permute-done | bytes 57376 | tf_op jit(solution)/shard_map/ppermute | solution.py:35
  73.0 0.1 collective-permute-start.15
  73.3 2.5 %collective-permute-start.16 = (bf16[224,128]{1,0:T(8,128)(2,1)S(1)}, bf16[224,128]{1,0:T(8,128)(2,1)S(1)}, u32[]{:S(2)}, u32[]{:S(2)}) collective-permute-start(bf16[224,128]{1,0:T(8,128)(2,1)S(1)} %get-tuple-element.44), channel_id=1, source_target_pairs={{0,96},{1,25},{2,98},{3,27},{4,100},{5,29},{6,102},{7,31},{8,104},... | collective-permute-start | bytes 172040 | tf_op jit(solution)/shard_map/ppermute | solution.py:35
  75.8 0.6 collective-permute-start.17
  76.4 1.0 collective-permute-done.15
  77.4 2.9 %collective-permute-done.17 = bf16[224,128]{1,0:T(8,128)(2,1)S(1)} collective-permute-done((bf16[224,128]{1,0:T(8,128)(2,1)S(1)}, bf16[224,128]{1,0:T(8,128)(2,1)S(1)}, u32[]{:S(2)}, u32[]{:S(2)}) %collective-permute-start.17) | collective-permute-done | bytes 57376 | tf_op jit(solution)/shard_map/ppermute | solution.py:35
  80.3 0.5 collective-permute-start.20
  80.9 2.0 %collective-permute-start.19 = (bf16[4,224,128]{2,1,0:T(8,128)(2,1)S(1)}, bf16[4,224,128]{2,1,0:T(8,128)(2,1)S(1)}, u32[]{:S(2)}, u32[]{:S(2)}) collective-permute-start(bf16[4,224,128]{2,1,0:T(8,128)(2,1)S(1)} %bitcast_dynamic-update-slice_fusion.4), channel_id=1, source_target_pairs={{0,24},{1,97},{2,26},{3,99},{4,28},{5,101},{6,30},{7,103},{8,0},{9... | collective-permute-start | bytes 688136 | tf_op jit(solution)/shard_map/ppermute | solution.py:35
  82.9 0.1 broadcast_in_dim.32
  83.0 6.8 %collective-permute-done.18 = bf16[4,224,128]{2,1,0:T(8,128)(2,1)S(1)} collective-permute-done((bf16[4,224,128]{2,1,0:T(8,128)(2,1)S(1)}, bf16[4,224,128]{2,1,0:T(8,128)(2,1)S(1)}, u32[]{:S(2)}, u32[]{:S(2)}) %collective-permute-start.18) | collective-permute-done | bytes 229408 | tf_op jit(solution)/shard_map/ppermute | solution.py:35
  90.0 9.6 %collective-permute-start.21 = (bf16[28,128,128]{2,1,0:T(8,128)(2,1)S(1)}, bf16[28,128,128]{2,1,0:T(8,128)(2,1)S(1)}, u32[]{:S(2)}, u32[]{:S(2)}) collective-permute-start(bf16[28,128,128]{2,1,0:T(8,128)(2,1)S(1)} %bitcast.60), channel_id=1, source_target_pairs={{0,1},{1,0},{2,3},{3,2},{4,5},{5,4},{6,7},{7,6},{8,9},{9,8},{10,11... | collective-permute-start | bytes 2752520 | tf_op jit(solution)/shard_map/ppermute | solution.py:35
  99.6 2.5 %shard_map.129 = bf16[3,10,23,128]{3,2,1,0:T(8,128)(2,1)} custom-call(bf16[3,384,128]{2,1,0:T(8,128)(2,1)S(1)} %get-tuple-element.24.d, bf16[3,10,23,128]{3,2,1,0:T(8,128)(2,1)S(1)} %get-tuple-element.60.xin, bf16[3,10,23,128]{3,2,1,0:T(8,128)(2,1)S(1)} %get-tuple-element.59.cot, bf16[3,3,3,128,128]{4,3,2,1,0:T(8,128)(2,1)S(1)} %get-tuple-element.58.k1, ...), custom_call_target="tpu_custom_call" | custom-call | flops 1000000000 | bytes 3000000 | tf_op jit(solution)/shard_map/pallas_call | solution.py:338
  102.1 1.8 %shard_map.133 = (f32[27,128,128]{2,1,0:T(8,128)}, f32[27,128,128]{2,1,0:T(8,128)}) custom-call(s32[5]{0:T(128)S(1)} %stack.95.pos, bf16[28,128,128]{2,1,0:T(8,128)(2,1)S(1)} %bitcast.61), custom_call_target="tpu_custom_call" | custom-call | flops 100000000 | bytes 1000000 | tf_op jit(solution)/shard_map/pallas_call | solution.py:369
  103.9 2.4 %shard_map.134 = (f32[27,128,128]{2,1,0:T(8,128)}, f32[27,128,128]{2,1,0:T(8,128)}, f32[1,128]{1,0:T(1,128)}, f32[1,128]{1,0:T(1,128)}) custom-call(s32[5]{0:T(128)S(1)} %stack.95.pos, bf16[28,128,128]{2,1,0:T(8,128)(2,1)S(1)} %bitcast.62, bf16[28,128,128]{2,1,0:T(8,128)(2,1)S(1)} %collective-permute-done.21.other, ...), custom_call_target="tpu_custom_call", output_to_operand_aliasing={{0}: (3, {}), {1}: (4, {})} | custom-call | flops 1000000 | bytes 1000000 | tf_op jit(solution)/shard_map/pallas_call | solution.py:378
  (42 shorter events, 0.5 us)
Async XLA Ops:
  0.6 10.2 %copy-start = (bf16[3,3,3,128,128]{4,3,2,1,0:T(8,128)(2,1)S(1)}, bf16[3,3,3,128,128]{4,3,2,1,0:T(8,128)(2,1)}, u32[]{:S(2)}) copy-start(bf16[3,3,3,128,128]{4,3,2,1,0:T(8,128)(2,1)} %param.13) | copy-start | bytes 2654212
  1.6 11.9 %collective-permute-start.1 = (bf16[2,3,2,23,128]{4,3,2,1,0:T(8,128)(2,1)S(1)}, bf16[2,3,2,23,128]{4,3,2,1,0:T(8,128)(2,1)S(1)}, u32[]{:S(2)}, u32[]{:S(2)}) collective-permute-start(bf16[2,3,2,23,128]{4,3,2,1,0:T(8,128)(2,1)S(1)} %pad_maximum_fusion.3), channel_id=1, source_target_pairs={{1,0},{2,1},{3,2},{4,3},{5,4},{6,5},{7,6},{8,7},{9,8},{10,9},{11,1... | collective-permute-start | bytes 211976 | tf_op jit(solution)/shard_map/ppermute | solution.py:74
  6.7 6.7 %collective-permute-start = (bf16[2,3,2,23,128]{4,3,2,1,0:T(8,128)(2,1)S(1)}, bf16[2,3,2,23,128]{4,3,2,1,0:T(8,128)(2,1)S(1)}, u32[]{:S(2)}, u32[]{:S(2)}) collective-permute-start(bf16[2,3,2,23,128]{4,3,2,1,0:T(8,128)(2,1)S(1)} %pad_maximum_fusion.2), channel_id=1, source_target_pairs={{0,1},{1,2},{2,3},{3,4},{4,5},{5,6},{6,7},{7,8},{8,9},{9,10},{10,1... | collective-permute-start | bytes 211976 | tf_op jit(solution)/shard_map/ppermute | solution.py:74
  10.9 2.4 %copy-start.1 = (f32[128]{0:T(128)S(1)}, f32[128]{0:T(128)}, u32[]{:S(2)}) copy-start(f32[128]{0:T(128)} %param.12) | copy-start | bytes 1540
  10.9 2.4 %copy-start.2 = (f32[128]{0:T(128)S(1)}, f32[128]{0:T(128)}, u32[]{:S(2)}) copy-start(f32[128]{0:T(128)} %param.14) | copy-start | bytes 1540
  10.9 2.4 %copy-start.3 = (f32[128]{0:T(128)S(1)}, f32[128]{0:T(128)}, u32[]{:S(2)}) copy-start(f32[128]{0:T(128)} %param.15) | copy-start | bytes 1540
  10.9 2.4 %copy-start.4 = (f32[128]{0:T(128)S(1)}, f32[128]{0:T(128)}, u32[]{:S(2)}) copy-start(f32[128]{0:T(128)} %param.16) | copy-start | bytes 1540
  10.9 2.4 %copy-start.5 = (f32[128]{0:T(128)S(1)}, f32[128]{0:T(128)}, u32[]{:S(2)}) copy-start(f32[128]{0:T(128)} %param.17) | copy-start | bytes 1540
  13.6 5.4 %collective-permute-start.3 = (bf16[2,3,14,2,128]{4,3,2,1,0:T(2,128)(2,1)S(1)}, bf16[2,3,14,2,128]{4,3,2,1,0:T(2,128)(2,1)S(1)}, u32[]{:S(2)}, u32[]{:S(2)}) collective-permute-start(bf16[2,3,14,2,128]{4,3,2,1,0:T(2,128)(2,1)S(1)} %pad_maximum_fusion.5), channel_id=1, source_target_pairs={{32,0},{64,32},{96,64},{128,96},{160,128},{192,160},{224,192},{33,... | collective-permute-start | bytes 129032 | tf_op jit(solution)/shard_map/ppermute | solution.py:74
  15.0 5.3 %collective-permute-start.2 = (bf16[2,3,14,2,128]{4,3,2,1,0:T(2,128)(2,1)S(1)}, bf16[2,3,14,2,128]{4,3,2,1,0:T(2,128)(2,1)S(1)}, u32[]{:S(2)}, u32[]{:S(2)}) collective-permute-start(bf16[2,3,14,2,128]{4,3,2,1,0:T(2,128)(2,1)S(1)} %pad_maximum_fusion.4), channel_id=1, source_target_pairs={{0,32},{32,64},{64,96},{96,128},{128,160},{160,192},{192,224},{1,3... | collective-permute-start | bytes 129032 | tf_op jit(solution)/shard_map/ppermute | solution.py:74
  27.2 2.6 %collective-permute-start.4 = (bf16[28,128,128]{2,1,0:T(8,128)(2,1)S(1)}, bf16[28,128,128]{2,1,0:T(8,128)(2,1)S(1)}, u32[]{:S(2)}, u32[]{:S(2)}) collective-permute-start(bf16[28,128,128]{2,1,0:T(8,128)(2,1)S(1)} %get-tuple-element.28), channel_id=1, source_target_pairs={{0,1},{1,0},{2,3},{3,2},{4,5},{5,4},{6,7},{7,6},{8,9},{9,8},{10,11... | collective-permute-start | bytes 2752520 | tf_op jit(solution)/shard_map/ppermute | solution.py:35
  30.6 8.0 %collective-permute-start.5 = (bf16[7,128,128]{2,1,0:T(8,128)(2,1)S(1)}, bf16[7,128,128]{2,1,0:T(8,128)(2,1)S(1)}, u32[]{:S(2)}, u32[]{:S(2)}) collective-permute-start(bf16[7,128,128]{2,1,0:T(8,128)(2,1)S(1)} %get-tuple-element.30), channel_id=1, source_target_pairs={{0,8},{1,33},{2,10},{3,35},{4,12},{5,37},{6,14},{7,39},{8,16},{9,4... | collective-permute-start | bytes 688136 | tf_op jit(solution)/shard_map/ppermute | solution.py:35
  32.9 9.4 %collective-permute-start.6 = (bf16[7,128,128]{2,1,0:T(8,128)(2,1)S(1)}, bf16[7,128,128]{2,1,0:T(8,128)(2,1)S(1)}, u32[]{:S(2)}, u32[]{:S(2)}) collective-permute-start(bf16[7,128,128]{2,1,0:T(8,128)(2,1)S(1)} %get-tuple-element.31), channel_id=1, source_target_pairs={{0,16},{1,65},{2,18},{3,67},{4,20},{5,69},{6,22},{7,71},{8,24},{9,... | collective-permute-start | bytes 688136 | tf_op jit(solution)/shard_map/ppermute | solution.py:35
  36.4 5.9 %collective-permute-start.7 = (bf16[7,128,128]{2,1,0:T(8,128)(2,1)S(1)}, bf16[7,128,128]{2,1,0:T(8,128)(2,1)S(1)}, u32[]{:S(2)}, u32[]{:S(2)}) collective-permute-start(bf16[7,128,128]{2,1,0:T(8,128)(2,1)S(1)} %get-tuple-element.32), channel_id=1, source_target_pairs={{0,24},{1,97},{2,26},{3,99},{4,28},{5,101},{6,30},{7,103},{8,0},{9... | collective-permute-start | bytes 688136 | tf_op jit(solution)/shard_map/ppermute | solution.py:35
  42.9 11.7 %collective-permute-start.8 = (bf16[224,128]{1,0:T(8,128)(2,1)S(1)}, bf16[224,128]{1,0:T(8,128)(2,1)S(1)}, u32[]{:S(2)}, u32[]{:S(2)}) collective-permute-start(bf16[224,128]{1,0:T(8,128)(2,1)S(1)} %get-tuple-element.34), channel_id=1, source_target_pairs={{0,32},{1,9},{2,34},{3,11},{4,36},{5,13},{6,38},{7,15},{8,40},{9,1... | collective-permute-start | bytes 172040 | tf_op jit(solution)/shard_map/ppermute | solution.py:35
  51.0 4.9 %collective-permute-start.9 = (bf16[224,128]{1,0:T(8,128)(2,1)S(1)}, bf16[224,128]{1,0:T(8,128)(2,1)S(1)}, u32[]{:S(2)}, u32[]{:S(2)}) collective-permute-start(bf16[224,128]{1,0:T(8,128)(2,1)S(1)} %get-tuple-element.35), channel_id=1, source_target_pairs={{0,64},{1,17},{2,66},{3,19},{4,68},{5,21},{6,70},{7,23},{8,72},{9,... | collective-permute-start | bytes 172040 | tf_op jit(solution)/shard_map/ppermute | solution.py:35
  53.7 3.0 %collective-permute-start.10 = (bf16[224,128]{1,0:T(8,128)(2,1)S(1)}, bf16[224,128]{1,0:T(8,128)(2,1)S(1)}, u32[]{:S(2)}, u32[]{:S(2)}) collective-permute-start(bf16[224,128]{1,0:T(8,128)(2,1)S(1)} %get-tuple-element.36), channel_id=1, source_target_pairs={{0,96},{1,25},{2,98},{3,27},{4,100},{5,29},{6,102},{7,31},{8,104},... | collective-permute-start | bytes 172040 | tf_op jit(solution)/shard_map/ppermute | solution.py:35
  56.8 6.7 %collective-permute-start.11 = (f32[224,128]{1,0:T(8,128)S(1)}, f32[224,128]{1,0:T(8,128)S(1)}, u32[]{:S(2)}, u32[]{:S(2)}) collective-permute-start(f32[224,128]{1,0:T(8,128)S(1)} %convert_add_fusion), channel_id=1, source_target_pairs={{0,128},{1,129},{2,130},{3,131},{4,132},{5,133},{6,134},{7,135},{8... | collective-permute-start | bytes 344072 | tf_op jit(solution)/shard_map/ppermute | solution.py:35
  63.6 4.0 %collective-permute-start.14 = (bf16[224,128]{1,0:T(8,128)(2,1)S(1)}, bf16[224,128]{1,0:T(8,128)(2,1)S(1)}, u32[]{:S(2)}, u32[]{:S(2)}) collective-permute-start(bf16[224,128]{1,0:T(8,128)(2,1)S(1)} %add_convert_fusion.1), channel_id=1, source_target_pairs={{0,6},{1,7},{2,0},{3,1},{4,2},{5,3},{6,4},{7,5},{8,14},{9,15},{10,... | collective-permute-start | bytes 172040 | tf_op jit(solution)/shard_map/ppermute | solution.py:35
  63.7 5.2 %collective-permute-start.13 = (bf16[224,128]{1,0:T(8,128)(2,1)S(1)}, bf16[224,128]{1,0:T(8,128)(2,1)S(1)}, u32[]{:S(2)}, u32[]{:S(2)}) collective-permute-start(bf16[224,128]{1,0:T(8,128)(2,1)S(1)} %add_convert_fusion.1), channel_id=1, source_target_pairs={{0,2},{1,3},{2,4},{3,5},{4,6},{5,7},{6,0},{7,1},{8,10},{9,11},{10,... | collective-permute-start | bytes 172040 | tf_op jit(solution)/shard_map/ppermute | solution.py:35
  66.0 6.9 %collective-permute-start.12 = (bf16[224,128]{1,0:T(8,128)(2,1)S(1)}, bf16[224,128]{1,0:T(8,128)(2,1)S(1)}, u32[]{:S(2)}, u32[]{:S(2)}) collective-permute-start(bf16[224,128]{1,0:T(8,128)(2,1)S(1)} %add_convert_fusion.1), channel_id=1, source_target_pairs={{0,4},{1,5},{2,6},{3,7},{4,0},{5,1},{6,2},{7,3},{8,12},{9,13},{10,... | collective-permute-start | bytes 172040 | tf_op jit(solution)/shard_map/ppermute | solution.py:35
  73.0 4.3 %collective-permute-start.15 = (bf16[224,128]{1,0:T(8,128)(2,1)S(1)}, bf16[224,128]{1,0:T(8,128)(2,1)S(1)}, u32[]{:S(2)}, u32[]{:S(2)}) collective-permute-start(bf16[224,128]{1,0:T(8,128)(2,1)S(1)} %get-tuple-element.44), channel_id=1, source_target_pairs={{0,32},{1,9},{2,34},{3,11},{4,36},{5,13},{6,38},{7,15},{8,40},{9,1... | collective-permute-start | bytes 172040 | tf_op jit(solution)/shard_map/ppermute | solution.py:35
  73.3 4.1 %collective-permute-start.16 = (bf16[224,128]{1,0:T(8,128)(2,1)S(1)}, bf16[224,128]{1,0:T(8,128)(2,1)S(1)}, u32[]{:S(2)}, u32[]{:S(2)}) collective-permute-start(bf16[224,128]{1,0:T(8,128)(2,1)S(1)} %get-tuple-element.44), channel_id=1, source_target_pairs={{0,96},{1,25},{2,98},{3,27},{4,100},{5,29},{6,102},{7,31},{8,104},... | collective-permute-start | bytes 172040 | tf_op jit(solution)/shard_map/ppermute | solution.py:35
  75.8 4.5 %collective-permute-start.17 = (bf16[224,128]{1,0:T(8,128)(2,1)S(1)}, bf16[224,128]{1,0:T(8,128)(2,1)S(1)}, u32[]{:S(2)}, u32[]{:S(2)}) collective-permute-start(bf16[224,128]{1,0:T(8,128)(2,1)S(1)} %get-tuple-element.44), channel_id=1, source_target_pairs={{0,64},{1,17},{2,66},{3,19},{4,68},{5,21},{6,70},{7,23},{8,72},{9,... | collective-permute-start | bytes 172040 | tf_op jit(solution)/shard_map/ppermute | solution.py:35
  80.3 9.6 %collective-permute-start.20 = (bf16[4,224,128]{2,1,0:T(8,128)(2,1)S(1)}, bf16[4,224,128]{2,1,0:T(8,128)(2,1)S(1)}, u32[]{:S(2)}, u32[]{:S(2)}) collective-permute-start(bf16[4,224,128]{2,1,0:T(8,128)(2,1)S(1)} %bitcast_dynamic-update-slice_fusion.4), channel_id=1, source_target_pairs={{0,16},{1,65},{2,18},{3,67},{4,20},{5,69},{6,22},{7,71},{8,24},{9,... | collective-permute-start | bytes 688136 | tf_op jit(solution)/shard_map/ppermute | solution.py:35
  80.9 9.0 %collective-permute-start.19 = (bf16[4,224,128]{2,1,0:T(8,128)(2,1)S(1)}, bf16[4,224,128]{2,1,0:T(8,128)(2,1)S(1)}, u32[]{:S(2)}, u32[]{:S(2)}) collective-permute-start(bf16[4,224,128]{2,1,0:T(8,128)(2,1)S(1)} %bitcast_dynamic-update-slice_fusion.4), channel_id=1, source_target_pairs={{0,24},{1,97},{2,26},{3,99},{4,28},{5,101},{6,30},{7,103},{8,0},{9... | collective-permute-start | bytes 688136 | tf_op jit(solution)/shard_map/ppermute | solution.py:35
  82.9 7.0 %collective-permute-start.18 = (bf16[4,224,128]{2,1,0:T(8,128)(2,1)S(1)}, bf16[4,224,128]{2,1,0:T(8,128)(2,1)S(1)}, u32[]{:S(2)}, u32[]{:S(2)}) collective-permute-start(bf16[4,224,128]{2,1,0:T(8,128)(2,1)S(1)} %bitcast_dynamic-update-slice_fusion.4), channel_id=1, source_target_pairs={{0,8},{1,33},{2,10},{3,35},{4,12},{5,37},{6,14},{7,39},{8,16},{9,4... | collective-permute-start | bytes 688136 | tf_op jit(solution)/shard_map/ppermute | solution.py:35
  90.0 13.9 %collective-permute-start.21 = (bf16[28,128,128]{2,1,0:T(8,128)(2,1)S(1)}, bf16[28,128,128]{2,1,0:T(8,128)(2,1)S(1)}, u32[]{:S(2)}, u32[]{:S(2)}) collective-permute-start(bf16[28,128,128]{2,1,0:T(8,128)(2,1)S(1)} %bitcast.60), channel_id=1, source_target_pairs={{0,1},{1,0},{2,3},{3,2},{4,5},{5,4},{6,7},{7,6},{8,9},{9,8},{10,11... | collective-permute-start | bytes 2752520 | tf_op jit(solution)/shard_map/ppermute | solution.py:35

commit v3 on v2

--- a/solution.py
+++ b/solution.py
@@ -25,44 +25,64 @@
     pairs = []
     for d in range(256):
         p = coords(d)
-        a = axis if isinstance(axis, str) else axis[p["c"]]
-        p[a] = (p[a] + k) % size
+        p[axis] = (p[axis] + k) % size
         pairs.append((d, device_of(p)))
     return pairs
 
 
+def place(v, flip):
+    return (v >> 1) ^ (v & 1) if flip == 1 else v >> 1
+
+
+def position(x, y, flip):
+    return place(x, flip) + 2 * place(y, flip)
+
+
+def flip_pairs(flips, m):
+    pairs = []
+    for d in range(256):
+        p = coords(d)
+        p["x"] ^= flips[p["c"]] * (m & 1)
+        p["y"] ^= flips[p["c"]] * (m >> 1)
+        pairs.append((d, device_of(p)))
+    return pairs
+
+
+def send_pairs(v, pairs):
+    return lax.ppermute(v, AXES, pairs)
+
+
 def shifted(v, axis, size, k):
-    return lax.ppermute(v, AXES, shift_pairs(axis, size, k))
-
-
-ORDER = (2, 1, 3)
-
-
-def scatter(send, axis):
-    got = {k: shifted(send[k - 1], axis, 4, k) for k in ORDER}
-    return got[1], got[2], got[3]
-
-
-def gather(v, axis, here):
-    got = {k: shifted(v, axis, 4, k) for k in ORDER}
+    return send_pairs(v, shift_pairs(axis, size, k))
+
+
+def exchange_squares(sends, flips):
+    return [send_pairs(sends[m - 1], flip_pairs(flips, m)) for m in (1, 2, 3)]
+
+
+def gather(v, flips, here):
+    got = exchange_squares([v] * 3, flips)
     out = lax.dynamic_update_index_in_dim(jnp.zeros((4,) + v.shape, v.dtype), v, here, 0)
-    for k in (1, 3, 2):
-        out = lax.dynamic_update_index_in_dim(out, got[k], (here - k) % 4, 0)
+    for m in (2, 1, 3):
+        out = lax.dynamic_update_index_in_dim(out, got[m - 1], here ^ m, 0)
     return out
+
+
+FIRST, SECOND = (1, 3), (3, 1)
 
 
 def total(pos, own, got):
     first, second = pos[3], pos[4]
     kept, *sends = combine(pos, own, got)
-    kept, *sends = fold(pos, kept, scatter(sends, ("x", "y")))
-    got = scatter(sends, ("y", "x"))
+    kept, *sends = fold(pos, kept, exchange_squares(sends, FIRST))
+    got = exchange_squares(sends, SECOND)
     v = kept + got[0].astype(f32) + got[1].astype(f32) + got[2].astype(f32)
     v = v + shifted(v, "zl", 2, 1)
     v = v.astype(bf16)
-    got = {k: shifted(v, "zh", 4, k) for k in ORDER}
+    got = {k: shifted(v, "zh", 4, k) for k in (1, 2, 3)}
     v = ((v.astype(f32) + got[2].astype(f32)) + (got[1].astype(f32) + got[3].astype(f32))).astype(bf16)
-    v = gather(v, ("y", "x"), second)
-    v = gather(v, ("x", "y"), first).reshape(28, 128, 128)
+    v = gather(v, SECOND, second)
+    v = gather(v, FIRST, first).reshape(28, 128, 128)
     other = shifted(v, "c", 2, 1)
     one, two = write_mine(pos, v)
     return write_other(pos, v, other, one, two)
@@ -231,7 +251,7 @@
 def combine_kernel(pos, own, got, kept, to1, to2, to3):
     def one(j, carry):
         for k, out in enumerate((kept, to1, to2, to3)):
-            b = lax.rem(pos[3] + k, 4) * 7 + j
+            b = jnp.bitwise_xor(pos[3], k) * 7 + j
             out[j] = (own[b] + got[b].astype(f32)).astype(out.dtype)
         return carry
 
@@ -240,7 +260,7 @@
 
 def fold_kernel(pos, own, got1, got2, got3, kept, to1, to2, to3):
     for k, out in enumerate((kept, to1, to2, to3)):
-        at = lax.rem(pos[4] + k, 4)
+        at = jnp.bitwise_xor(pos[4], k)
         value = own[at] + got1[at].astype(f32) + got2[at].astype(f32) + got3[at].astype(f32)
         out[...] = value.astype(out.dtype)
 
@@ -273,10 +293,9 @@
     write_half(pos[2], mine, one, two, wide, sems)
 
 
-def other_kernel(pos, mine, other, one_in, two_in, one, two, bias_one, bias_two, wide, sems):
+def other_kernel(pos, mine, other, one_in, two_in, one, two, bias_one, bias_two, wide, sems, rows_out, row_sems):
     def biases(src):
-        bias_one[...] = src[27, 0:1, :].astype(f32) * FACTOR
-        bias_two[...] = src[27, 8:9, :].astype(f32) * FACTOR
+        rows_out[...] = src[27, 0:16, :].astype(f32) * FACTOR
 
     @pl.when(pos[2] == 0)
     def _():
@@ -286,7 +305,15 @@
     def _():
         biases(other)
 
+    copies = [
+        pltpu.make_async_copy(rows_out.at[pl.ds(8 * i, 1)], out, row_sems.at[i])
+        for i, out in enumerate((bias_one, bias_two))
+    ]
+    for copy in copies:
+        copy.start()
     write_half(1 - pos[2], other, one, two, wide, sems)
+    for copy in copies:
+        copy.wait()
 
 
 VMEM = pl.BlockSpec(memory_space=pltpu.VMEM)
@@ -377,8 +404,11 @@
     bias = ((1, 128), f32)
     return call(
         other_kernel, [GRAD, GRAD, bias, bias], [SMEM, VMEM, VMEM, HBM, HBM],
-        [pltpu.VMEM(*GRAD), pltpu.SemaphoreType.DMA((3,))],
-        8, 10**6, 10**6, (HBM, HBM, VMEM, VMEM), {3: 0, 4: 1},
+        [
+            pltpu.VMEM(*GRAD), pltpu.SemaphoreType.DMA((3,)),
+            pltpu.VMEM((16, 128), f32), pltpu.SemaphoreType.DMA((2,)),
+        ],
+        8, 10**6, 10**6, (HBM,) * 4, {3: 0, 4: 1},
     )(pos, mine, other, one, two)
 
 
@@ -395,7 +425,8 @@
     above, below = exchange(edge(slice(0, 2)), edge(slice(21, 23)), "ha", 8)
     ha, wa = lax.axis_index("ha"), lax.axis_index("wa")
     y, x, c = ha % 4, wa // 8, wa % 2
-    first, second = jnp.where(c == 0, x, y), jnp.where(c == 0, y, x)
+    one, three = position(x, y, 1), position(x, y, 3)
+    first, second = jnp.where(c == 0, one, three), jnp.where(c == 0, three, one)
     pos = jnp.stack([ha * 23 - 2, wa * 10 - 2, c, first, second]).astype(jnp.int32)
     vectors = jnp.pad(jnp.stack([bias_one, scale_one, shift_one, scale_two, shift_two]), ((0, 3), (0, 0)))
     xin, cot, k1, k2 = (jnp.where(wa < 32, v, jnp.zeros_like(v)) for v in (xin, cot, kernel_one, kernel_two))

time: 107 us -> 109 us (1.019)
  waiting for transfers between devices: 29.7 us -> 31.2 us
    ppermute x18, waiting for transfers between devices: 28.4 us -> 29.9 us  [send_pairs(): return lax.ppermute(v, AXES, pairs)]
  transfers between devices with their start and end apart: 22 -> 22, of which waited for: 13 -> 14; matrix products, arithmetic and copies ran while one was open for 4% -> 4% of each run, Pallas kernels for 5% -> 5%
where the time goes in v3:
time: 109 us; the launch traced here: 108 us
  starting transfers between devices  54.8 us (50%)
  waiting for transfers between devices  31.2 us (29%)
  Pallas kernels  15.9 us (15%)
  other arithmetic  2.77 us (3%)
  local copies, waits for them, and re-layouts  2.4 us (2%)
  between operations  1.2 us (1%)
    ppermute x18, starting transfers between devices, send_pairs(): return lax.ppermute(v, AXES, pairs)  41.3 us
    ppermute x18, waiting for transfers between devices, send_pairs(): return lax.ppermute(v, AXES, pairs)  29.9 us
    ppermute x4, starting transfers between devices, exchange(): return (lax.ppermute(high, axis, up), lax.ppermute(low, axis, down))  13.5 us
    pallas_call x1, Pallas kernels, local(): call(local_kernel, [((28, 128, 128), bf16), ((128, 128), f32), ((3, 384,...  6.75 us
    pallas_call x1, Pallas kernels, input_grad(): call(input_kernel, [((3, 10, 23, 128), bf16)], [VMEM] * 5, [pltpu.VMEM((4...  2.47 us
    select_n x2, other arithmetic, body(): jnp.where(wa < 32, v, jnp.zeros_like(v))  2.35 us
  transfers between devices with their start and end apart: 22, of which 14 were waited for; matrix products, arithmetic and copies ran while one was open for 4% of the time, Pallas kernels for 5%

profile of v3, /device:TPU:1, one launch (start us, length us, event | category | flops | bytes accessed | tf_op | source)
XLA Modules:
  0.0 108.2 jit_solution(13736393066313119229)
XLA Ops:
  0.6 0.9 slice_bitcast_fusion.2
  1.6 5.1 %collective-permute-start.1 = (bf16[2,3,2,23,128]{4,3,2,1,0:T(8,128)(2,1)S(1)}, bf16[2,3,2,23,128]{4,3,2,1,0:T(8,128)(2,1)S(1)}, u32[]{:S(2)}, u32[]{:S(2)}) collective-permute-start(bf16[2,3,2,23,128]{4,3,2,1,0:T(8,128)(2,1)S(1)} %pad_maximum_fusion.3), channel_id=1, source_target_pairs={{1,0},{2,1},{3,2},{4,3},{5,4},{6,5},{7,6},{8,7},{9,8},{10,9},{11,1... | collective-permute-start | bytes 211976 | tf_op jit(solution)/shard_map/ppermute | solution.py:94
  6.7 3.1 %collective-permute-start = (bf16[2,3,2,23,128]{4,3,2,1,0:T(8,128)(2,1)S(1)}, bf16[2,3,2,23,128]{4,3,2,1,0:T(8,128)(2,1)S(1)}, u32[]{:S(2)}, u32[]{:S(2)}) collective-permute-start(bf16[2,3,2,23,128]{4,3,2,1,0:T(8,128)(2,1)S(1)} %pad_maximum_fusion.2), channel_id=1, source_target_pairs={{0,1},{1,2},{2,3},{3,4},{4,5},{5,6},{6,7},{7,8},{8,9},{9,10},{10,1... | collective-permute-start | bytes 211976 | tf_op jit(solution)/shard_map/ppermute | solution.py:94
  9.8 1.0 broadcast_select_fusion.2
  10.9 1.3 %broadcast_select_fusion = (bf16[3,3,3,128,128]{4,3,2,1,0:T(8,128)(2,1)S(1)}, bf16[3,3,3,128,128]{4,3,2,1,0:T(8,128)(2,1)S(1)}) fusion(bf16[3,3,3,128,128]{4,3,2,1,0:T(8,128)(2,1)S(1)} %copy-done, pred[]{:T(512)S(6)} %lt.44, bf16[3,3,3,128,128]{4,3,2,1,0:T(8,128)(2,1)} %param.11), kind=kLoop, calls=%fused_computation | loop fusion | flops 884736 | bytes 3538945 | tf_op jit(solution)/shard_map/jit(_where)/select_n | solution.py:432
  12.3 1.0 slice_bitcast_fusion.6
  13.4 0.1 stack.95.pos
  13.6 1.3 %collective-permute-start.3 = (bf16[2,3,14,2,128]{4,3,2,1,0:T(2,128)(2,1)S(1)}, bf16[2,3,14,2,128]{4,3,2,1,0:T(2,128)(2,1)S(1)}, u32[]{:S(2)}, u32[]{:S(2)}) collective-permute-start(bf16[2,3,14,2,128]{4,3,2,1,0:T(2,128)(2,1)S(1)} %pad_maximum_fusion.5), channel_id=1, source_target_pairs={{32,0},{64,32},{96,64},{128,96},{160,128},{192,160},{224,192},{33,... | collective-permute-start | bytes 129032 | tf_op jit(solution)/shard_map/ppermute | solution.py:94
  15.0 4.0 %collective-permute-start.2 = (bf16[2,3,14,2,128]{4,3,2,1,0:T(2,128)(2,1)S(1)}, bf16[2,3,14,2,128]{4,3,2,1,0:T(2,128)(2,1)S(1)}, u32[]{:S(2)}, u32[]{:S(2)}) collective-permute-start(bf16[2,3,14,2,128]{4,3,2,1,0:T(2,128)(2,1)S(1)} %pad_maximum_fusion.4), channel_id=1, source_target_pairs={{0,32},{32,64},{64,96},{96,128},{128,160},{160,192},{192,224},{1,3... | collective-permute-start | bytes 129032 | tf_op jit(solution)/shard_map/ppermute | solution.py:94
  19.0 1.3 %collective-permute-done.2 = bf16[2,3,14,2,128]{4,3,2,1,0:T(2,128)(2,1)S(1)} collective-permute-done((bf16[2,3,14,2,128]{4,3,2,1,0:T(2,128)(2,1)S(1)}, bf16[2,3,14,2,128]{4,3,2,1,0:T(2,128)(2,1)S(1)}, u32[]{:S(2)}, u32[]{:S(2)}) %collective-permute-start.2) | collective-permute-done | bytes 43040 | tf_op jit(solution)/shard_map/ppermute | solution.py:94
  20.3 0.1 pad_maximum_fusion.1.ends
  20.4 6.7 %shard_map.128 = (bf16[28,128,128]{2,1,0:T(8,128)(2,1)S(1)}, f32[128,128]{1,0:T(8,128)S(1)}, bf16[3,384,128]{2,1,0:T(8,128)(2,1)S(1)}, bf16[2,384,1024]{2,1,0:T(8,128)(2,1)S(1)}, bf16[2,1024,384]{2,1,0:T(8,128)(2,1)S(1)}) custom-call(s32[5]{0:T(128)S(1)} %stack.95.pos, bf16[3,10,23,128]{3,2,1,0:T(8,128)(2,1)S(1)} %get-tuple-element.60.xin, ...), custom_call_target="tpu_custom_call" | custom-call | flops 3000000000 | bytes 8000000 | tf_op jit(solution)/shard_map/pallas_call | solution.py:338
  27.2 0.5 collective-permute-start.4
  27.7 1.6 %shard_map.130.own = f32[28,128,128]{2,1,0:T(8,128)S(1)} custom-call(s32[5]{0:T(128)S(1)} %stack.95.pos, bf16[2,384,1024]{2,1,0:T(8,128)(2,1)S(1)} %get-tuple-element.25.field, bf16[2,1024,384]{2,1,0:T(8,128)(2,1)S(1)} %get-tuple-element.26.cotan, f32[128,128]{1,0:T(8,128)S(1)} %get-tuple-element.27.biases), custom_call_target="tpu_custom_call" | custom-call | flops 1000000000 | bytes 3000000 | tf_op jit(solution)/shard_map/pallas_call | solution.py:359
  29.3 0.5 collective-permute-done.4.got
  29.8 0.8 shard_map.131
  30.6 9.3 %collective-permute-start.5 = (bf16[7,128,128]{2,1,0:T(8,128)(2,1)S(1)}, bf16[7,128,128]{2,1,0:T(8,128)(2,1)S(1)}, u32[]{:S(2)}, u32[]{:S(2)}) collective-permute-start(bf16[7,128,128]{2,1,0:T(8,128)(2,1)S(1)} %get-tuple-element.30), channel_id=1, source_target_pairs={{0,8},{1,25},{2,10},{3,27},{4,12},{5,29},{6,14},{7,31},{8,0},{9,17... | collective-permute-start | bytes 688136 | tf_op jit(solution)/shard_map/ppermute | solution.py:52
  39.9 4.8 %collective-permute-start.6 = (bf16[7,128,128]{2,1,0:T(8,128)(2,1)S(1)}, bf16[7,128,128]{2,1,0:T(8,128)(2,1)S(1)}, u32[]{:S(2)}, u32[]{:S(2)}) collective-permute-start(bf16[7,128,128]{2,1,0:T(8,128)(2,1)S(1)} %get-tuple-element.31), channel_id=1, source_target_pairs={{0,32},{1,97},{2,34},{3,99},{4,36},{5,101},{6,38},{7,103},{8,40},{... | collective-permute-start | bytes 688136 | tf_op jit(solution)/shard_map/ppermute | solution.py:52
  44.8 5.4 %collective-permute-done.6 = bf16[7,128,128]{2,1,0:T(8,128)(2,1)S(1)} collective-permute-done((bf16[7,128,128]{2,1,0:T(8,128)(2,1)S(1)}, bf16[7,128,128]{2,1,0:T(8,128)(2,1)S(1)}, u32[]{:S(2)}, u32[]{:S(2)}) %collective-permute-start.6) | collective-permute-done | bytes 229408 | tf_op jit(solution)/shard_map/ppermute | solution.py:52
  50.2 2.8 %collective-permute-done.7 = bf16[7,128,128]{2,1,0:T(8,128)(2,1)S(1)} collective-permute-done((bf16[7,128,128]{2,1,0:T(8,128)(2,1)S(1)}, bf16[7,128,128]{2,1,0:T(8,128)(2,1)S(1)}, u32[]{:S(2)}, u32[]{:S(2)}) %collective-permute-start.7) | collective-permute-done | bytes 229408 | tf_op jit(solution)/shard_map/ppermute | solution.py:52
  52.9 0.6 shard_map.132
  53.6 0.1 collective-permute-start.8
  53.7 0.1 collective-permute-start.9
  53.8 2.5 %collective-permute-start.10 = (bf16[224,128]{1,0:T(8,128)(2,1)S(1)}, bf16[224,128]{1,0:T(8,128)(2,1)S(1)}, u32[]{:S(2)}, u32[]{:S(2)}) collective-permute-start(bf16[224,128]{1,0:T(8,128)(2,1)S(1)} %get-tuple-element.36), channel_id=1, source_target_pairs={{0,120},{1,41},{2,122},{3,43},{4,124},{5,45},{6,126},{7,47},{8,112... | collective-permute-start | bytes 172040 | tf_op jit(solution)/shard_map/ppermute | solution.py:52
  56.3 0.7 collective-permute-done.8
  57.0 0.1 collective-permute-done.9
  57.1 0.8 collective-permute-done.10
  57.9 2.2 %collective-permute-start.11 = (f32[224,128]{1,0:T(8,128)S(1)}, f32[224,128]{1,0:T(8,128)S(1)}, u32[]{:S(2)}, u32[]{:S(2)}) collective-permute-start(f32[224,128]{1,0:T(8,128)S(1)} %convert_add_fusion), channel_id=1, source_target_pairs={{0,128},{1,129},{2,130},{3,131},{4,132},{5,133},{6,134},{7,135},{8... | collective-permute-start | bytes 344072 | tf_op jit(solution)/shard_map/ppermute | solution.py:52
  60.1 2.4 %collective-permute-done.11 = f32[224,128]{1,0:T(8,128)S(1)} collective-permute-done((f32[224,128]{1,0:T(8,128)S(1)}, f32[224,128]{1,0:T(8,128)S(1)}, u32[]{:S(2)}, u32[]{:S(2)}) %collective-permute-start.11) | collective-permute-done | bytes 114720 | tf_op jit(solution)/shard_map/ppermute | solution.py:52
  62.7 2.4 %collective-permute-start.13 = (bf16[224,128]{1,0:T(8,128)(2,1)S(1)}, bf16[224,128]{1,0:T(8,128)(2,1)S(1)}, u32[]{:S(2)}, u32[]{:S(2)}) collective-permute-start(bf16[224,128]{1,0:T(8,128)(2,1)S(1)} %add_convert_fusion.1), channel_id=1, source_target_pairs={{0,2},{1,3},{2,4},{3,5},{4,6},{5,7},{6,0},{7,1},{8,10},{9,11},{10,... | collective-permute-start | bytes 172040 | tf_op jit(solution)/shard_map/ppermute | solution.py:52
  65.0 0.2 collective-permute-start.12
  65.2 1.5 %collective-permute-done.14 = bf16[224,128]{1,0:T(8,128)(2,1)S(1)} collective-permute-done((bf16[224,128]{1,0:T(8,128)(2,1)S(1)}, bf16[224,128]{1,0:T(8,128)(2,1)S(1)}, u32[]{:S(2)}, u32[]{:S(2)}) %collective-permute-start.14) | collective-permute-done | bytes 57376 | tf_op jit(solution)/shard_map/ppermute | solution.py:52
  66.7 1.7 %collective-permute-done.13 = bf16[224,128]{1,0:T(8,128)(2,1)S(1)} collective-permute-done((bf16[224,128]{1,0:T(8,128)(2,1)S(1)}, bf16[224,128]{1,0:T(8,128)(2,1)S(1)}, u32[]{:S(2)}, u32[]{:S(2)}) %collective-permute-start.13) | collective-permute-done | bytes 57376 | tf_op jit(solution)/shard_map/ppermute | solution.py:52
  68.4 3.5 %collective-permute-done.12 = bf16[224,128]{1,0:T(8,128)(2,1)S(1)} collective-permute-done((bf16[224,128]{1,0:T(8,128)(2,1)S(1)}, bf16[224,128]{1,0:T(8,128)(2,1)S(1)}, u32[]{:S(2)}, u32[]{:S(2)}) %collective-permute-start.12) | collective-permute-done | bytes 57376 | tf_op jit(solution)/shard_map/ppermute | solution.py:52
  72.0 1.2 %collective-permute-start.15 = (bf16[224,128]{1,0:T(8,128)(2,1)S(1)}, bf16[224,128]{1,0:T(8,128)(2,1)S(1)}, u32[]{:S(2)}, u32[]{:S(2)}) collective-permute-start(bf16[224,128]{1,0:T(8,128)(2,1)S(1)} %get-tuple-element.44), channel_id=1, source_target_pairs={{0,96},{1,33},{2,98},{3,35},{4,100},{5,37},{6,102},{7,39},{8,104},... | collective-permute-start | bytes 172040 | tf_op jit(solution)/shard_map/ppermute | solution.py:52
  73.3 2.6 %collective-permute-start.16 = (bf16[224,128]{1,0:T(8,128)(2,1)S(1)}, bf16[224,128]{1,0:T(8,128)(2,1)S(1)}, u32[]{:S(2)}, u32[]{:S(2)}) collective-permute-start(bf16[224,128]{1,0:T(8,128)(2,1)S(1)} %get-tuple-element.44), channel_id=1, source_target_pairs={{0,24},{1,9},{2,26},{3,11},{4,28},{5,13},{6,30},{7,15},{8,16},{9,1... | collective-permute-start | bytes 172040 | tf_op jit(solution)/shard_map/ppermute | solution.py:52
  75.8 0.1 collective-permute-start.17
  76.0 1.7 %collective-permute-done.16 = bf16[224,128]{1,0:T(8,128)(2,1)S(1)} collective-permute-done((bf16[224,128]{1,0:T(8,128)(2,1)S(1)}, bf16[224,128]{1,0:T(8,128)(2,1)S(1)}, u32[]{:S(2)}, u32[]{:S(2)}) %collective-permute-start.16) | collective-permute-done | bytes 57376 | tf_op jit(solution)/shard_map/ppermute | solution.py:52
  77.7 2.1 %collective-permute-done.17 = bf16[224,128]{1,0:T(8,128)(2,1)S(1)} collective-permute-done((bf16[224,128]{1,0:T(8,128)(2,1)S(1)}, bf16[224,128]{1,0:T(8,128)(2,1)S(1)}, u32[]{:S(2)}, u32[]{:S(2)}) %collective-permute-start.17) | collective-permute-done | bytes 57376 | tf_op jit(solution)/shard_map/ppermute | solution.py:52
  79.8 2.6 %collective-permute-start.20 = (bf16[4,224,128]{2,1,0:T(8,128)(2,1)S(1)}, bf16[4,224,128]{2,1,0:T(8,128)(2,1)S(1)}, u32[]{:S(2)}, u32[]{:S(2)}) collective-permute-start(bf16[4,224,128]{2,1,0:T(8,128)(2,1)S(1)} %bitcast_dynamic-update-slice_fusion.4), channel_id=1, source_target_pairs={{0,40},{1,121},{2,42},{3,123},{4,44},{5,125},{6,46},{7,127},{8,32}... | collective-permute-start | bytes 688136 | tf_op jit(solution)/shard_map/ppermute | solution.py:52
  82.3 2.2 %collective-permute-start.19 = (bf16[4,224,128]{2,1,0:T(8,128)(2,1)S(1)}, bf16[4,224,128]{2,1,0:T(8,128)(2,1)S(1)}, u32[]{:S(2)}, u32[]{:S(2)}) collective-permute-start(bf16[4,224,128]{2,1,0:T(8,128)(2,1)S(1)} %bitcast_dynamic-update-slice_fusion.4), channel_id=1, source_target_pairs={{0,8},{1,25},{2,10},{3,27},{4,12},{5,29},{6,14},{7,31},{8,0},{9,17... | collective-permute-start | bytes 688136 | tf_op jit(solution)/shard_map/ppermute | solution.py:52
  84.6 0.4 collective-permute-start.18
  84.9 0.1 broadcast_in_dim.32
  85.1 6.7 %collective-permute-done.18 = bf16[4,224,128]{2,1,0:T(8,128)(2,1)S(1)} collective-permute-done((bf16[4,224,128]{2,1,0:T(8,128)(2,1)S(1)}, bf16[4,224,128]{2,1,0:T(8,128)(2,1)S(1)}, u32[]{:S(2)}, u32[]{:S(2)}) %collective-permute-start.18) | collective-permute-done | bytes 229408 | tf_op jit(solution)/shard_map/ppermute | solution.py:52
  91.9 10.0 %collective-permute-start.21 = (bf16[28,128,128]{2,1,0:T(8,128)(2,1)S(1)}, bf16[28,128,128]{2,1,0:T(8,128)(2,1)S(1)}, u32[]{:S(2)}, u32[]{:S(2)}) collective-permute-start(bf16[28,128,128]{2,1,0:T(8,128)(2,1)S(1)} %bitcast.60), channel_id=1, source_target_pairs={{0,1},{1,0},{2,3},{3,2},{4,5},{5,4},{6,7},{7,6},{8,9},{9,8},{10,11... | collective-permute-start | bytes 2752520 | tf_op jit(solution)/shard_map/ppermute | solution.py:52
  101.9 2.5 %shard_map.129 = bf16[3,10,23,128]{3,2,1,0:T(8,128)(2,1)} custom-call(bf16[3,384,128]{2,1,0:T(8,128)(2,1)S(1)} %get-tuple-element.24.d, bf16[3,10,23,128]{3,2,1,0:T(8,128)(2,1)S(1)} %get-tuple-element.60.xin, bf16[3,10,23,128]{3,2,1,0:T(8,128)(2,1)S(1)} %get-tuple-element.59.cot, bf16[3,3,3,128,128]{4,3,2,1,0:T(8,128)(2,1)S(1)} %get-tuple-element.58.k1, ...), custom_call_target="tpu_custom_call" | custom-call | flops 1000000000 | bytes 3000000 | tf_op jit(solution)/shard_map/pallas_call | solution.py:365
  104.3 1.8 %shard_map.133 = (f32[27,128,128]{2,1,0:T(8,128)}, f32[27,128,128]{2,1,0:T(8,128)}) custom-call(s32[5]{0:T(128)S(1)} %stack.95.pos, bf16[28,128,128]{2,1,0:T(8,128)(2,1)S(1)} %bitcast.61), custom_call_target="tpu_custom_call" | custom-call | flops 100000000 | bytes 1000000 | tf_op jit(solution)/shard_map/pallas_call | solution.py:396
  106.2 1.9 %shard_map.134 = (f32[27,128,128]{2,1,0:T(8,128)}, f32[27,128,128]{2,1,0:T(8,128)}, f32[1,128]{1,0:T(1,128)}, f32[1,128]{1,0:T(1,128)}) custom-call(s32[5]{0:T(128)S(1)} %stack.95.pos, bf16[28,128,128]{2,1,0:T(8,128)(2,1)S(1)} %bitcast.62, bf16[28,128,128]{2,1,0:T(8,128)(2,1)S(1)} %collective-permute-done.21.other, ...), custom_call_target="tpu_custom_call", output_to_operand_aliasing={{0}: (3, {}), {1}: (4, {})} | custom-call | flops 1000000 | bytes 1000000 | tf_op jit(solution)/shard_map/pallas_call | solution.py:405
  (42 shorter events, 0.7 us)
Async XLA Ops:
  0.6 10.2 %copy-start = (bf16[3,3,3,128,128]{4,3,2,1,0:T(8,128)(2,1)S(1)}, bf16[3,3,3,128,128]{4,3,2,1,0:T(8,128)(2,1)}, u32[]{:S(2)}) copy-start(bf16[3,3,3,128,128]{4,3,2,1,0:T(8,128)(2,1)} %param.13) | copy-start | bytes 2654212
  1.6 11.9 %collective-permute-start.1 = (bf16[2,3,2,23,128]{4,3,2,1,0:T(8,128)(2,1)S(1)}, bf16[2,3,2,23,128]{4,3,2,1,0:T(8,128)(2,1)S(1)}, u32[]{:S(2)}, u32[]{:S(2)}) collective-permute-start(bf16[2,3,2,23,128]{4,3,2,1,0:T(8,128)(2,1)S(1)} %pad_maximum_fusion.3), channel_id=1, source_target_pairs={{1,0},{2,1},{3,2},{4,3},{5,4},{6,5},{7,6},{8,7},{9,8},{10,9},{11,1... | collective-permute-start | bytes 211976 | tf_op jit(solution)/shard_map/ppermute | solution.py:94
  6.7 6.7 %collective-permute-start = (bf16[2,3,2,23,128]{4,3,2,1,0:T(8,128)(2,1)S(1)}, bf16[2,3,2,23,128]{4,3,2,1,0:T(8,128)(2,1)S(1)}, u32[]{:S(2)}, u32[]{:S(2)}) collective-permute-start(bf16[2,3,2,23,128]{4,3,2,1,0:T(8,128)(2,1)S(1)} %pad_maximum_fusion.2), channel_id=1, source_target_pairs={{0,1},{1,2},{2,3},{3,4},{4,5},{5,6},{6,7},{7,8},{8,9},{9,10},{10,1... | collective-permute-start | bytes 211976 | tf_op jit(solution)/shard_map/ppermute | solution.py:94
  10.9 2.4 %copy-start.1 = (f32[128]{0:T(128)S(1)}, f32[128]{0:T(128)}, u32[]{:S(2)}) copy-start(f32[128]{0:T(128)} %param.12) | copy-start | bytes 1540
  10.9 2.4 %copy-start.2 = (f32[128]{0:T(128)S(1)}, f32[128]{0:T(128)}, u32[]{:S(2)}) copy-start(f32[128]{0:T(128)} %param.14) | copy-start | bytes 1540
  10.9 2.4 %copy-start.3 = (f32[128]{0:T(128)S(1)}, f32[128]{0:T(128)}, u32[]{:S(2)}) copy-start(f32[128]{0:T(128)} %param.15) | copy-start | bytes 1540
  10.9 2.4 %copy-start.4 = (f32[128]{0:T(128)S(1)}, f32[128]{0:T(128)}, u32[]{:S(2)}) copy-start(f32[128]{0:T(128)} %param.16) | copy-start | bytes 1540
  10.9 2.4 %copy-start.5 = (f32[128]{0:T(128)S(1)}, f32[128]{0:T(128)}, u32[]{:S(2)}) copy-start(f32[128]{0:T(128)} %param.17) | copy-start | bytes 1540
  13.6 5.4 %collective-permute-start.3 = (bf16[2,3,14,2,128]{4,3,2,1,0:T(2,128)(2,1)S(1)}, bf16[2,3,14,2,128]{4,3,2,1,0:T(2,128)(2,1)S(1)}, u32[]{:S(2)}, u32[]{:S(2)}) collective-permute-start(bf16[2,3,14,2,128]{4,3,2,1,0:T(2,128)(2,1)S(1)} %pad_maximum_fusion.5), channel_id=1, source_target_pairs={{32,0},{64,32},{96,64},{128,96},{160,128},{192,160},{224,192},{33,... | collective-permute-start | bytes 129032 | tf_op jit(solution)/shard_map/ppermute | solution.py:94
  15.0 5.3 %collective-permute-start.2 = (bf16[2,3,14,2,128]{4,3,2,1,0:T(2,128)(2,1)S(1)}, bf16[2,3,14,2,128]{4,3,2,1,0:T(2,128)(2,1)S(1)}, u32[]{:S(2)}, u32[]{:S(2)}) collective-permute-start(bf16[2,3,14,2,128]{4,3,2,1,0:T(2,128)(2,1)S(1)} %pad_maximum_fusion.4), channel_id=1, source_target_pairs={{0,32},{32,64},{64,96},{96,128},{128,160},{160,192},{192,224},{1,3... | collective-permute-start | bytes 129032 | tf_op jit(solution)/shard_map/ppermute | solution.py:94
  27.2 2.6 %collective-permute-start.4 = (bf16[28,128,128]{2,1,0:T(8,128)(2,1)S(1)}, bf16[28,128,128]{2,1,0:T(8,128)(2,1)S(1)}, u32[]{:S(2)}, u32[]{:S(2)}) collective-permute-start(bf16[28,128,128]{2,1,0:T(8,128)(2,1)S(1)} %get-tuple-element.28), channel_id=1, source_target_pairs={{0,1},{1,0},{2,3},{3,2},{4,5},{5,4},{6,7},{7,6},{8,9},{9,8},{10,11... | collective-permute-start | bytes 2752520 | tf_op jit(solution)/shard_map/ppermute | solution.py:52
  30.6 14.2 %collective-permute-start.5 = (bf16[7,128,128]{2,1,0:T(8,128)(2,1)S(1)}, bf16[7,128,128]{2,1,0:T(8,128)(2,1)S(1)}, u32[]{:S(2)}, u32[]{:S(2)}) collective-permute-start(bf16[7,128,128]{2,1,0:T(8,128)(2,1)S(1)} %get-tuple-element.30), channel_id=1, source_target_pairs={{0,8},{1,25},{2,10},{3,27},{4,12},{5,29},{6,14},{7,31},{8,0},{9,17... | collective-permute-start | bytes 688136 | tf_op jit(solution)/shard_map/ppermute | solution.py:52
  39.9 10.3 %collective-permute-start.6 = (bf16[7,128,128]{2,1,0:T(8,128)(2,1)S(1)}, bf16[7,128,128]{2,1,0:T(8,128)(2,1)S(1)}, u32[]{:S(2)}, u32[]{:S(2)}) collective-permute-start(bf16[7,128,128]{2,1,0:T(8,128)(2,1)S(1)} %get-tuple-element.31), channel_id=1, source_target_pairs={{0,32},{1,97},{2,34},{3,99},{4,36},{5,101},{6,38},{7,103},{8,40},{... | collective-permute-start | bytes 688136 | tf_op jit(solution)/shard_map/ppermute | solution.py:52
  44.7 8.2 %collective-permute-start.7 = (bf16[7,128,128]{2,1,0:T(8,128)(2,1)S(1)}, bf16[7,128,128]{2,1,0:T(8,128)(2,1)S(1)}, u32[]{:S(2)}, u32[]{:S(2)}) collective-permute-start(bf16[7,128,128]{2,1,0:T(8,128)(2,1)S(1)} %get-tuple-element.32), channel_id=1, source_target_pairs={{0,40},{1,121},{2,42},{3,123},{4,44},{5,125},{6,46},{7,127},{8,32}... | collective-permute-start | bytes 688136 | tf_op jit(solution)/shard_map/ppermute | solution.py:52
  53.6 3.4 %collective-permute-start.8 = (bf16[224,128]{1,0:T(8,128)(2,1)S(1)}, bf16[224,128]{1,0:T(8,128)(2,1)S(1)}, u32[]{:S(2)}, u32[]{:S(2)}) collective-permute-start(bf16[224,128]{1,0:T(8,128)(2,1)S(1)} %get-tuple-element.34), channel_id=1, source_target_pairs={{0,24},{1,9},{2,26},{3,11},{4,28},{5,13},{6,30},{7,15},{8,16},{9,1... | collective-permute-start | bytes 172040 | tf_op jit(solution)/shard_map/ppermute | solution.py:52
  53.7 3.4 %collective-permute-start.9 = (bf16[224,128]{1,0:T(8,128)(2,1)S(1)}, bf16[224,128]{1,0:T(8,128)(2,1)S(1)}, u32[]{:S(2)}, u32[]{:S(2)}) collective-permute-start(bf16[224,128]{1,0:T(8,128)(2,1)S(1)} %get-tuple-element.35), channel_id=1, source_target_pairs={{0,96},{1,33},{2,98},{3,35},{4,100},{5,37},{6,102},{7,39},{8,104},... | collective-permute-start | bytes 172040 | tf_op jit(solution)/shard_map/ppermute | solution.py:52
  53.8 4.1 %collective-permute-start.10 = (bf16[224,128]{1,0:T(8,128)(2,1)S(1)}, bf16[224,128]{1,0:T(8,128)(2,1)S(1)}, u32[]{:S(2)}, u32[]{:S(2)}) collective-permute-start(bf16[224,128]{1,0:T(8,128)(2,1)S(1)} %get-tuple-element.36), channel_id=1, source_target_pairs={{0,120},{1,41},{2,122},{3,43},{4,124},{5,45},{6,126},{7,47},{8,112... | collective-permute-start | bytes 172040 | tf_op jit(solution)/shard_map/ppermute | solution.py:52
  57.9 4.6 %collective-permute-start.11 = (f32[224,128]{1,0:T(8,128)S(1)}, f32[224,128]{1,0:T(8,128)S(1)}, u32[]{:S(2)}, u32[]{:S(2)}) collective-permute-start(f32[224,128]{1,0:T(8,128)S(1)} %convert_add_fusion), channel_id=1, source_target_pairs={{0,128},{1,129},{2,130},{3,131},{4,132},{5,133},{6,134},{7,135},{8... | collective-permute-start | bytes 344072 | tf_op jit(solution)/shard_map/ppermute | solution.py:52
  62.6 4.1 %collective-permute-start.14 = (bf16[224,128]{1,0:T(8,128)(2,1)S(1)}, bf16[224,128]{1,0:T(8,128)(2,1)S(1)}, u32[]{:S(2)}, u32[]{:S(2)}) collective-permute-start(bf16[224,128]{1,0:T(8,128)(2,1)S(1)} %add_convert_fusion.1), channel_id=1, source_target_pairs={{0,6},{1,7},{2,0},{3,1},{4,2},{5,3},{6,4},{7,5},{8,14},{9,15},{10,... | collective-permute-start | bytes 172040 | tf_op jit(solution)/shard_map/ppermute | solution.py:52
  62.7 5.8 %collective-permute-start.13 = (bf16[224,128]{1,0:T(8,128)(2,1)S(1)}, bf16[224,128]{1,0:T(8,128)(2,1)S(1)}, u32[]{:S(2)}, u32[]{:S(2)}) collective-permute-start(bf16[224,128]{1,0:T(8,128)(2,1)S(1)} %add_convert_fusion.1), channel_id=1, source_target_pairs={{0,2},{1,3},{2,4},{3,5},{4,6},{5,7},{6,0},{7,1},{8,10},{9,11},{10,... | collective-permute-start | bytes 172040 | tf_op jit(solution)/shard_map/ppermute | solution.py:52
  65.0 6.9 %collective-permute-start.12 = (bf16[224,128]{1,0:T(8,128)(2,1)S(1)}, bf16[224,128]{1,0:T(8,128)(2,1)S(1)}, u32[]{:S(2)}, u32[]{:S(2)}) collective-permute-start(bf16[224,128]{1,0:T(8,128)(2,1)S(1)} %add_convert_fusion.1), channel_id=1, source_target_pairs={{0,4},{1,5},{2,6},{3,7},{4,0},{5,1},{6,2},{7,3},{8,12},{9,13},{10,... | collective-permute-start | bytes 172040 | tf_op jit(solution)/shard_map/ppermute | solution.py:52
  72.0 3.9 %collective-permute-start.15 = (bf16[224,128]{1,0:T(8,128)(2,1)S(1)}, bf16[224,128]{1,0:T(8,128)(2,1)S(1)}, u32[]{:S(2)}, u32[]{:S(2)}) collective-permute-start(bf16[224,128]{1,0:T(8,128)(2,1)S(1)} %get-tuple-element.44), channel_id=1, source_target_pairs={{0,96},{1,33},{2,98},{3,35},{4,100},{5,37},{6,102},{7,39},{8,104},... | collective-permute-start | bytes 172040 | tf_op jit(solution)/shard_map/ppermute | solution.py:52
  73.3 4.4 %collective-permute-start.16 = (bf16[224,128]{1,0:T(8,128)(2,1)S(1)}, bf16[224,128]{1,0:T(8,128)(2,1)S(1)}, u32[]{:S(2)}, u32[]{:S(2)}) collective-permute-start(bf16[224,128]{1,0:T(8,128)(2,1)S(1)} %get-tuple-element.44), channel_id=1, source_target_pairs={{0,24},{1,9},{2,26},{3,11},{4,28},{5,13},{6,30},{7,15},{8,16},{9,1... | collective-permute-start | bytes 172040 | tf_op jit(solution)/shard_map/ppermute | solution.py:52
  75.8 3.9 %collective-permute-start.17 = (bf16[224,128]{1,0:T(8,128)(2,1)S(1)}, bf16[224,128]{1,0:T(8,128)(2,1)S(1)}, u32[]{:S(2)}, u32[]{:S(2)}) collective-permute-start(bf16[224,128]{1,0:T(8,128)(2,1)S(1)} %get-tuple-element.44), channel_id=1, source_target_pairs={{0,120},{1,41},{2,122},{3,43},{4,124},{5,45},{6,126},{7,47},{8,112... | collective-permute-start | bytes 172040 | tf_op jit(solution)/shard_map/ppermute | solution.py:52
  79.8 12.1 %collective-permute-start.20 = (bf16[4,224,128]{2,1,0:T(8,128)(2,1)S(1)}, bf16[4,224,128]{2,1,0:T(8,128)(2,1)S(1)}, u32[]{:S(2)}, u32[]{:S(2)}) collective-permute-start(bf16[4,224,128]{2,1,0:T(8,128)(2,1)S(1)} %bitcast_dynamic-update-slice_fusion.4), channel_id=1, source_target_pairs={{0,40},{1,121},{2,42},{3,123},{4,44},{5,125},{6,46},{7,127},{8,32}... | collective-permute-start | bytes 688136 | tf_op jit(solution)/shard_map/ppermute | solution.py:52
  82.3 9.5 %collective-permute-start.19 = (bf16[4,224,128]{2,1,0:T(8,128)(2,1)S(1)}, bf16[4,224,128]{2,1,0:T(8,128)(2,1)S(1)}, u32[]{:S(2)}, u32[]{:S(2)}) collective-permute-start(bf16[4,224,128]{2,1,0:T(8,128)(2,1)S(1)} %bitcast_dynamic-update-slice_fusion.4), channel_id=1, source_target_pairs={{0,8},{1,25},{2,10},{3,27},{4,12},{5,29},{6,14},{7,31},{8,0},{9,17... | collective-permute-start | bytes 688136 | tf_op jit(solution)/shard_map/ppermute | solution.py:52
  84.6 7.2 %collective-permute-start.18 = (bf16[4,224,128]{2,1,0:T(8,128)(2,1)S(1)}, bf16[4,224,128]{2,1,0:T(8,128)(2,1)S(1)}, u32[]{:S(2)}, u32[]{:S(2)}) collective-permute-start(bf16[4,224,128]{2,1,0:T(8,128)(2,1)S(1)} %bitcast_dynamic-update-slice_fusion.4), channel_id=1, source_target_pairs={{0,32},{1,97},{2,34},{3,99},{4,36},{5,101},{6,38},{7,103},{8,40},{... | collective-permute-start | bytes 688136 | tf_op jit(solution)/shard_map/ppermute | solution.py:52
  91.9 14.3 %collective-permute-start.21 = (bf16[28,128,128]{2,1,0:T(8,128)(2,1)S(1)}, bf16[28,128,128]{2,1,0:T(8,128)(2,1)S(1)}, u32[]{:S(2)}, u32[]{:S(2)}) collective-permute-start(bf16[28,128,128]{2,1,0:T(8,128)(2,1)S(1)} %bitcast.60), channel_id=1, source_target_pairs={{0,1},{1,0},{2,3},{3,2},{4,5},{5,4},{6,7},{7,6},{8,9},{9,8},{10,11... | collective-permute-start | bytes 2752520 | tf_op jit(solution)/shard_map/ppermute | solution.py:52

commit v4 on v3

--- a/solution.py
+++ b/solution.py
@@ -88,10 +88,14 @@
     return write_other(pos, v, other, one, two)
 
 
-def exchange(low, high, axis, size):
-    up = [(i, i + 1) for i in range(size - 1)]
-    down = [(i + 1, i) for i in range(size - 1)]
-    return lax.ppermute(high, axis, up), lax.ppermute(low, axis, down)
+def exchange(low, high, axis, size, odd):
+    def swap(first, sent):
+        pairs = [(a, b) for i in range(first, size - 1, 2) for a, b in ((i, i + 1), (i + 1, i))]
+        return lax.ppermute(sent, axis, pairs)
+
+    far = swap(1, jnp.where(odd, high, low))
+    near = swap(0, jnp.where(odd, low, high))
+    return near, far
 
 
 def adjoint(field, k, kw, acc, n):
@@ -119,7 +123,7 @@
     send_out, bias_out, d_out, field, cotan,
     line, x_all, a3, g3, a2, acc, acc2,
 ):
-    row0, col0, core = pos[0], pos[1], pos[2]
+    row0, col0, core, odd = pos[0], pos[1], pos[2], pos[5]
     bias1, scale1, shift1, scale2, shift2 = (vectors[i:i + 1, :] for i in range(5))
     line[...] = jnp.zeros_like(line)
     x_all[...] = jnp.zeros_like(x_all)
@@ -139,9 +143,9 @@
             if 2 <= w < 12:
                 dst[at + 2:at + 25, :] = main[t, w - 2].astype(f32)
             else:
-                dst[at + 2:at + 25, :] = sides[w // 12, which, t, w % 12].astype(f32)
-            dst[at:at + 2, :] = ends[0, which, t, w].astype(f32)
-            dst[at + 25:at + 27, :] = ends[1, which, t, w].astype(f32)
+                dst[at + 2:at + 25, :] = sides[core if w >= 12 else 1 - core, which, t, w % 12].astype(f32)
+            dst[at:at + 2, :] = ends[1 - odd, which, t, w].astype(f32)
+            dst[at + 25:at + 27, :] = ends[odd, which, t, w].astype(f32)
 
     def own_cells(half, t, first):
         at = pl.ds(pl.multiple_of(t * 320, 64), 320)
@@ -416,21 +420,27 @@
     xin, cot = jnp.swapaxes(block_input, 1, 2), jnp.swapaxes(cotangent, 1, 2)
     low = jnp.stack([xin[:, :2], cot[:, :2]])
     high = jnp.stack([xin[:, 8:], cot[:, 8:]])
-    left, right = exchange(low, high, "wa", 32)
+    ha, wa = lax.axis_index("ha"), lax.axis_index("wa")
+    y, x, c = ha % 4, wa // 8, wa % 2
+    near, far = exchange(low, high, "wa", 32, c == 1)
+    left, right = jnp.where(c == 0, far, near), jnp.where(c == 0, near, far)
+
+    def fetch(*arrays):
+        return lax.optimization_barrier(tuple(jnp.where(wa < 32, v, jnp.zeros_like(v)) for v in arrays))
+
+    xin, cot = fetch(xin, cot)
+    k1, k2 = fetch(kernel_one, kernel_two)
+    vectors = jnp.pad(jnp.stack([bias_one, scale_one, shift_one, scale_two, shift_two]), ((0, 3), (0, 0)))
 
     def edge(s):
         main = jnp.stack([xin[:, :, s], cot[:, :, s]])
         return jnp.concatenate([left[:, :, :, s], main, right[:, :, :, s]], axis=2)
 
-    above, below = exchange(edge(slice(0, 2)), edge(slice(21, 23)), "ha", 8)
-    ha, wa = lax.axis_index("ha"), lax.axis_index("wa")
-    y, x, c = ha % 4, wa // 8, wa % 2
+    ends = jnp.stack(exchange(edge(slice(0, 2)), edge(slice(21, 23)), "ha", 8, ha % 2 == 1))
     one, three = position(x, y, 1), position(x, y, 3)
     first, second = jnp.where(c == 0, one, three), jnp.where(c == 0, three, one)
-    pos = jnp.stack([ha * 23 - 2, wa * 10 - 2, c, first, second]).astype(jnp.int32)
-    vectors = jnp.pad(jnp.stack([bias_one, scale_one, shift_one, scale_two, shift_two]), ((0, 3), (0, 0)))
-    xin, cot, k1, k2 = (jnp.where(wa < 32, v, jnp.zeros_like(v)) for v in (xin, cot, kernel_one, kernel_two))
-    send, biases, d, field, cotan = local(pos, xin, cot, jnp.stack([left, right]), jnp.stack([above, below]), k1, k2, vectors)
+    pos = jnp.stack([ha * 23 - 2, wa * 10 - 2, c, first, second, ha % 2]).astype(jnp.int32)
+    send, biases, d, field, cotan = local(pos, xin, cot, jnp.stack([near, far]), ends, k1, k2, vectors)
     got = shifted(send, "c", 2, 1)
     own = own_grads(pos, field, cotan, biases)
     gin = input_grad(d, xin, cot, k1, vectors)

time: 109 us -> 101 us (0.927)
  the two profiles are of different devices: /device:TPU:1 before, /device:TPU:33 now
where the time goes in v4:
time: 101 us
  starting transfers between devices  51.9 us (51%)
  waiting for transfers between devices  27.2 us (27%)
  Pallas kernels  15.9 us (16%)
  other arithmetic  2.86 us (3%)
  local copies, waits for them, and re-layouts  1.48 us (1%)
  between operations  1.2 us (1%)
    ppermute x18, starting transfers between devices, send_pairs(): return lax.ppermute(v, AXES, pairs)  41.8 us
    ppermute x18, waiting for transfers between devices, send_pairs(): return lax.ppermute(v, AXES, pairs)  24.7 us
    ppermute x4, starting transfers between devices, swap(): return lax.ppermute(sent, axis, pairs)  10.1 us
    pallas_call x1, Pallas kernels, local(): call(local_kernel, [((28, 128, 128), bf16), ((128, 128), f32), ((3, 384,...  6.75 us
    ppermute x4, waiting for transfers between devices, swap(): return lax.ppermute(sent, axis, pairs)  2.54 us
    pallas_call x1, Pallas kernels, input_grad(): call(input_kernel, [((3, 10, 23, 128), bf16)], [VMEM] * 5, [pltpu.VMEM((4...  2.46 us
    select_n x2, other arithmetic, fetch(): jnp.where(wa < 32, v, jnp.zeros_like(v))  2.35 us
  transfers between devices with their start and end apart: 22, of which 14 were waited for; matrix products, arithmetic and copies ran while one was open for 3% of the time, Pallas kernels for 6%

profile of v4, /device:TPU:33, one launch (start us, length us, event | category | flops | bytes accessed | tf_op | source)
XLA Modules:
  0.0 100.5 jit_solution(2177776227768781724)
XLA Ops:
  0.7 0.9 slice_bitcast_fusion.2
  1.6 0.8 collective-permute-start
  2.4 4.8 %collective-permute-start.1 = (bf16[2,3,2,23,128]{4,3,2,1,0:T(8,128)(2,1)S(1)}, bf16[2,3,2,23,128]{4,3,2,1,0:T(8,128)(2,1)S(1)}, u32[]{:S(2)}, u32[]{:S(2)}) collective-permute-start(bf16[2,3,2,23,128]{4,3,2,1,0:T(8,128)(2,1)S(1)} %get-tuple-element.67), channel_id=1, source_target_pairs={{1,2},{2,1},{3,4},{4,3},{5,6},{6,5},{7,8},{8,7},{9,10},{10,9},{11,... | collective-permute-start | bytes 211976 | tf_op jit(solution)/shard_map/ppermute | solution.py:94
  7.2 1.0 %broadcast_select_fusion.2 = (bf16[3,10,23,128]{3,2,1,0:T(8,128)(2,1)S(1)}, bf16[3,10,23,128]{3,2,1,0:T(8,128)(2,1)S(1)}) fusion(pred[]{:T(512)S(6)} %lt.51, bf16[3,23,10,128]{3,1,2,0:T(8,128)(2,1)} %param.10, bf16[3,23,10,128]{3,1,2,0:T(8,128)(2,1)} %param.9), kind=kLoop, calls=%fused_computation.6 | loop fusion | flops 176640 | bytes 706561 | tf_op jit(solution)/shard_map/jit(_where)/select_n | solution.py:429
  8.3 1.3 %broadcast_select_fusion = (bf16[3,3,3,128,128]{4,3,2,1,0:T(8,128)(2,1)S(1)}, bf16[3,3,3,128,128]{4,3,2,1,0:T(8,128)(2,1)S(1)}) fusion(bf16[3,3,3,128,128]{4,3,2,1,0:T(8,128)(2,1)S(1)} %copy-done, pred[]{:T(512)S(6)} %lt.51, bf16[3,3,3,128,128]{4,3,2,1,0:T(8,128)(2,1)} %param.11), kind=kLoop, calls=%fused_computation | loop fusion | flops 884736 | bytes 3538945 | tf_op jit(solution)/shard_map/jit(_where)/select_n | solution.py:429
  9.8 0.1 stack.99.pos
  10.0 0.2 broadcast_select_fusion.5
  10.2 4.2 %collective-permute-start.3 = (bf16[2,3,14,2,128]{4,3,2,1,0:T(2,128)(2,1)S(1)}, bf16[2,3,14,2,128]{4,3,2,1,0:T(2,128)(2,1)S(1)}, u32[]{:S(2)}, u32[]{:S(2)}) collective-permute-start(bf16[2,3,14,2,128]{4,3,2,1,0:T(2,128)(2,1)S(1)} %broadcast_select_fusion.4), channel_id=1, source_target_pairs={{32,64},{64,32},{96,128},{128,96},{160,192},{192,160},{33,65},{65,... | collective-permute-start | bytes 129032 | tf_op jit(solution)/shard_map/ppermute | solution.py:94
  14.4 0.4 collective-permute-start.2
  14.8 2.3 %collective-permute-done.3 = bf16[2,3,14,2,128]{4,3,2,1,0:T(2,128)(2,1)S(1)} collective-permute-done((bf16[2,3,14,2,128]{4,3,2,1,0:T(2,128)(2,1)S(1)}, bf16[2,3,14,2,128]{4,3,2,1,0:T(2,128)(2,1)S(1)}, u32[]{:S(2)}, u32[]{:S(2)}) %collective-permute-start.3) | collective-permute-done | bytes 43040 | tf_op jit(solution)/shard_map/ppermute | solution.py:94
  17.1 0.3 collective-permute-done.2
  17.4 0.1 pad_maximum_fusion.1.ends
  17.5 6.8 %shard_map.128 = (bf16[28,128,128]{2,1,0:T(8,128)(2,1)S(1)}, f32[128,128]{1,0:T(8,128)S(1)}, bf16[3,384,128]{2,1,0:T(8,128)(2,1)S(1)}, bf16[2,384,1024]{2,1,0:T(8,128)(2,1)S(1)}, bf16[2,1024,384]{2,1,0:T(8,128)(2,1)S(1)}) custom-call(s32[6]{0:T(128)S(1)} %stack.99.pos, bf16[3,10,23,128]{3,2,1,0:T(8,128)(2,1)S(1)} %get-tuple-element.28.xin, ...), custom_call_target="tpu_custom_call" | custom-call | flops 3000000000 | bytes 8000000 | tf_op jit(solution)/shard_map/pallas_call | solution.py:342
  24.3 0.1 collective-permute-start.4
  24.4 1.6 %shard_map.130.own = f32[28,128,128]{2,1,0:T(8,128)S(1)} custom-call(s32[6]{0:T(128)S(1)} %stack.99.pos, bf16[2,384,1024]{2,1,0:T(8,128)(2,1)S(1)} %get-tuple-element.33.field, bf16[2,1024,384]{2,1,0:T(8,128)(2,1)S(1)} %get-tuple-element.34.cotan, f32[128,128]{1,0:T(8,128)S(1)} %get-tuple-element.35.biases), custom_call_target="tpu_custom_call" | custom-call | flops 1000000000 | bytes 3000000 | tf_op jit(solution)/shard_map/pallas_call | solution.py:363
  25.9 0.9 collective-permute-done.4.got
  26.8 0.8 shard_map.131
  27.6 7.4 %collective-permute-start.5 = (bf16[7,128,128]{2,1,0:T(8,128)(2,1)S(1)}, bf16[7,128,128]{2,1,0:T(8,128)(2,1)S(1)}, u32[]{:S(2)}, u32[]{:S(2)}) collective-permute-start(bf16[7,128,128]{2,1,0:T(8,128)(2,1)S(1)} %get-tuple-element.38), channel_id=1, source_target_pairs={{0,8},{1,25},{2,10},{3,27},{4,12},{5,29},{6,14},{7,31},{8,0},{9,17... | collective-permute-start | bytes 688136 | tf_op jit(solution)/shard_map/ppermute | solution.py:52
  35.0 2.5 %collective-permute-start.7 = (bf16[7,128,128]{2,1,0:T(8,128)(2,1)S(1)}, bf16[7,128,128]{2,1,0:T(8,128)(2,1)S(1)}, u32[]{:S(2)}, u32[]{:S(2)}) collective-permute-start(bf16[7,128,128]{2,1,0:T(8,128)(2,1)S(1)} %get-tuple-element.40), channel_id=1, source_target_pairs={{0,40},{1,121},{2,42},{3,123},{4,44},{5,125},{6,46},{7,127},{8,32}... | collective-permute-start | bytes 688136 | tf_op jit(solution)/shard_map/ppermute | solution.py:52
  37.5 1.1 %collective-permute-done.5 = bf16[7,128,128]{2,1,0:T(8,128)(2,1)S(1)} collective-permute-done((bf16[7,128,128]{2,1,0:T(8,128)(2,1)S(1)}, bf16[7,128,128]{2,1,0:T(8,128)(2,1)S(1)}, u32[]{:S(2)}, u32[]{:S(2)}) %collective-permute-start.5) | collective-permute-done | bytes 229408 | tf_op jit(solution)/shard_map/ppermute | solution.py:52
  38.5 5.0 %collective-permute-done.6 = bf16[7,128,128]{2,1,0:T(8,128)(2,1)S(1)} collective-permute-done((bf16[7,128,128]{2,1,0:T(8,128)(2,1)S(1)}, bf16[7,128,128]{2,1,0:T(8,128)(2,1)S(1)}, u32[]{:S(2)}, u32[]{:S(2)}) %collective-permute-start.6) | collective-permute-done | bytes 229408 | tf_op jit(solution)/shard_map/ppermute | solution.py:52
  43.5 0.6 shard_map.132
  44.2 0.1 collective-permute-start.8
  44.3 0.1 collective-permute-start.9
  44.4 2.5 %collective-permute-start.10 = (bf16[224,128]{1,0:T(8,128)(2,1)S(1)}, bf16[224,128]{1,0:T(8,128)(2,1)S(1)}, u32[]{:S(2)}, u32[]{:S(2)}) collective-permute-start(bf16[224,128]{1,0:T(8,128)(2,1)S(1)} %get-tuple-element.44), channel_id=1, source_target_pairs={{0,120},{1,41},{2,122},{3,43},{4,124},{5,45},{6,126},{7,47},{8,112... | collective-permute-start | bytes 172040 | tf_op jit(solution)/shard_map/ppermute | solution.py:52
  46.9 0.4 collective-permute-done.8
  47.3 0.4 collective-permute-done.9
  47.7 0.8 collective-permute-done.10
  48.5 1.7 %collective-permute-start.11 = (f32[224,128]{1,0:T(8,128)S(1)}, f32[224,128]{1,0:T(8,128)S(1)}, u32[]{:S(2)}, u32[]{:S(2)}) collective-permute-start(f32[224,128]{1,0:T(8,128)S(1)} %convert_add_fusion), channel_id=1, source_target_pairs={{0,128},{1,129},{2,130},{3,131},{4,132},{5,133},{6,134},{7,135},{8... | collective-permute-start | bytes 344072 | tf_op jit(solution)/shard_map/ppermute | solution.py:52
  50.2 2.2 %collective-permute-done.11 = f32[224,128]{1,0:T(8,128)S(1)} collective-permute-done((f32[224,128]{1,0:T(8,128)S(1)}, f32[224,128]{1,0:T(8,128)S(1)}, u32[]{:S(2)}, u32[]{:S(2)}) %collective-permute-start.11) | collective-permute-done | bytes 114720 | tf_op jit(solution)/shard_map/ppermute | solution.py:52
  52.5 3.1 %collective-permute-start.14 = (bf16[224,128]{1,0:T(8,128)(2,1)S(1)}, bf16[224,128]{1,0:T(8,128)(2,1)S(1)}, u32[]{:S(2)}, u32[]{:S(2)}) collective-permute-start(bf16[224,128]{1,0:T(8,128)(2,1)S(1)} %add_convert_fusion.1), channel_id=1, source_target_pairs={{0,6},{1,7},{2,0},{3,1},{4,2},{5,3},{6,4},{7,5},{8,14},{9,15},{10,... | collective-permute-start | bytes 172040 | tf_op jit(solution)/shard_map/ppermute | solution.py:52
  55.6 3.1 %collective-permute-start.12 = (bf16[224,128]{1,0:T(8,128)(2,1)S(1)}, bf16[224,128]{1,0:T(8,128)(2,1)S(1)}, u32[]{:S(2)}, u32[]{:S(2)}) collective-permute-start(bf16[224,128]{1,0:T(8,128)(2,1)S(1)} %add_convert_fusion.1), channel_id=1, source_target_pairs={{0,4},{1,5},{2,6},{3,7},{4,0},{5,1},{6,2},{7,3},{8,12},{9,13},{10,... | collective-permute-start | bytes 172040 | tf_op jit(solution)/shard_map/ppermute | solution.py:52
  58.7 2.4 %collective-permute-done.13 = bf16[224,128]{1,0:T(8,128)(2,1)S(1)} collective-permute-done((bf16[224,128]{1,0:T(8,128)(2,1)S(1)}, bf16[224,128]{1,0:T(8,128)(2,1)S(1)}, u32[]{:S(2)}, u32[]{:S(2)}) %collective-permute-start.13) | collective-permute-done | bytes 57376 | tf_op jit(solution)/shard_map/ppermute | solution.py:52
  61.1 1.5 %collective-permute-done.12 = bf16[224,128]{1,0:T(8,128)(2,1)S(1)} collective-permute-done((bf16[224,128]{1,0:T(8,128)(2,1)S(1)}, bf16[224,128]{1,0:T(8,128)(2,1)S(1)}, u32[]{:S(2)}, u32[]{:S(2)}) %collective-permute-start.12) | collective-permute-done | bytes 57376 | tf_op jit(solution)/shard_map/ppermute | solution.py:52
  62.6 0.1 bitcast_dynamic-update-slice_fusion.7
  62.7 1.1 %collective-permute-start.15 = (bf16[224,128]{1,0:T(8,128)(2,1)S(1)}, bf16[224,128]{1,0:T(8,128)(2,1)S(1)}, u32[]{:S(2)}, u32[]{:S(2)}) collective-permute-start(bf16[224,128]{1,0:T(8,128)(2,1)S(1)} %get-tuple-element.52), channel_id=1, source_target_pairs={{0,96},{1,33},{2,98},{3,35},{4,100},{5,37},{6,102},{7,39},{8,104},... | collective-permute-start | bytes 172040 | tf_op jit(solution)/shard_map/ppermute | solution.py:52
  63.7 2.9 %collective-permute-start.16 = (bf16[224,128]{1,0:T(8,128)(2,1)S(1)}, bf16[224,128]{1,0:T(8,128)(2,1)S(1)}, u32[]{:S(2)}, u32[]{:S(2)}) collective-permute-start(bf16[224,128]{1,0:T(8,128)(2,1)S(1)} %get-tuple-element.52), channel_id=1, source_target_pairs={{0,24},{1,9},{2,26},{3,11},{4,28},{5,13},{6,30},{7,15},{8,16},{9,1... | collective-permute-start | bytes 172040 | tf_op jit(solution)/shard_map/ppermute | solution.py:52
  66.6 1.8 %collective-permute-done.16 = bf16[224,128]{1,0:T(8,128)(2,1)S(1)} collective-permute-done((bf16[224,128]{1,0:T(8,128)(2,1)S(1)}, bf16[224,128]{1,0:T(8,128)(2,1)S(1)}, u32[]{:S(2)}, u32[]{:S(2)}) %collective-permute-start.16) | collective-permute-done | bytes 57376 | tf_op jit(solution)/shard_map/ppermute | solution.py:52
  68.5 2.3 %collective-permute-done.17 = bf16[224,128]{1,0:T(8,128)(2,1)S(1)} collective-permute-done((bf16[224,128]{1,0:T(8,128)(2,1)S(1)}, bf16[224,128]{1,0:T(8,128)(2,1)S(1)}, u32[]{:S(2)}, u32[]{:S(2)}) %collective-permute-start.17) | collective-permute-done | bytes 57376 | tf_op jit(solution)/shard_map/ppermute | solution.py:52
  70.8 1.4 %collective-permute-start.20 = (bf16[4,224,128]{2,1,0:T(8,128)(2,1)S(1)}, bf16[4,224,128]{2,1,0:T(8,128)(2,1)S(1)}, u32[]{:S(2)}, u32[]{:S(2)}) collective-permute-start(bf16[4,224,128]{2,1,0:T(8,128)(2,1)S(1)} %bitcast_dynamic-update-slice_fusion.4), channel_id=1, source_target_pairs={{0,40},{1,121},{2,42},{3,123},{4,44},{5,125},{6,46},{7,127},{8,32}... | collective-permute-start | bytes 688136 | tf_op jit(solution)/shard_map/ppermute | solution.py:52
  72.2 2.2 %collective-permute-start.19 = (bf16[4,224,128]{2,1,0:T(8,128)(2,1)S(1)}, bf16[4,224,128]{2,1,0:T(8,128)(2,1)S(1)}, u32[]{:S(2)}, u32[]{:S(2)}) collective-permute-start(bf16[4,224,128]{2,1,0:T(8,128)(2,1)S(1)} %bitcast_dynamic-update-slice_fusion.4), channel_id=1, source_target_pairs={{0,8},{1,25},{2,10},{3,27},{4,12},{5,29},{6,14},{7,31},{8,0},{9,17... | collective-permute-start | bytes 688136 | tf_op jit(solution)/shard_map/ppermute | solution.py:52
  74.4 1.6 %collective-permute-start.18 = (bf16[4,224,128]{2,1,0:T(8,128)(2,1)S(1)}, bf16[4,224,128]{2,1,0:T(8,128)(2,1)S(1)}, u32[]{:S(2)}, u32[]{:S(2)}) collective-permute-start(bf16[4,224,128]{2,1,0:T(8,128)(2,1)S(1)} %bitcast_dynamic-update-slice_fusion.4), channel_id=1, source_target_pairs={{0,32},{1,97},{2,34},{3,99},{4,36},{5,101},{6,38},{7,103},{8,40},{... | collective-permute-start | bytes 688136 | tf_op jit(solution)/shard_map/ppermute | solution.py:52
  76.0 0.1 broadcast_in_dim.32
  76.2 5.9 %collective-permute-done.18 = bf16[4,224,128]{2,1,0:T(8,128)(2,1)S(1)} collective-permute-done((bf16[4,224,128]{2,1,0:T(8,128)(2,1)S(1)}, bf16[4,224,128]{2,1,0:T(8,128)(2,1)S(1)}, u32[]{:S(2)}, u32[]{:S(2)}) %collective-permute-start.18) | collective-permute-done | bytes 229408 | tf_op jit(solution)/shard_map/ppermute | solution.py:52
  82.2 12.1 %collective-permute-start.21 = (bf16[28,128,128]{2,1,0:T(8,128)(2,1)S(1)}, bf16[28,128,128]{2,1,0:T(8,128)(2,1)S(1)}, u32[]{:S(2)}, u32[]{:S(2)}) collective-permute-start(bf16[28,128,128]{2,1,0:T(8,128)(2,1)S(1)} %bitcast.61), channel_id=1, source_target_pairs={{0,1},{1,0},{2,3},{3,2},{4,5},{5,4},{6,7},{7,6},{8,9},{9,8},{10,11... | collective-permute-start | bytes 2752520 | tf_op jit(solution)/shard_map/ppermute | solution.py:52
  94.2 2.5 %shard_map.129 = bf16[3,10,23,128]{3,2,1,0:T(8,128)(2,1)} custom-call(bf16[3,384,128]{2,1,0:T(8,128)(2,1)S(1)} %get-tuple-element.32.d, bf16[3,10,23,128]{3,2,1,0:T(8,128)(2,1)S(1)} %get-tuple-element.28.xin, bf16[3,10,23,128]{3,2,1,0:T(8,128)(2,1)S(1)} %get-tuple-element.29.cot, bf16[3,3,3,128,128]{4,3,2,1,0:T(8,128)(2,1)S(1)} %get-tuple-element.30.k1, ...), custom_call_target="tpu_custom_call" | custom-call | flops 1000000000 | bytes 3000000 | tf_op jit(solution)/shard_map/pallas_call | solution.py:369
  96.7 1.8 %shard_map.133 = (f32[27,128,128]{2,1,0:T(8,128)}, f32[27,128,128]{2,1,0:T(8,128)}) custom-call(s32[6]{0:T(128)S(1)} %stack.99.pos, bf16[28,128,128]{2,1,0:T(8,128)(2,1)S(1)} %bitcast.62), custom_call_target="tpu_custom_call" | custom-call | flops 100000000 | bytes 1000000 | tf_op jit(solution)/shard_map/pallas_call | solution.py:400
  98.5 1.9 %shard_map.134 = (f32[27,128,128]{2,1,0:T(8,128)}, f32[27,128,128]{2,1,0:T(8,128)}, f32[1,128]{1,0:T(1,128)}, f32[1,128]{1,0:T(1,128)}) custom-call(s32[6]{0:T(128)S(1)} %stack.99.pos, bf16[28,128,128]{2,1,0:T(8,128)(2,1)S(1)} %bitcast.63, bf16[28,128,128]{2,1,0:T(8,128)(2,1)S(1)} %collective-permute-done.21.other, ...), custom_call_target="tpu_custom_call", output_to_operand_aliasing={{0}: (3, {}), {1}: (4, {})} | custom-call | flops 1000000 | bytes 1000000 | tf_op jit(solution)/shard_map/pallas_call | solution.py:409
  (43 shorter events, 0.6 us)
Async XLA Ops:
  0.6 7.6 %copy-start = (bf16[3,3,3,128,128]{4,3,2,1,0:T(8,128)(2,1)S(1)}, bf16[3,3,3,128,128]{4,3,2,1,0:T(8,128)(2,1)}, u32[]{:S(2)}) copy-start(bf16[3,3,3,128,128]{4,3,2,1,0:T(8,128)(2,1)} %param.13) | copy-start | bytes 2654212
  1.6 8.3 %collective-permute-start = (bf16[2,3,2,23,128]{4,3,2,1,0:T(8,128)(2,1)S(1)}, bf16[2,3,2,23,128]{4,3,2,1,0:T(8,128)(2,1)S(1)}, u32[]{:S(2)}, u32[]{:S(2)}) collective-permute-start(bf16[2,3,2,23,128]{4,3,2,1,0:T(8,128)(2,1)S(1)} %get-tuple-element.66), channel_id=1, source_target_pairs={{0,1},{1,0},{2,3},{3,2},{4,5},{5,4},{6,7},{7,6},{8,9},{9,8},{10,11... | collective-permute-start | bytes 211976 | tf_op jit(solution)/shard_map/ppermute | solution.py:94
  2.4 7.5 %collective-permute-start.1 = (bf16[2,3,2,23,128]{4,3,2,1,0:T(8,128)(2,1)S(1)}, bf16[2,3,2,23,128]{4,3,2,1,0:T(8,128)(2,1)S(1)}, u32[]{:S(2)}, u32[]{:S(2)}) collective-permute-start(bf16[2,3,2,23,128]{4,3,2,1,0:T(8,128)(2,1)S(1)} %get-tuple-element.67), channel_id=1, source_target_pairs={{1,2},{2,1},{3,4},{4,3},{5,6},{6,5},{7,8},{8,7},{9,10},{10,9},{11,... | collective-permute-start | bytes 211976 | tf_op jit(solution)/shard_map/ppermute | solution.py:94
  8.3 1.5 %copy-start.1 = (f32[128]{0:T(128)S(1)}, f32[128]{0:T(128)}, u32[]{:S(2)}) copy-start(f32[128]{0:T(128)} %param.12) | copy-start | bytes 1540
  8.3 1.5 %copy-start.2 = (f32[128]{0:T(128)S(1)}, f32[128]{0:T(128)}, u32[]{:S(2)}) copy-start(f32[128]{0:T(128)} %param.14) | copy-start | bytes 1540
  8.3 1.5 %copy-start.3 = (f32[128]{0:T(128)S(1)}, f32[128]{0:T(128)}, u32[]{:S(2)}) copy-start(f32[128]{0:T(128)} %param.15) | copy-start | bytes 1540
  8.3 1.5 %copy-start.4 = (f32[128]{0:T(128)S(1)}, f32[128]{0:T(128)}, u32[]{:S(2)}) copy-start(f32[128]{0:T(128)} %param.16) | copy-start | bytes 1540
  8.3 1.5 %copy-start.5 = (f32[128]{0:T(128)S(1)}, f32[128]{0:T(128)}, u32[]{:S(2)}) copy-start(f32[128]{0:T(128)} %param.17) | copy-start | bytes 1540
  10.2 6.9 %collective-permute-start.3 = (bf16[2,3,14,2,128]{4,3,2,1,0:T(2,128)(2,1)S(1)}, bf16[2,3,14,2,128]{4,3,2,1,0:T(2,128)(2,1)S(1)}, u32[]{:S(2)}, u32[]{:S(2)}) collective-permute-start(bf16[2,3,14,2,128]{4,3,2,1,0:T(2,128)(2,1)S(1)} %broadcast_select_fusion.4), channel_id=1, source_target_pairs={{32,64},{64,32},{96,128},{128,96},{160,192},{192,160},{33,65},{65,... | collective-permute-start | bytes 129032 | tf_op jit(solution)/shard_map/ppermute | solution.py:94
  14.4 3.0 %collective-permute-start.2 = (bf16[2,3,14,2,128]{4,3,2,1,0:T(2,128)(2,1)S(1)}, bf16[2,3,14,2,128]{4,3,2,1,0:T(2,128)(2,1)S(1)}, u32[]{:S(2)}, u32[]{:S(2)}) collective-permute-start(bf16[2,3,14,2,128]{4,3,2,1,0:T(2,128)(2,1)S(1)} %get-tuple-element.53), channel_id=1, source_target_pairs={{0,32},{32,0},{64,96},{96,64},{128,160},{160,128},{192,224},{224,1... | collective-permute-start | bytes 129032 | tf_op jit(solution)/shard_map/ppermute | solution.py:94
  24.3 2.6 %collective-permute-start.4 = (bf16[28,128,128]{2,1,0:T(8,128)(2,1)S(1)}, bf16[28,128,128]{2,1,0:T(8,128)(2,1)S(1)}, u32[]{:S(2)}, u32[]{:S(2)}) collective-permute-start(bf16[28,128,128]{2,1,0:T(8,128)(2,1)S(1)} %get-tuple-element.36), channel_id=1, source_target_pairs={{0,1},{1,0},{2,3},{3,2},{4,5},{5,4},{6,7},{7,6},{8,9},{9,8},{10,11... | collective-permute-start | bytes 2752520 | tf_op jit(solution)/shard_map/ppermute | solution.py:52
  27.6 11.0 %collective-permute-start.5 = (bf16[7,128,128]{2,1,0:T(8,128)(2,1)S(1)}, bf16[7,128,128]{2,1,0:T(8,128)(2,1)S(1)}, u32[]{:S(2)}, u32[]{:S(2)}) collective-permute-start(bf16[7,128,128]{2,1,0:T(8,128)(2,1)S(1)} %get-tuple-element.38), channel_id=1, source_target_pairs={{0,8},{1,25},{2,10},{3,27},{4,12},{5,29},{6,14},{7,31},{8,0},{9,17... | collective-permute-start | bytes 688136 | tf_op jit(solution)/shard_map/ppermute | solution.py:52
  35.0 8.5 %collective-permute-start.6 = (bf16[7,128,128]{2,1,0:T(8,128)(2,1)S(1)}, bf16[7,128,128]{2,1,0:T(8,128)(2,1)S(1)}, u32[]{:S(2)}, u32[]{:S(2)}) collective-permute-start(bf16[7,128,128]{2,1,0:T(8,128)(2,1)S(1)} %get-tuple-element.39), channel_id=1, source_target_pairs={{0,32},{1,97},{2,34},{3,99},{4,36},{5,101},{6,38},{7,103},{8,40},{... | collective-permute-start | bytes 688136 | tf_op jit(solution)/shard_map/ppermute | solution.py:52
  35.0 8.5 %collective-permute-start.7 = (bf16[7,128,128]{2,1,0:T(8,128)(2,1)S(1)}, bf16[7,128,128]{2,1,0:T(8,128)(2,1)S(1)}, u32[]{:S(2)}, u32[]{:S(2)}) collective-permute-start(bf16[7,128,128]{2,1,0:T(8,128)(2,1)S(1)} %get-tuple-element.40), channel_id=1, source_target_pairs={{0,40},{1,121},{2,42},{3,123},{4,44},{5,125},{6,46},{7,127},{8,32}... | collective-permute-start | bytes 688136 | tf_op jit(solution)/shard_map/ppermute | solution.py:52
  44.2 3.1 %collective-permute-start.8 = (bf16[224,128]{1,0:T(8,128)(2,1)S(1)}, bf16[224,128]{1,0:T(8,128)(2,1)S(1)}, u32[]{:S(2)}, u32[]{:S(2)}) collective-permute-start(bf16[224,128]{1,0:T(8,128)(2,1)S(1)} %get-tuple-element.42), channel_id=1, source_target_pairs={{0,24},{1,9},{2,26},{3,11},{4,28},{5,13},{6,30},{7,15},{8,16},{9,1... | collective-permute-start | bytes 172040 | tf_op jit(solution)/shard_map/ppermute | solution.py:52
  44.3 3.4 %collective-permute-start.9 = (bf16[224,128]{1,0:T(8,128)(2,1)S(1)}, bf16[224,128]{1,0:T(8,128)(2,1)S(1)}, u32[]{:S(2)}, u32[]{:S(2)}) collective-permute-start(bf16[224,128]{1,0:T(8,128)(2,1)S(1)} %get-tuple-element.43), channel_id=1, source_target_pairs={{0,96},{1,33},{2,98},{3,35},{4,100},{5,37},{6,102},{7,39},{8,104},... | collective-permute-start | bytes 172040 | tf_op jit(solution)/shard_map/ppermute | solution.py:52
  44.4 4.1 %collective-permute-start.10 = (bf16[224,128]{1,0:T(8,128)(2,1)S(1)}, bf16[224,128]{1,0:T(8,128)(2,1)S(1)}, u32[]{:S(2)}, u32[]{:S(2)}) collective-permute-start(bf16[224,128]{1,0:T(8,128)(2,1)S(1)} %get-tuple-element.44), channel_id=1, source_target_pairs={{0,120},{1,41},{2,122},{3,43},{4,124},{5,45},{6,126},{7,47},{8,112... | collective-permute-start | bytes 172040 | tf_op jit(solution)/shard_map/ppermute | solution.py:52
  48.5 4.0 %collective-permute-start.11 = (f32[224,128]{1,0:T(8,128)S(1)}, f32[224,128]{1,0:T(8,128)S(1)}, u32[]{:S(2)}, u32[]{:S(2)}) collective-permute-start(f32[224,128]{1,0:T(8,128)S(1)} %convert_add_fusion), channel_id=1, source_target_pairs={{0,128},{1,129},{2,130},{3,131},{4,132},{5,133},{6,134},{7,135},{8... | collective-permute-start | bytes 344072 | tf_op jit(solution)/shard_map/ppermute | solution.py:52
  52.5 6.2 %collective-permute-start.14 = (bf16[224,128]{1,0:T(8,128)(2,1)S(1)}, bf16[224,128]{1,0:T(8,128)(2,1)S(1)}, u32[]{:S(2)}, u32[]{:S(2)}) collective-permute-start(bf16[224,128]{1,0:T(8,128)(2,1)S(1)} %add_convert_fusion.1), channel_id=1, source_target_pairs={{0,6},{1,7},{2,0},{3,1},{4,2},{5,3},{6,4},{7,5},{8,14},{9,15},{10,... | collective-permute-start | bytes 172040 | tf_op jit(solution)/shard_map/ppermute | solution.py:52
  55.6 5.5 %collective-permute-start.13 = (bf16[224,128]{1,0:T(8,128)(2,1)S(1)}, bf16[224,128]{1,0:T(8,128)(2,1)S(1)}, u32[]{:S(2)}, u32[]{:S(2)}) collective-permute-start(bf16[224,128]{1,0:T(8,128)(2,1)S(1)} %add_convert_fusion.1), channel_id=1, source_target_pairs={{0,2},{1,3},{2,4},{3,5},{4,6},{5,7},{6,0},{7,1},{8,10},{9,11},{10,... | collective-permute-start | bytes 172040 | tf_op jit(solution)/shard_map/ppermute | solution.py:52
  55.6 7.0 %collective-permute-start.12 = (bf16[224,128]{1,0:T(8,128)(2,1)S(1)}, bf16[224,128]{1,0:T(8,128)(2,1)S(1)}, u32[]{:S(2)}, u32[]{:S(2)}) collective-permute-start(bf16[224,128]{1,0:T(8,128)(2,1)S(1)} %add_convert_fusion.1), channel_id=1, source_target_pairs={{0,4},{1,5},{2,6},{3,7},{4,0},{5,1},{6,2},{7,3},{8,12},{9,13},{10,... | collective-permute-start | bytes 172040 | tf_op jit(solution)/shard_map/ppermute | solution.py:52
  62.7 3.9 %collective-permute-start.15 = (bf16[224,128]{1,0:T(8,128)(2,1)S(1)}, bf16[224,128]{1,0:T(8,128)(2,1)S(1)}, u32[]{:S(2)}, u32[]{:S(2)}) collective-permute-start(bf16[224,128]{1,0:T(8,128)(2,1)S(1)} %get-tuple-element.52), channel_id=1, source_target_pairs={{0,96},{1,33},{2,98},{3,35},{4,100},{5,37},{6,102},{7,39},{8,104},... | collective-permute-start | bytes 172040 | tf_op jit(solution)/shard_map/ppermute | solution.py:52
  63.7 4.7 %collective-permute-start.16 = (bf16[224,128]{1,0:T(8,128)(2,1)S(1)}, bf16[224,128]{1,0:T(8,128)(2,1)S(1)}, u32[]{:S(2)}, u32[]{:S(2)}) collective-permute-start(bf16[224,128]{1,0:T(8,128)(2,1)S(1)} %get-tuple-element.52), channel_id=1, source_target_pairs={{0,24},{1,9},{2,26},{3,11},{4,28},{5,13},{6,30},{7,15},{8,16},{9,1... | collective-permute-start | bytes 172040 | tf_op jit(solution)/shard_map/ppermute | solution.py:52
  66.6 4.2 %collective-permute-start.17 = (bf16[224,128]{1,0:T(8,128)(2,1)S(1)}, bf16[224,128]{1,0:T(8,128)(2,1)S(1)}, u32[]{:S(2)}, u32[]{:S(2)}) collective-permute-start(bf16[224,128]{1,0:T(8,128)(2,1)S(1)} %get-tuple-element.52), channel_id=1, source_target_pairs={{0,120},{1,41},{2,122},{3,43},{4,124},{5,45},{6,126},{7,47},{8,112... | collective-permute-start | bytes 172040 | tf_op jit(solution)/shard_map/ppermute | solution.py:52
  70.8 11.3 %collective-permute-start.20 = (bf16[4,224,128]{2,1,0:T(8,128)(2,1)S(1)}, bf16[4,224,128]{2,1,0:T(8,128)(2,1)S(1)}, u32[]{:S(2)}, u32[]{:S(2)}) collective-permute-start(bf16[4,224,128]{2,1,0:T(8,128)(2,1)S(1)} %bitcast_dynamic-update-slice_fusion.4), channel_id=1, source_target_pairs={{0,40},{1,121},{2,42},{3,123},{4,44},{5,125},{6,46},{7,127},{8,32}... | collective-permute-start | bytes 688136 | tf_op jit(solution)/shard_map/ppermute | solution.py:52
  72.2 9.9 %collective-permute-start.19 = (bf16[4,224,128]{2,1,0:T(8,128)(2,1)S(1)}, bf16[4,224,128]{2,1,0:T(8,128)(2,1)S(1)}, u32[]{:S(2)}, u32[]{:S(2)}) collective-permute-start(bf16[4,224,128]{2,1,0:T(8,128)(2,1)S(1)} %bitcast_dynamic-update-slice_fusion.4), channel_id=1, source_target_pairs={{0,8},{1,25},{2,10},{3,27},{4,12},{5,29},{6,14},{7,31},{8,0},{9,17... | collective-permute-start | bytes 688136 | tf_op jit(solution)/shard_map/ppermute | solution.py:52
  74.4 7.6 %collective-permute-start.18 = (bf16[4,224,128]{2,1,0:T(8,128)(2,1)S(1)}, bf16[4,224,128]{2,1,0:T(8,128)(2,1)S(1)}, u32[]{:S(2)}, u32[]{:S(2)}) collective-permute-start(bf16[4,224,128]{2,1,0:T(8,128)(2,1)S(1)} %bitcast_dynamic-update-slice_fusion.4), channel_id=1, source_target_pairs={{0,32},{1,97},{2,34},{3,99},{4,36},{5,101},{6,38},{7,103},{8,40},{... | collective-permute-start | bytes 688136 | tf_op jit(solution)/shard_map/ppermute | solution.py:52
  82.2 16.3 %collective-permute-start.21 = (bf16[28,128,128]{2,1,0:T(8,128)(2,1)S(1)}, bf16[28,128,128]{2,1,0:T(8,128)(2,1)S(1)}, u32[]{:S(2)}, u32[]{:S(2)}) collective-permute-start(bf16[28,128,128]{2,1,0:T(8,128)(2,1)S(1)} %bitcast.61), channel_id=1, source_target_pairs={{0,1},{1,0},{2,3},{3,2},{4,5},{5,4},{6,7},{7,6},{8,9},{9,8},{10,11... | collective-permute-start | bytes 2752520 | tf_op jit(solution)/shard_map/ppermute | solution.py:52

commit v5 on v4

--- a/solution.py
+++ b/solution.py
@@ -77,8 +77,8 @@
     kept, *sends = fold(pos, kept, exchange_squares(sends, FIRST))
     got = exchange_squares(sends, SECOND)
     v = kept + got[0].astype(f32) + got[1].astype(f32) + got[2].astype(f32)
-    v = v + shifted(v, "zl", 2, 1)
     v = v.astype(bf16)
+    v = (v.astype(f32) + shifted(v, "zl", 2, 1).astype(f32)).astype(bf16)
     got = {k: shifted(v, "zh", 4, k) for k in (1, 2, 3)}
     v = ((v.astype(f32) + got[2].astype(f32)) + (got[1].astype(f32) + got[3].astype(f32))).astype(bf16)
     v = gather(v, SECOND, second)
@@ -425,13 +425,6 @@
     near, far = exchange(low, high, "wa", 32, c == 1)
     left, right = jnp.where(c == 0, far, near), jnp.where(c == 0, near, far)
 
-    def fetch(*arrays):
-        return lax.optimization_barrier(tuple(jnp.where(wa < 32, v, jnp.zeros_like(v)) for v in arrays))
-
-    xin, cot = fetch(xin, cot)
-    k1, k2 = fetch(kernel_one, kernel_two)
-    vectors = jnp.pad(jnp.stack([bias_one, scale_one, shift_one, scale_two, shift_two]), ((0, 3), (0, 0)))
-
     def edge(s):
         main = jnp.stack([xin[:, :, s], cot[:, :, s]])
         return jnp.concatenate([left[:, :, :, s], main, right[:, :, :, s]], axis=2)
@@ -440,6 +433,8 @@
     one, three = position(x, y, 1), position(x, y, 3)
     first, second = jnp.where(c == 0, one, three), jnp.where(c == 0, three, one)
     pos = jnp.stack([ha * 23 - 2, wa * 10 - 2, c, first, second, ha % 2]).astype(jnp.int32)
+    vectors = jnp.pad(jnp.stack([bias_one, scale_one, shift_one, scale_two, shift_two]), ((0, 3), (0, 0)))
+    xin, cot, k1, k2 = (jnp.where(wa < 32, v, jnp.zeros_like(v)) for v in (xin, cot, kernel_one, kernel_two))
     send, biases, d, field, cotan = local(pos, xin, cot, jnp.stack([near, far]), ends, k1, k2, vectors)
     got = shifted(send, "c", 2, 1)
     own = own_grads(pos, field, cotan, biases)

time: 101 us -> 99.2 us (0.982)
  the two profiles are of different devices: /device:TPU:33 before, /device:TPU:1 now
where the time goes in v5:
time: 99.2 us; the launch traced here: 98.9 us
  starting transfers between devices  46.2 us (47%)
  waiting for transfers between devices  30.4 us (31%)
  Pallas kernels  15.9 us (16%)
  other arithmetic  2.86 us (3%)
  local copies, waits for them, and re-layouts  2.4 us (2%)
  between operations  1.2 us (1%)
    ppermute x18, starting transfers between devices, send_pairs(): return lax.ppermute(v, AXES, pairs)  35.7 us
    ppermute x18, waiting for transfers between devices, send_pairs(): return lax.ppermute(v, AXES, pairs)  28.5 us
    ppermute x4, starting transfers between devices, swap(): return lax.ppermute(sent, axis, pairs)  10.4 us
    pallas_call x1, Pallas kernels, local(): call(local_kernel, [((28, 128, 128), bf16), ((128, 128), f32), ((3, 384,...  6.75 us
    pallas_call x1, Pallas kernels, input_grad(): call(input_kernel, [((3, 10, 23, 128), bf16)], [VMEM] * 5, [pltpu.VMEM((4...  2.46 us
    select_n x2, other arithmetic, body(): jnp.where(wa < 32, v, jnp.zeros_like(v))  2.35 us
  transfers between devices with their start and end apart: 22, of which 15 were waited for; matrix products, arithmetic and copies ran while one was open for 4% of the time, Pallas kernels for 6%

profile of v5, /device:TPU:1, one launch (start us, length us, event | category | flops | bytes accessed | tf_op | source)
XLA Modules:
  0.0 98.9 jit_solution(4039576673724292615)
XLA Ops:
  0.7 0.9 slice_bitcast_fusion.2
  1.6 3.3 %collective-permute-start = (bf16[2,3,2,23,128]{4,3,2,1,0:T(8,128)(2,1)S(1)}, bf16[2,3,2,23,128]{4,3,2,1,0:T(8,128)(2,1)S(1)}, u32[]{:S(2)}, u32[]{:S(2)}) collective-permute-start(bf16[2,3,2,23,128]{4,3,2,1,0:T(8,128)(2,1)S(1)} %get-tuple-element.58), channel_id=1, source_target_pairs={{0,1},{1,0},{2,3},{3,2},{4,5},{5,4},{6,7},{7,6},{8,9},{9,8},{10,11... | collective-permute-start | bytes 211976 | tf_op jit(solution)/shard_map/ppermute | solution.py:94
  4.9 3.1 %collective-permute-start.1 = (bf16[2,3,2,23,128]{4,3,2,1,0:T(8,128)(2,1)S(1)}, bf16[2,3,2,23,128]{4,3,2,1,0:T(8,128)(2,1)S(1)}, u32[]{:S(2)}, u32[]{:S(2)}) collective-permute-start(bf16[2,3,2,23,128]{4,3,2,1,0:T(8,128)(2,1)S(1)} %get-tuple-element.59), channel_id=1, source_target_pairs={{1,2},{2,1},{3,4},{4,3},{5,6},{6,5},{7,8},{8,7},{9,10},{10,9},{11,... | collective-permute-start | bytes 211976 | tf_op jit(solution)/shard_map/ppermute | solution.py:94
  8.0 1.0 %broadcast_select_fusion.2 = (bf16[3,10,23,128]{3,2,1,0:T(8,128)(2,1)S(1)}, bf16[3,10,23,128]{3,2,1,0:T(8,128)(2,1)S(1)}) fusion(pred[]{:T(512)S(6)} %lt.51, bf16[3,23,10,128]{3,1,2,0:T(8,128)(2,1)} %param.10, bf16[3,23,10,128]{3,1,2,0:T(8,128)(2,1)} %param.9), kind=kLoop, calls=%fused_computation.6 | loop fusion | flops 176640 | bytes 706561 | tf_op jit(solution)/shard_map/jit(_where)/select_n | solution.py:437
  9.1 1.3 %broadcast_select_fusion = (bf16[3,3,3,128,128]{4,3,2,1,0:T(8,128)(2,1)S(1)}, bf16[3,3,3,128,128]{4,3,2,1,0:T(8,128)(2,1)S(1)}) fusion(bf16[3,3,3,128,128]{4,3,2,1,0:T(8,128)(2,1)S(1)} %copy-done, pred[]{:T(512)S(6)} %lt.51, bf16[3,3,3,128,128]{4,3,2,1,0:T(8,128)(2,1)} %param.11), kind=kLoop, calls=%fused_computation | loop fusion | flops 884736 | bytes 3538945 | tf_op jit(solution)/shard_map/jit(_where)/select_n | solution.py:437
  10.4 1.0 slice_bitcast_fusion.4
  11.6 0.5 collective-permute-done.1
  12.2 0.2 broadcast_select_fusion.5
  12.5 0.7 collective-permute-start.3
  13.1 3.4 %collective-permute-start.2 = (bf16[2,3,14,2,128]{4,3,2,1,0:T(2,128)(2,1)S(1)}, bf16[2,3,14,2,128]{4,3,2,1,0:T(2,128)(2,1)S(1)}, u32[]{:S(2)}, u32[]{:S(2)}) collective-permute-start(bf16[2,3,14,2,128]{4,3,2,1,0:T(2,128)(2,1)S(1)} %get-tuple-element.45), channel_id=1, source_target_pairs={{0,32},{32,0},{64,96},{96,64},{128,160},{160,128},{192,224},{224,1... | collective-permute-start | bytes 129032 | tf_op jit(solution)/shard_map/ppermute | solution.py:94
  16.6 1.4 %collective-permute-done.2 = bf16[2,3,14,2,128]{4,3,2,1,0:T(2,128)(2,1)S(1)} collective-permute-done((bf16[2,3,14,2,128]{4,3,2,1,0:T(2,128)(2,1)S(1)}, bf16[2,3,14,2,128]{4,3,2,1,0:T(2,128)(2,1)S(1)}, u32[]{:S(2)}, u32[]{:S(2)}) %collective-permute-start.2) | collective-permute-done | bytes 43040 | tf_op jit(solution)/shard_map/ppermute | solution.py:94
  18.0 0.1 pad_maximum_fusion.1.ends
  18.1 6.8 %shard_map.128 = (bf16[28,128,128]{2,1,0:T(8,128)(2,1)S(1)}, f32[128,128]{1,0:T(8,128)S(1)}, bf16[3,384,128]{2,1,0:T(8,128)(2,1)S(1)}, bf16[2,384,1024]{2,1,0:T(8,128)(2,1)S(1)}, bf16[2,1024,384]{2,1,0:T(8,128)(2,1)S(1)}) custom-call(s32[6]{0:T(128)S(1)} %stack.99.pos, bf16[3,10,23,128]{3,2,1,0:T(8,128)(2,1)S(1)} %get-tuple-element.67.xin, ...), custom_call_target="tpu_custom_call" | custom-call | flops 3000000000 | bytes 8000000 | tf_op jit(solution)/shard_map/pallas_call | solution.py:342
  24.9 1.6 %shard_map.130.own = f32[28,128,128]{2,1,0:T(8,128)S(1)} custom-call(s32[6]{0:T(128)S(1)} %stack.99.pos, bf16[2,384,1024]{2,1,0:T(8,128)(2,1)S(1)} %get-tuple-element.25.field, bf16[2,1024,384]{2,1,0:T(8,128)(2,1)S(1)} %get-tuple-element.26.cotan, f32[128,128]{1,0:T(8,128)S(1)} %get-tuple-element.27.biases), custom_call_target="tpu_custom_call" | custom-call | flops 1000000000 | bytes 3000000 | tf_op jit(solution)/shard_map/pallas_call | solution.py:363
  26.5 0.9 collective-permute-done.4.got
  27.4 0.8 shard_map.131
  28.2 7.1 %collective-permute-start.5 = (bf16[7,128,128]{2,1,0:T(8,128)(2,1)S(1)}, bf16[7,128,128]{2,1,0:T(8,128)(2,1)S(1)}, u32[]{:S(2)}, u32[]{:S(2)}) collective-permute-start(bf16[7,128,128]{2,1,0:T(8,128)(2,1)S(1)} %get-tuple-element.30), channel_id=1, source_target_pairs={{0,8},{1,25},{2,10},{3,27},{4,12},{5,29},{6,14},{7,31},{8,0},{9,17... | collective-permute-start | bytes 688136 | tf_op jit(solution)/shard_map/ppermute | solution.py:52
  35.3 3.6 %collective-permute-start.6 = (bf16[7,128,128]{2,1,0:T(8,128)(2,1)S(1)}, bf16[7,128,128]{2,1,0:T(8,128)(2,1)S(1)}, u32[]{:S(2)}, u32[]{:S(2)}) collective-permute-start(bf16[7,128,128]{2,1,0:T(8,128)(2,1)S(1)} %get-tuple-element.31), channel_id=1, source_target_pairs={{0,32},{1,97},{2,34},{3,99},{4,36},{5,101},{6,38},{7,103},{8,40},{... | collective-permute-start | bytes 688136 | tf_op jit(solution)/shard_map/ppermute | solution.py:52
  38.9 5.4 %collective-permute-done.6 = bf16[7,128,128]{2,1,0:T(8,128)(2,1)S(1)} collective-permute-done((bf16[7,128,128]{2,1,0:T(8,128)(2,1)S(1)}, bf16[7,128,128]{2,1,0:T(8,128)(2,1)S(1)}, u32[]{:S(2)}, u32[]{:S(2)}) %collective-permute-start.6) | collective-permute-done | bytes 229408 | tf_op jit(solution)/shard_map/ppermute | solution.py:52
  44.3 2.8 %collective-permute-done.7 = bf16[7,128,128]{2,1,0:T(8,128)(2,1)S(1)} collective-permute-done((bf16[7,128,128]{2,1,0:T(8,128)(2,1)S(1)}, bf16[7,128,128]{2,1,0:T(8,128)(2,1)S(1)}, u32[]{:S(2)}, u32[]{:S(2)}) %collective-permute-start.7) | collective-permute-done | bytes 229408 | tf_op jit(solution)/shard_map/ppermute | solution.py:52
  47.1 0.6 shard_map.132
  47.7 0.1 collective-permute-start.8
  47.8 0.1 collective-permute-start.9
  47.9 2.5 %collective-permute-start.10 = (bf16[224,128]{1,0:T(8,128)(2,1)S(1)}, bf16[224,128]{1,0:T(8,128)(2,1)S(1)}, u32[]{:S(2)}, u32[]{:S(2)}) collective-permute-start(bf16[224,128]{1,0:T(8,128)(2,1)S(1)} %get-tuple-element.36), channel_id=1, source_target_pairs={{0,120},{1,41},{2,122},{3,43},{4,124},{5,45},{6,126},{7,47},{8,112... | collective-permute-start | bytes 172040 | tf_op jit(solution)/shard_map/ppermute | solution.py:52
  50.5 0.7 collective-permute-done.8
  51.1 0.1 collective-permute-done.9
  51.2 0.8 collective-permute-done.10
  52.1 0.1 collective-permute-start.11
  52.2 3.3 %collective-permute-done.11 = bf16[224,128]{1,0:T(8,128)(2,1)S(1)} collective-permute-done((bf16[224,128]{1,0:T(8,128)(2,1)S(1)}, bf16[224,128]{1,0:T(8,128)(2,1)S(1)}, u32[]{:S(2)}, u32[]{:S(2)}) %collective-permute-start.11) | collective-permute-done | bytes 57376 | tf_op jit(solution)/shard_map/ppermute | solution.py:52
  55.5 0.7 collective-permute-start.14
  56.2 1.7 %collective-permute-start.13 = (bf16[224,128]{1,0:T(8,128)(2,1)S(1)}, bf16[224,128]{1,0:T(8,128)(2,1)S(1)}, u32[]{:S(2)}, u32[]{:S(2)}) collective-permute-start(bf16[224,128]{1,0:T(8,128)(2,1)S(1)} %add_convert_fusion.1), channel_id=1, source_target_pairs={{0,2},{1,3},{2,4},{3,5},{4,6},{5,7},{6,0},{7,1},{8,10},{9,11},{10,... | collective-permute-start | bytes 172040 | tf_op jit(solution)/shard_map/ppermute | solution.py:52
  57.9 2.6 %collective-permute-start.12 = (bf16[224,128]{1,0:T(8,128)(2,1)S(1)}, bf16[224,128]{1,0:T(8,128)(2,1)S(1)}, u32[]{:S(2)}, u32[]{:S(2)}) collective-permute-start(bf16[224,128]{1,0:T(8,128)(2,1)S(1)} %add_convert_fusion.1), channel_id=1, source_target_pairs={{0,4},{1,5},{2,6},{3,7},{4,0},{5,1},{6,2},{7,3},{8,12},{9,13},{10,... | collective-permute-start | bytes 172040 | tf_op jit(solution)/shard_map/ppermute | solution.py:52
  60.5 1.6 %collective-permute-done.13 = bf16[224,128]{1,0:T(8,128)(2,1)S(1)} collective-permute-done((bf16[224,128]{1,0:T(8,128)(2,1)S(1)}, bf16[224,128]{1,0:T(8,128)(2,1)S(1)}, u32[]{:S(2)}, u32[]{:S(2)}) %collective-permute-start.13) | collective-permute-done | bytes 57376 | tf_op jit(solution)/shard_map/ppermute | solution.py:52
  62.1 2.7 %collective-permute-done.12 = bf16[224,128]{1,0:T(8,128)(2,1)S(1)} collective-permute-done((bf16[224,128]{1,0:T(8,128)(2,1)S(1)}, bf16[224,128]{1,0:T(8,128)(2,1)S(1)}, u32[]{:S(2)}, u32[]{:S(2)}) %collective-permute-start.12) | collective-permute-done | bytes 57376 | tf_op jit(solution)/shard_map/ppermute | solution.py:52
  65.0 1.1 %collective-permute-start.15 = (bf16[224,128]{1,0:T(8,128)(2,1)S(1)}, bf16[224,128]{1,0:T(8,128)(2,1)S(1)}, u32[]{:S(2)}, u32[]{:S(2)}) collective-permute-start(bf16[224,128]{1,0:T(8,128)(2,1)S(1)} %get-tuple-element.44), channel_id=1, source_target_pairs={{0,96},{1,33},{2,98},{3,35},{4,100},{5,37},{6,102},{7,39},{8,104},... | collective-permute-start | bytes 172040 | tf_op jit(solution)/shard_map/ppermute | solution.py:52
  66.1 1.9 %collective-permute-start.16 = (bf16[224,128]{1,0:T(8,128)(2,1)S(1)}, bf16[224,128]{1,0:T(8,128)(2,1)S(1)}, u32[]{:S(2)}, u32[]{:S(2)}) collective-permute-start(bf16[224,128]{1,0:T(8,128)(2,1)S(1)} %get-tuple-element.44), channel_id=1, source_target_pairs={{0,24},{1,9},{2,26},{3,11},{4,28},{5,13},{6,30},{7,15},{8,16},{9,1... | collective-permute-start | bytes 172040 | tf_op jit(solution)/shard_map/ppermute | solution.py:52
  68.0 0.1 collective-permute-done.15
  68.1 1.7 %collective-permute-done.16 = bf16[224,128]{1,0:T(8,128)(2,1)S(1)} collective-permute-done((bf16[224,128]{1,0:T(8,128)(2,1)S(1)}, bf16[224,128]{1,0:T(8,128)(2,1)S(1)}, u32[]{:S(2)}, u32[]{:S(2)}) %collective-permute-start.16) | collective-permute-done | bytes 57376 | tf_op jit(solution)/shard_map/ppermute | solution.py:52
  69.8 2.3 %collective-permute-done.17 = bf16[224,128]{1,0:T(8,128)(2,1)S(1)} collective-permute-done((bf16[224,128]{1,0:T(8,128)(2,1)S(1)}, bf16[224,128]{1,0:T(8,128)(2,1)S(1)}, u32[]{:S(2)}, u32[]{:S(2)}) %collective-permute-start.17) | collective-permute-done | bytes 57376 | tf_op jit(solution)/shard_map/ppermute | solution.py:52
  72.2 0.7 collective-permute-start.20
  72.9 2.8 %collective-permute-start.19 = (bf16[4,224,128]{2,1,0:T(8,128)(2,1)S(1)}, bf16[4,224,128]{2,1,0:T(8,128)(2,1)S(1)}, u32[]{:S(2)}, u32[]{:S(2)}) collective-permute-start(bf16[4,224,128]{2,1,0:T(8,128)(2,1)S(1)} %bitcast_dynamic-update-slice_fusion.4), channel_id=1, source_target_pairs={{0,8},{1,25},{2,10},{3,27},{4,12},{5,29},{6,14},{7,31},{8,0},{9,17... | collective-permute-start | bytes 688136 | tf_op jit(solution)/shard_map/ppermute | solution.py:52
  75.7 1.6 %collective-permute-start.18 = (bf16[4,224,128]{2,1,0:T(8,128)(2,1)S(1)}, bf16[4,224,128]{2,1,0:T(8,128)(2,1)S(1)}, u32[]{:S(2)}, u32[]{:S(2)}) collective-permute-start(bf16[4,224,128]{2,1,0:T(8,128)(2,1)S(1)} %bitcast_dynamic-update-slice_fusion.4), channel_id=1, source_target_pairs={{0,32},{1,97},{2,34},{3,99},{4,36},{5,101},{6,38},{7,103},{8,40},{... | collective-permute-start | bytes 688136 | tf_op jit(solution)/shard_map/ppermute | solution.py:52
  77.3 0.1 broadcast_in_dim.32
  77.5 6.0 %collective-permute-done.18 = bf16[4,224,128]{2,1,0:T(8,128)(2,1)S(1)} collective-permute-done((bf16[4,224,128]{2,1,0:T(8,128)(2,1)S(1)}, bf16[4,224,128]{2,1,0:T(8,128)(2,1)S(1)}, u32[]{:S(2)}, u32[]{:S(2)}) %collective-permute-start.18) | collective-permute-done | bytes 229408 | tf_op jit(solution)/shard_map/ppermute | solution.py:52
  83.7 8.9 %collective-permute-start.21 = (bf16[28,128,128]{2,1,0:T(8,128)(2,1)S(1)}, bf16[28,128,128]{2,1,0:T(8,128)(2,1)S(1)}, u32[]{:S(2)}, u32[]{:S(2)}) collective-permute-start(bf16[28,128,128]{2,1,0:T(8,128)(2,1)S(1)} %bitcast.61), channel_id=1, source_target_pairs={{0,1},{1,0},{2,3},{3,2},{4,5},{5,4},{6,7},{7,6},{8,9},{9,8},{10,11... | collective-permute-start | bytes 2752520 | tf_op jit(solution)/shard_map/ppermute | solution.py:52
  92.6 2.5 %shard_map.129 = bf16[3,10,23,128]{3,2,1,0:T(8,128)(2,1)} custom-call(bf16[3,384,128]{2,1,0:T(8,128)(2,1)S(1)} %get-tuple-element.24.d, bf16[3,10,23,128]{3,2,1,0:T(8,128)(2,1)S(1)} %get-tuple-element.67.xin, bf16[3,10,23,128]{3,2,1,0:T(8,128)(2,1)S(1)} %get-tuple-element.66.cot, bf16[3,3,3,128,128]{4,3,2,1,0:T(8,128)(2,1)S(1)} %get-tuple-element.65.k1, ...), custom_call_target="tpu_custom_call" | custom-call | flops 1000000000 | bytes 3000000 | tf_op jit(solution)/shard_map/pallas_call | solution.py:369
  95.1 1.8 %shard_map.133 = (f32[27,128,128]{2,1,0:T(8,128)}, f32[27,128,128]{2,1,0:T(8,128)}) custom-call(s32[6]{0:T(128)S(1)} %stack.99.pos, bf16[28,128,128]{2,1,0:T(8,128)(2,1)S(1)} %bitcast.62), custom_call_target="tpu_custom_call" | custom-call | flops 100000000 | bytes 1000000 | tf_op jit(solution)/shard_map/pallas_call | solution.py:400
  96.9 1.9 %shard_map.134 = (f32[27,128,128]{2,1,0:T(8,128)}, f32[27,128,128]{2,1,0:T(8,128)}, f32[1,128]{1,0:T(1,128)}, f32[1,128]{1,0:T(1,128)}) custom-call(s32[6]{0:T(128)S(1)} %stack.99.pos, bf16[28,128,128]{2,1,0:T(8,128)(2,1)S(1)} %bitcast.63, bf16[28,128,128]{2,1,0:T(8,128)(2,1)S(1)} %collective-permute-done.21.other, ...), custom_call_target="tpu_custom_call", output_to_operand_aliasing={{0}: (3, {}), {1}: (4, {})} | custom-call | flops 1000000 | bytes 1000000 | tf_op jit(solution)/shard_map/pallas_call | solution.py:409
  (42 shorter events, 0.7 us)
Async XLA Ops:
  0.6 8.4 %copy-start = (bf16[3,3,3,128,128]{4,3,2,1,0:T(8,128)(2,1)S(1)}, bf16[3,3,3,128,128]{4,3,2,1,0:T(8,128)(2,1)}, u32[]{:S(2)}) copy-start(bf16[3,3,3,128,128]{4,3,2,1,0:T(8,128)(2,1)} %param.13) | copy-start | bytes 2654212
  1.6 10.0 %collective-permute-start = (bf16[2,3,2,23,128]{4,3,2,1,0:T(8,128)(2,1)S(1)}, bf16[2,3,2,23,128]{4,3,2,1,0:T(8,128)(2,1)S(1)}, u32[]{:S(2)}, u32[]{:S(2)}) collective-permute-start(bf16[2,3,2,23,128]{4,3,2,1,0:T(8,128)(2,1)S(1)} %get-tuple-element.58), channel_id=1, source_target_pairs={{0,1},{1,0},{2,3},{3,2},{4,5},{5,4},{6,7},{7,6},{8,9},{9,8},{10,11... | collective-permute-start | bytes 211976 | tf_op jit(solution)/shard_map/ppermute | solution.py:94
  4.9 7.3 %collective-permute-start.1 = (bf16[2,3,2,23,128]{4,3,2,1,0:T(8,128)(2,1)S(1)}, bf16[2,3,2,23,128]{4,3,2,1,0:T(8,128)(2,1)S(1)}, u32[]{:S(2)}, u32[]{:S(2)}) collective-permute-start(bf16[2,3,2,23,128]{4,3,2,1,0:T(8,128)(2,1)S(1)} %get-tuple-element.59), channel_id=1, source_target_pairs={{1,2},{2,1},{3,4},{4,3},{5,6},{6,5},{7,8},{8,7},{9,10},{10,9},{11,... | collective-permute-start | bytes 211976 | tf_op jit(solution)/shard_map/ppermute | solution.py:94
  9.1 2.4 %copy-start.1 = (f32[128]{0:T(128)S(1)}, f32[128]{0:T(128)}, u32[]{:S(2)}) copy-start(f32[128]{0:T(128)} %param.12) | copy-start | bytes 1540
  9.1 2.4 %copy-start.2 = (f32[128]{0:T(128)S(1)}, f32[128]{0:T(128)}, u32[]{:S(2)}) copy-start(f32[128]{0:T(128)} %param.14) | copy-start | bytes 1540
  9.1 2.4 %copy-start.3 = (f32[128]{0:T(128)S(1)}, f32[128]{0:T(128)}, u32[]{:S(2)}) copy-start(f32[128]{0:T(128)} %param.15) | copy-start | bytes 1540
  9.1 2.4 %copy-start.4 = (f32[128]{0:T(128)S(1)}, f32[128]{0:T(128)}, u32[]{:S(2)}) copy-start(f32[128]{0:T(128)} %param.16) | copy-start | bytes 1540
  9.1 2.4 %copy-start.5 = (f32[128]{0:T(128)S(1)}, f32[128]{0:T(128)}, u32[]{:S(2)}) copy-start(f32[128]{0:T(128)} %param.17) | copy-start | bytes 1540
  12.5 4.1 %collective-permute-start.3 = (bf16[2,3,14,2,128]{4,3,2,1,0:T(2,128)(2,1)S(1)}, bf16[2,3,14,2,128]{4,3,2,1,0:T(2,128)(2,1)S(1)}, u32[]{:S(2)}, u32[]{:S(2)}) collective-permute-start(bf16[2,3,14,2,128]{4,3,2,1,0:T(2,128)(2,1)S(1)} %broadcast_select_fusion.4), channel_id=1, source_target_pairs={{32,64},{64,32},{96,128},{128,96},{160,192},{192,160},{33,65},{65,... | collective-permute-start | bytes 129032 | tf_op jit(solution)/shard_map/ppermute | solution.py:94
  13.1 4.8 %collective-permute-start.2 = (bf16[2,3,14,2,128]{4,3,2,1,0:T(2,128)(2,1)S(1)}, bf16[2,3,14,2,128]{4,3,2,1,0:T(2,128)(2,1)S(1)}, u32[]{:S(2)}, u32[]{:S(2)}) collective-permute-start(bf16[2,3,14,2,128]{4,3,2,1,0:T(2,128)(2,1)S(1)} %get-tuple-element.45), channel_id=1, source_target_pairs={{0,32},{32,0},{64,96},{96,64},{128,160},{160,128},{192,224},{224,1... | collective-permute-start | bytes 129032 | tf_op jit(solution)/shard_map/ppermute | solution.py:94
  24.8 2.6 %collective-permute-start.4 = (bf16[28,128,128]{2,1,0:T(8,128)(2,1)S(1)}, bf16[28,128,128]{2,1,0:T(8,128)(2,1)S(1)}, u32[]{:S(2)}, u32[]{:S(2)}) collective-permute-start(bf16[28,128,128]{2,1,0:T(8,128)(2,1)S(1)} %get-tuple-element.28), channel_id=1, source_target_pairs={{0,1},{1,0},{2,3},{3,2},{4,5},{5,4},{6,7},{7,6},{8,9},{9,8},{10,11... | collective-permute-start | bytes 2752520 | tf_op jit(solution)/shard_map/ppermute | solution.py:52
  28.2 10.7 %collective-permute-start.5 = (bf16[7,128,128]{2,1,0:T(8,128)(2,1)S(1)}, bf16[7,128,128]{2,1,0:T(8,128)(2,1)S(1)}, u32[]{:S(2)}, u32[]{:S(2)}) collective-permute-start(bf16[7,128,128]{2,1,0:T(8,128)(2,1)S(1)} %get-tuple-element.30), channel_id=1, source_target_pairs={{0,8},{1,25},{2,10},{3,27},{4,12},{5,29},{6,14},{7,31},{8,0},{9,17... | collective-permute-start | bytes 688136 | tf_op jit(solution)/shard_map/ppermute | solution.py:52
  35.3 9.0 %collective-permute-start.6 = (bf16[7,128,128]{2,1,0:T(8,128)(2,1)S(1)}, bf16[7,128,128]{2,1,0:T(8,128)(2,1)S(1)}, u32[]{:S(2)}, u32[]{:S(2)}) collective-permute-start(bf16[7,128,128]{2,1,0:T(8,128)(2,1)S(1)} %get-tuple-element.31), channel_id=1, source_target_pairs={{0,32},{1,97},{2,34},{3,99},{4,36},{5,101},{6,38},{7,103},{8,40},{... | collective-permute-start | bytes 688136 | tf_op jit(solution)/shard_map/ppermute | solution.py:52
  38.9 8.2 %collective-permute-start.7 = (bf16[7,128,128]{2,1,0:T(8,128)(2,1)S(1)}, bf16[7,128,128]{2,1,0:T(8,128)(2,1)S(1)}, u32[]{:S(2)}, u32[]{:S(2)}) collective-permute-start(bf16[7,128,128]{2,1,0:T(8,128)(2,1)S(1)} %get-tuple-element.32), channel_id=1, source_target_pairs={{0,40},{1,121},{2,42},{3,123},{4,44},{5,125},{6,46},{7,127},{8,32}... | collective-permute-start | bytes 688136 | tf_op jit(solution)/shard_map/ppermute | solution.py:52
  47.7 3.4 %collective-permute-start.8 = (bf16[224,128]{1,0:T(8,128)(2,1)S(1)}, bf16[224,128]{1,0:T(8,128)(2,1)S(1)}, u32[]{:S(2)}, u32[]{:S(2)}) collective-permute-start(bf16[224,128]{1,0:T(8,128)(2,1)S(1)} %get-tuple-element.34), channel_id=1, source_target_pairs={{0,24},{1,9},{2,26},{3,11},{4,28},{5,13},{6,30},{7,15},{8,16},{9,1... | collective-permute-start | bytes 172040 | tf_op jit(solution)/shard_map/ppermute | solution.py:52
  47.8 3.4 %collective-permute-start.9 = (bf16[224,128]{1,0:T(8,128)(2,1)S(1)}, bf16[224,128]{1,0:T(8,128)(2,1)S(1)}, u32[]{:S(2)}, u32[]{:S(2)}) collective-permute-start(bf16[224,128]{1,0:T(8,128)(2,1)S(1)} %get-tuple-element.35), channel_id=1, source_target_pairs={{0,96},{1,33},{2,98},{3,35},{4,100},{5,37},{6,102},{7,39},{8,104},... | collective-permute-start | bytes 172040 | tf_op jit(solution)/shard_map/ppermute | solution.py:52
  47.9 4.1 %collective-permute-start.10 = (bf16[224,128]{1,0:T(8,128)(2,1)S(1)}, bf16[224,128]{1,0:T(8,128)(2,1)S(1)}, u32[]{:S(2)}, u32[]{:S(2)}) collective-permute-start(bf16[224,128]{1,0:T(8,128)(2,1)S(1)} %get-tuple-element.36), channel_id=1, source_target_pairs={{0,120},{1,41},{2,122},{3,43},{4,124},{5,45},{6,126},{7,47},{8,112... | collective-permute-start | bytes 172040 | tf_op jit(solution)/shard_map/ppermute | solution.py:52
  52.1 3.4 %collective-permute-start.11 = (bf16[224,128]{1,0:T(8,128)(2,1)S(1)}, bf16[224,128]{1,0:T(8,128)(2,1)S(1)}, u32[]{:S(2)}, u32[]{:S(2)}) collective-permute-start(bf16[224,128]{1,0:T(8,128)(2,1)S(1)} %add_convert_fusion.2), channel_id=1, source_target_pairs={{0,128},{1,129},{2,130},{3,131},{4,132},{5,133},{6,134},{7,135},{8... | collective-permute-start | bytes 172040 | tf_op jit(solution)/shard_map/ppermute | solution.py:52
  55.5 5.0 %collective-permute-start.14 = (bf16[224,128]{1,0:T(8,128)(2,1)S(1)}, bf16[224,128]{1,0:T(8,128)(2,1)S(1)}, u32[]{:S(2)}, u32[]{:S(2)}) collective-permute-start(bf16[224,128]{1,0:T(8,128)(2,1)S(1)} %add_convert_fusion.1), channel_id=1, source_target_pairs={{0,6},{1,7},{2,0},{3,1},{4,2},{5,3},{6,4},{7,5},{8,14},{9,15},{10,... | collective-permute-start | bytes 172040 | tf_op jit(solution)/shard_map/ppermute | solution.py:52
  56.2 5.9 %collective-permute-start.13 = (bf16[224,128]{1,0:T(8,128)(2,1)S(1)}, bf16[224,128]{1,0:T(8,128)(2,1)S(1)}, u32[]{:S(2)}, u32[]{:S(2)}) collective-permute-start(bf16[224,128]{1,0:T(8,128)(2,1)S(1)} %add_convert_fusion.1), channel_id=1, source_target_pairs={{0,2},{1,3},{2,4},{3,5},{4,6},{5,7},{6,0},{7,1},{8,10},{9,11},{10,... | collective-permute-start | bytes 172040 | tf_op jit(solution)/shard_map/ppermute | solution.py:52
  57.9 6.9 %collective-permute-start.12 = (bf16[224,128]{1,0:T(8,128)(2,1)S(1)}, bf16[224,128]{1,0:T(8,128)(2,1)S(1)}, u32[]{:S(2)}, u32[]{:S(2)}) collective-permute-start(bf16[224,128]{1,0:T(8,128)(2,1)S(1)} %add_convert_fusion.1), channel_id=1, source_target_pairs={{0,4},{1,5},{2,6},{3,7},{4,0},{5,1},{6,2},{7,3},{8,12},{9,13},{10,... | collective-permute-start | bytes 172040 | tf_op jit(solution)/shard_map/ppermute | solution.py:52
  65.0 3.1 %collective-permute-start.15 = (bf16[224,128]{1,0:T(8,128)(2,1)S(1)}, bf16[224,128]{1,0:T(8,128)(2,1)S(1)}, u32[]{:S(2)}, u32[]{:S(2)}) collective-permute-start(bf16[224,128]{1,0:T(8,128)(2,1)S(1)} %get-tuple-element.44), channel_id=1, source_target_pairs={{0,96},{1,33},{2,98},{3,35},{4,100},{5,37},{6,102},{7,39},{8,104},... | collective-permute-start | bytes 172040 | tf_op jit(solution)/shard_map/ppermute | solution.py:52
  66.1 3.8 %collective-permute-start.16 = (bf16[224,128]{1,0:T(8,128)(2,1)S(1)}, bf16[224,128]{1,0:T(8,128)(2,1)S(1)}, u32[]{:S(2)}, u32[]{:S(2)}) collective-permute-start(bf16[224,128]{1,0:T(8,128)(2,1)S(1)} %get-tuple-element.44), channel_id=1, source_target_pairs={{0,24},{1,9},{2,26},{3,11},{4,28},{5,13},{6,30},{7,15},{8,16},{9,1... | collective-permute-start | bytes 172040 | tf_op jit(solution)/shard_map/ppermute | solution.py:52
  68.0 4.2 %collective-permute-start.17 = (bf16[224,128]{1,0:T(8,128)(2,1)S(1)}, bf16[224,128]{1,0:T(8,128)(2,1)S(1)}, u32[]{:S(2)}, u32[]{:S(2)}) collective-permute-start(bf16[224,128]{1,0:T(8,128)(2,1)S(1)} %get-tuple-element.44), channel_id=1, source_target_pairs={{0,120},{1,41},{2,122},{3,43},{4,124},{5,45},{6,126},{7,47},{8,112... | collective-permute-start | bytes 172040 | tf_op jit(solution)/shard_map/ppermute | solution.py:52
  72.2 11.4 %collective-permute-start.20 = (bf16[4,224,128]{2,1,0:T(8,128)(2,1)S(1)}, bf16[4,224,128]{2,1,0:T(8,128)(2,1)S(1)}, u32[]{:S(2)}, u32[]{:S(2)}) collective-permute-start(bf16[4,224,128]{2,1,0:T(8,128)(2,1)S(1)} %bitcast_dynamic-update-slice_fusion.4), channel_id=1, source_target_pairs={{0,40},{1,121},{2,42},{3,123},{4,44},{5,125},{6,46},{7,127},{8,32}... | collective-permute-start | bytes 688136 | tf_op jit(solution)/shard_map/ppermute | solution.py:52
  72.9 10.7 %collective-permute-start.19 = (bf16[4,224,128]{2,1,0:T(8,128)(2,1)S(1)}, bf16[4,224,128]{2,1,0:T(8,128)(2,1)S(1)}, u32[]{:S(2)}, u32[]{:S(2)}) collective-permute-start(bf16[4,224,128]{2,1,0:T(8,128)(2,1)S(1)} %bitcast_dynamic-update-slice_fusion.4), channel_id=1, source_target_pairs={{0,8},{1,25},{2,10},{3,27},{4,12},{5,29},{6,14},{7,31},{8,0},{9,17... | collective-permute-start | bytes 688136 | tf_op jit(solution)/shard_map/ppermute | solution.py:52
  75.7 7.8 %collective-permute-start.18 = (bf16[4,224,128]{2,1,0:T(8,128)(2,1)S(1)}, bf16[4,224,128]{2,1,0:T(8,128)(2,1)S(1)}, u32[]{:S(2)}, u32[]{:S(2)}) collective-permute-start(bf16[4,224,128]{2,1,0:T(8,128)(2,1)S(1)} %bitcast_dynamic-update-slice_fusion.4), channel_id=1, source_target_pairs={{0,32},{1,97},{2,34},{3,99},{4,36},{5,101},{6,38},{7,103},{8,40},{... | collective-permute-start | bytes 688136 | tf_op jit(solution)/shard_map/ppermute | solution.py:52
  83.7 13.2 %collective-permute-start.21 = (bf16[28,128,128]{2,1,0:T(8,128)(2,1)S(1)}, bf16[28,128,128]{2,1,0:T(8,128)(2,1)S(1)}, u32[]{:S(2)}, u32[]{:S(2)}) collective-permute-start(bf16[28,128,128]{2,1,0:T(8,128)(2,1)S(1)} %bitcast.61), channel_id=1, source_target_pairs={{0,1},{1,0},{2,3},{3,2},{4,5},{5,4},{6,7},{7,6},{8,9},{9,8},{10,11... | collective-permute-start | bytes 2752520 | tf_op jit(solution)/shard_map/ppermute | solution.py:52
